TPU v7x, 256 devices: a whole 4x4x8 slice. The times are simulated.
256 devices in a mesh: rows: 64 (over z, x, core), rep: 4 (over y).
Axes of the slice: x: 4, y: 4, z: 8, core: 2. Of those that a mesh axis runs over, the one named last changes fastest.
Arguments:
- p_blocks: bfloat16 [512, 12, 128, 128], P('rows'), may hold values from -1.25 to 1.25
- d_blocks: bfloat16 [512, 12, 128, 128], P('rows'), may hold values from -1.25 to 1.25
- p_cols: int32 [512, 12], replicated, may hold values from 0 to 511, as said below
- d_cols: int32 [512, 12], replicated, may hold values from 0 to 511, as said below
- out_pcols: int32 [512, 12], P('rows'), may hold values from 0 to 511, as said below
- out_dcols: int32 [512, 12], P('rows'), may hold values from 0 to 511, as said below
- row_slot: int32 [512], replicated, may hold values from 0 to 511, as said below
- branch: int32 [512], P('rows'), may hold values from 0 to 1
Outputs:
- next_p: bfloat16 [512, 12, 128, 128], P('rows', 'rep')
- next_d: bfloat16 [512, 12, 128, 128], P('rows', 'rep')
Inputs may be any that keep to these rules, and one draw needn't show every extreme that they name: row_slot is a permutation; global block row g is stored at position row_slot[g], on index row_slot[g] // 8 of rows, and never more than 3 positions away from g. `p_cols`: the stored row s that holds global block row g names 12 different global block columns, g among them, each equal to (g + o) mod 512 with -12 <= o <= 12. `d_cols`: as for p_cols. `out_pcols`: as for p_cols. `out_dcols`: as for p_cols.
All inputs are finite; a program needn't handle non-finite values.
Results may differ from a plain program's by a relative error of at most 0.0095.
Values may be sent and summed in bfloat16 or wider, within the bound.
No kernel may reach another device: no remote copies, remote signals or barrier semaphores. Data moves between devices by JAX's collectives and lax.ppermute only.
A program may use at most 192 MiB of HBM per device.

v0:
```python
import functools

import jax
import jax.numpy as jnp
import numpy as np
from jax import lax
from jax.experimental import pallas as pl
from jax.experimental.pallas import tpu as pltpu
from jax.sharding import PartitionSpec as P


SPREAD_ROWS = 3
GROUP = 8
VMEM_LIMIT = 67_000_000


def window_table(slab, margin):
    far = margin - 2 * slab
    sizes = (slab, slab, slab, slab - far, far, far, slab, far)
    own, in1, out1, near2, far2, out3, in2, in3 = np.cumsum((0,) + sizes[:-1])

    def run(start, count):
        return list(range(start, start + count))

    core0 = (
        run(out3, far) + run(near2, slab - far) + run(far2, far) + run(out1, slab)
        + run(own, slab) + run(in1, slab) + run(in2, slab) + run(in3, far)
    )
    core1 = (
        run(in3, far) + run(in2, slab) + run(in1, slab) + run(own, slab)
        + run(out1, slab) + run(far2, far) + run(near2, slab - far) + run(out3, far)
    )
    return sizes, np.array(core0 + core1, np.int32)


def swapped(value, even_step, odd_step):
    count = lax.axis_size("rows")
    pairs = [(i, (i + (odd_step if i % 2 else even_step)) % count) for i in range(count)]
    return lax.ppermute(value, "rows", pairs)


def pack_kernel(far, place_ref, blocks_ref, part_ref, near_ref, far_ref, edge_ref, held, sems):
    slab, per = held.shape[:2]
    core, rep = place_ref[0] % 2, place_ref[1]
    load = pltpu.make_async_copy(blocks_ref.at[:, pl.ds(rep * per, per)], held, sems.at[0])
    load.start()
    load.wait()
    rest = slab - far
    stores = [
        pltpu.make_async_copy(held, part_ref, sems.at[1]),
        pltpu.make_async_copy(held.at[pl.ds(core * far, rest)], near_ref, sems.at[2]),
        pltpu.make_async_copy(held.at[pl.ds((1 - core) * rest, far)], far_ref, sems.at[3]),
        pltpu.make_async_copy(held.at[pl.ds(core * rest, far)], edge_ref, sems.at[4]),
    ]
    for store in stores:
        store.start()
    for store in stores:
        store.wait()


def packed(blocks, place, per, far):
    slab, _, side, _ = blocks.shape
    shapes = [(slab, per), (slab - far, per), (far, per), (far, per)]
    return pl.pallas_call(
        functools.partial(pack_kernel, far),
        in_specs=[pl.BlockSpec(memory_space=pltpu.SMEM), pl.BlockSpec(memory_space=pl.ANY)],
        out_specs=[pl.BlockSpec(memory_space=pl.ANY)] * 4,
        out_shape=[jax.ShapeDtypeStruct(s + (side, side), blocks.dtype) for s in shapes],
        scratch_shapes=[
            pltpu.VMEM((slab, per, side, side), blocks.dtype),
            pltpu.SemaphoreType.DMA((5,)),
        ],
        compiler_params=pltpu.CompilerParams(vmem_limit_bytes=VMEM_LIMIT),
        cost_estimate=pl.CostEstimate(
            flops=2_000_000_000, bytes_accessed=2 * slab * per * side * side, transcendentals=0
        ),
        name="pack",
    )(place, blocks)


class Meta:
    def __init__(self, slab, slots, per):
        self.slab, self.slots, self.per = slab, slots, per
        self.square_pitch = slots * per + GROUP
        self.tangent_pitch = 2 * slots * per + GROUP
        self.square_count = 0
        self.tangent_count = slab
        self.kept = 2 * slab
        self.square = self.kept + 2 * slab * per
        self.tangent = self.square + slab * self.square_pitch
        self.size = self.tangent + slab * self.tangent_pitch


def plan_kernel(
    lay, margin, window_rows,
    place_ref, table_ref, pcols, dcols, opcols, odcols, row_slot, meta, inv_p, inv_d, inv_k,
):
    slab, slots, per = lay.slab, lay.slots, lay.per
    rows = row_slot.shape[0]
    index, rep = place_ref[0], place_ref[1]
    row_start = index * slab
    table_base = (index % 2) * window_rows

    def clear(step, carry):
        for u in range(16):
            for inv in (inv_p, inv_d, inv_k):
                inv[step * 16 + u] = slots
        return carry

    lax.fori_loop(0, rows // 16, clear, 0)

    def row(s, carry):
        out_base = s * slots
        own_base = (row_start + s) * slots
        for j in range(slots):
            inv_p[opcols[out_base + j]] = j
            inv_d[odcols[out_base + j]] = j
        square_at = lay.square + s * lay.square_pitch
        tangent_at = lay.tangent + s * lay.tangent_pitch
        square_start, tangent_start = square_at, tangent_at

        def located(column):
            stored = row_slot[column]
            offset = (stored - row_start + margin + rows) & (rows - 1)
            return table_ref[table_base + offset] * per, stored * slots + rep * per

        for k in range(slots):
            here, ids = located(pcols[own_base + k])
            for m in range(per):
                target = inv_p[pcols[ids + m]]
                meta[square_at] = target + ((here + m) << 4) + (k << 13)
                square_at += jnp.where(target < slots, 1, 0)
                target = inv_d[dcols[ids + m]]
                meta[tangent_at] = target + ((here + window_rows * per + m) << 4) + (k << 13)
                tangent_at += jnp.where(target < slots, 1, 0)
            here, ids = located(dcols[own_base + k])
            for m in range(per):
                target = inv_d[pcols[ids + m]]
                meta[tangent_at] = target + ((here + m) << 4) + ((k + slots) << 13)
                tangent_at += jnp.where(target < slots, 1, 0)
        for u in range(GROUP):
            meta[square_at + u] = slots
            meta[tangent_at + u] = slots
        meta[lay.square_count + s] = square_at - square_start
        meta[lay.tangent_count + s] = tangent_at - tangent_start
        for j in range(slots):
            inv_p[opcols[out_base + j]] = slots
            inv_d[odcols[out_base + j]] = slots

        for which, (cols, outs) in enumerate(((pcols, opcols), (dcols, odcols))):
            for k in range(slots):
                inv_k[cols[own_base + k]] = k
            for j in range(per):
                at = lay.kept + (which * slab + s) * per + j
                meta[at] = inv_k[outs[out_base + rep * per + j]]
            for k in range(slots):
                inv_k[cols[own_base + k]] = slots
        return carry

    lax.fori_loop(0, slab, row, 0)


def planned(lay, margin, window_rows, table, place, p_cols, d_cols, out_pcols, out_dcols, row_slot):
    rows = row_slot.shape[0]
    smem = pl.BlockSpec(memory_space=pltpu.SMEM)
    return pl.pallas_call(
        functools.partial(plan_kernel, lay, margin, window_rows),
        in_specs=[smem] * 7,
        out_specs=smem,
        out_shape=jax.ShapeDtypeStruct((lay.size,), jnp.int32),
        scratch_shapes=[pltpu.SMEM((rows,), jnp.int32)] * 3,
        compiler_params=pltpu.CompilerParams(vmem_limit_bytes=VMEM_LIMIT),
        cost_estimate=pl.CostEstimate(flops=6_000_000_000, bytes_accessed=65536, transcendentals=0),
        name="plan",
    )(
        place, jnp.asarray(table), p_cols.reshape(-1), d_cols.reshape(-1),
        out_pcols.reshape(-1), out_dcols.reshape(-1), row_slot,
    )


def kept_kernel(lay, meta, p_ref, d_ref, out_ref, held, sems, out_sem):
    slab, slots, per = lay.slab, lay.slots, lay.per
    loads = []
    for which, blocks in enumerate((p_ref, d_ref)):
        for s in range(slab):
            for j in range(per):
                n = (which * slab + s) * per + j
                k = meta[lay.kept + n]
                load = pltpu.make_async_copy(
                    blocks.at[s, jnp.minimum(k, slots - 1)], held.at[which, s, j], sems.at[n]
                )
                load.start()
                loads.append((load, k, which, s, j))
    for load, k, which, s, j in loads:
        load.wait()

        @pl.when(k == slots)
        def _():
            held[which, s, j] = jnp.zeros(held.shape[3:], held.dtype)

    store = pltpu.make_async_copy(held, out_ref, out_sem)
    store.start()
    store.wait()


def kept_blocks(lay, meta, p_blocks, d_blocks):
    slab, _, side, _ = p_blocks.shape
    shape = (2, slab, lay.per, side, side)
    return pl.pallas_call(
        functools.partial(kept_kernel, lay),
        in_specs=[pl.BlockSpec(memory_space=pltpu.SMEM)] + [pl.BlockSpec(memory_space=pl.ANY)] * 2,
        out_specs=pl.BlockSpec(memory_space=pl.ANY),
        out_shape=jax.ShapeDtypeStruct(shape, p_blocks.dtype),
        scratch_shapes=[
            pltpu.VMEM(shape, p_blocks.dtype),
            pltpu.SemaphoreType.DMA((2 * slab * lay.per,)),
            pltpu.SemaphoreType.DMA,
        ],
        compiler_params=pltpu.CompilerParams(vmem_limit_bytes=VMEM_LIMIT),
        cost_estimate=pl.CostEstimate(flops=3_000_000_000, bytes_accessed=1 << 21, transcendentals=0),
        name="kept",
    )(meta, p_blocks, d_blocks)


def product_kernel(n_left, sizes, count_at, list_at, pitch, quarters, meta, *refs):
    left_refs = refs[:n_left]
    pieces = refs[n_left : n_left + n_left * len(sizes)]
    out_ref, left, window, total, left_sems, sems = refs[-6:]
    row = pl.program_id(0)
    slab, slots = left_refs[0].shape[:2]
    per = slots // quarters

    def left_copy(s, n):
        return pltpu.make_async_copy(
            left_refs[n].at[s], left.at[s, pl.ds(n * slots, slots)], left_sems.at[s, n]
        )

    @pl.when(row == 0)
    def _():
        copies, base = [], 0
        for index, piece in enumerate(pieces):
            size = sizes[index % len(sizes)]
            copies.append(
                pltpu.make_async_copy(
                    piece, window.at[pl.ds(base * per, size * per)], sems.at[index]
                )
            )
            base += size
        for copy in copies:
            copy.start()
        for s in range(slab):
            for n in range(n_left):
                left_copy(s, n).start()
        for copy in copies:
            copy.wait()

    for n in range(n_left):
        left_copy(row, n).wait()
    total[...] = jnp.zeros_like(total)

    def step(group, carry):
        for u in range(GROUP):
            code = meta[list_at + row * pitch + group * GROUP + u]
            target = code & 15
            total[target] += jnp.dot(
                left[row, code >> 13], window[(code >> 4) & 511],
                preferred_element_type=jnp.float32,
            )
        return carry

    groups = (meta[count_at + row] + GROUP - 1) // GROUP
    lax.fori_loop(0, groups, step, 0)
    for j in range(slots):
        out_ref[j // per, 0, j % per] = total[j].astype(out_ref.dtype)


def block_products(lay, lefts, windows, sizes, meta, tangent, quarters):
    slab, slots, side, _ = lefts[0].shape
    per = lay.per
    pieces = [piece.reshape(-1, side, side) for window in windows for piece in window]
    rows_in = len(windows) * sum(sizes)
    dtype = lefts[0].dtype
    where = (
        (lay.tangent_count, lay.tangent, lay.tangent_pitch)
        if tangent
        else (lay.square_count, lay.square, lay.square_pitch)
    )
    any_spec = pl.BlockSpec(memory_space=pl.ANY)
    return pl.pallas_call(
        functools.partial(product_kernel, len(lefts), sizes, *where, quarters),
        grid_spec=pltpu.PrefetchScalarGridSpec(
            num_scalar_prefetch=1,
            grid=(slab,),
            in_specs=[any_spec] * (len(lefts) + len(pieces)),
            out_specs=pl.BlockSpec((quarters, 1, per, side, side), lambda s, *_: (0, s, 0, 0, 0)),
            scratch_shapes=[
                pltpu.VMEM((slab, len(lefts) * slots, side, side), dtype),
                pltpu.VMEM((rows_in * per, side, side), dtype),
                pltpu.VMEM((slots + 1, side, side), jnp.float32),
                pltpu.SemaphoreType.DMA((slab, len(lefts))),
                pltpu.SemaphoreType.DMA((len(pieces),)),
            ],
        ),
        out_shape=jax.ShapeDtypeStruct((quarters, slab, per, side, side), jnp.bfloat16),
        compiler_params=pltpu.CompilerParams(
            dimension_semantics=("arbitrary",), vmem_limit_bytes=VMEM_LIMIT
        ),
        cost_estimate=pl.CostEstimate(
            flops=12_000_000_000 if tangent else 8_000_000_000,
            bytes_accessed=2 * (rows_in * per + 2 * slab * slots) * side * side,
            transcendentals=0,
        ),
        name="tangent_products" if tangent else "square_products",
    )(meta, *lefts, *pieces)


def finish_kernel(rows, branch_ref, parts_ref, kept_ref, out_ref):
    step = pl.program_id(0)
    for s in range(rows):
        squaring = branch_ref[step * rows + s] == 1
        total = parts_ref[0, s].astype(jnp.float32)
        for q in range(1, parts_ref.shape[0]):
            total = total + parts_ref[q, s].astype(jnp.float32)
        kept = kept_ref[0, s].astype(jnp.float32)
        out_ref[s] = jnp.where(squaring, total, 2.0 * kept - total).astype(out_ref.dtype)


def finish(parts, kept, which, branch):
    quarters, slab, per, side, _ = parts.shape
    rows = 2
    return pl.pallas_call(
        functools.partial(finish_kernel, rows),
        grid_spec=pltpu.PrefetchScalarGridSpec(
            num_scalar_prefetch=1,
            grid=(slab // rows,),
            in_specs=[
                pl.BlockSpec((quarters, rows, per, side, side), lambda s, *_: (0, s, 0, 0, 0)),
                pl.BlockSpec((1, rows, per, side, side), lambda s, *_: (which, s, 0, 0, 0)),
            ],
            out_specs=pl.BlockSpec((rows, per, side, side), lambda s, *_: (s, 0, 0, 0)),
        ),
        out_shape=jax.ShapeDtypeStruct((slab, per, side, side), jnp.bfloat16),
        compiler_params=pltpu.CompilerParams(
            dimension_semantics=("arbitrary",), vmem_limit_bytes=VMEM_LIMIT
        ),
        cost_estimate=pl.CostEstimate(flops=4_000_000_000, bytes_accessed=5 << 20, transcendentals=0),
        name="finish",
    )(branch, parts, kept)


def step(p_blocks, d_blocks, p_cols, d_cols, out_pcols, out_dcols, row_slot, branch):
    slab, slots, _, _ = p_blocks.shape
    quarters = lax.axis_size("rep")
    per = slots // quarters
    margin = slots + 2 * SPREAD_ROWS
    far = margin - 2 * slab
    sizes, table = window_table(slab, margin)
    lay = Meta(slab, slots, per)
    place = jnp.stack([lax.axis_index("rows"), lax.axis_index("rep")]).astype(jnp.int32)

    def outer(blocks, place):
        part, near, rest, edge = packed(blocks, place, per, far)
        out1 = swapped(part, -1, 1)
        far2 = swapped(rest, 2, -2)
        near2 = swapped(near, 2, -2)
        out3 = swapped(edge, -3, 3)
        in1 = swapped(part, 1, -1)
        return part, in1, out1, near2, far2, out3

    def inner(pieces):
        return pieces + (swapped(pieces[2], 1, -1), swapped(pieces[4], 1, -1))

    p_window = outer(p_blocks, place)
    d_place, p_part = lax.optimization_barrier((place, p_window[0]))
    p_window = (p_part,) + p_window[1:]
    d_window = outer(d_blocks, d_place)
    meta = planned(
        lay, margin, sum(sizes), table, d_place, p_cols, d_cols, out_pcols, out_dcols, row_slot
    )
    p_window = inner(p_window)
    d_window = inner(d_window)
    square = block_products(lay, (p_blocks,), (p_window,), sizes, meta, False, quarters)
    square, kept_meta = lax.optimization_barrier((square, meta))
    square = lax.all_to_all(square, "rep", split_axis=0, concat_axis=0, tiled=True)
    kept = kept_blocks(lay, kept_meta, p_blocks, d_blocks)
    kept, tangent_meta = lax.optimization_barrier((kept, kept_meta))
    tangent = block_products(
        lay, (p_blocks, d_blocks), (p_window, d_window), sizes, tangent_meta, True, quarters
    )
    tangent, square = lax.optimization_barrier((tangent, square))
    tangent = lax.all_to_all(tangent, "rep", split_axis=0, concat_axis=0, tiled=True)
    return finish(square, kept, 0, branch), finish(tangent, kept, 1, branch)


def solution(mesh):
    return jax.shard_map(
        step,
        mesh=mesh,
        in_specs=(
            P("rows", None, None, None),
            P("rows", None, None, None),
            P(),
            P(),
            P("rows", None),
            P("rows", None),
            P(),
            P("rows"),
        ),
        out_specs=(P("rows", "rep", None, None), P("rows", "rep", None, None)),
        check_vma=False,
    )
```

profile of v0, /device:TPU:8, one launch (start us, length us, event | category | flops | bytes accessed | tf_op | source)
XLA Modules:
  0.0 150.2 jit_solution(9543186368126686975)
XLA Ops:
  0.6 0.6 pad_add_fusion.place_ref
  1.2 3.2 %pack.2 = (bf16[8,3,128,128]{3,2,1,0:T(8,128)(2,1)}, bf16[6,3,128,128]{3,2,1,0:T(8,128)(2,1)}, bf16[2,3,128,128]{3,2,1,0:T(8,128)(2,1)}, bf16[2,3,128,128]{3,2,1,0:T(8,128)(2,1)}) custom-call(s32[2]{0:T(128)} %pad_add_fusion.place_ref, bf16[8,12,128,128]{3,2,1,0:T(8,128)(2,1)} %refs_0_.3), custom_call_target="tpu_custom_call" | custom-call | flops 2000000000 | bytes 786432 | tf_op jit(solution)/shard_map/pack/pallas_call | solution.py:64
  4.4 7.6 %collective-permute-start.1 = (bf16[8,3,128,128]{3,2,1,0:T(8,128)(2,1)}, bf16[8,3,128,128]{3,2,1,0:T(8,128)(2,1)}, u32[]{:S(2)}, u32[]{:S(2)}) collective-permute-start(bf16[8,3,128,128]{3,2,1,0:T(8,128)(2,1)} %get-tuple-element.20), channel_id=1, source_target_pairs={{0,252},{4,8},{8,4},{12,16},{16,12},{20,24},{24,20},{28,32},{32,28... | collective-permute-start | bytes 2359304 | tf_op jit(solution)/shard_map/ppermute | solution.py:39
  12.0 0.0 collective-permute-start.3
  12.0 0.2 collective-permute-start
  12.2 11.9 %collective-permute-done.1 = bf16[8,3,128,128]{3,2,1,0:T(8,128)(2,1)} collective-permute-done((bf16[8,3,128,128]{3,2,1,0:T(8,128)(2,1)}, bf16[8,3,128,128]{3,2,1,0:T(8,128)(2,1)}, u32[]{:S(2)}, u32[]{:S(2)}) %collective-permute-start.1) | collective-permute-done | bytes 786464 | tf_op jit(solution)/shard_map/ppermute | solution.py:39
  24.1 0.0 collective-permute-start.5
  24.1 2.7 %collective-permute-start.4 = (bf16[2,3,128,128]{3,2,1,0:T(8,128)(2,1)}, bf16[2,3,128,128]{3,2,1,0:T(8,128)(2,1)}, u32[]{:S(2)}, u32[]{:S(2)}) collective-permute-start(bf16[2,3,128,128]{3,2,1,0:T(8,128)(2,1)} %get-tuple-element.23), channel_id=1, source_target_pairs={{0,244},{4,16},{8,252},{12,24},{16,4},{20,32},{24,12},{28,40},{32,... | collective-permute-start | bytes 589832 | tf_op jit(solution)/shard_map/ppermute | solution.py:39
  26.8 2.8 %collective-permute-start.2 = (bf16[6,3,128,128]{3,2,1,0:T(8,128)(2,1)}, bf16[6,3,128,128]{3,2,1,0:T(8,128)(2,1)}, u32[]{:S(2)}, u32[]{:S(2)}) collective-permute-start(bf16[6,3,128,128]{3,2,1,0:T(8,128)(2,1)} %get-tuple-element.21), channel_id=1, source_target_pairs={{0,8},{4,252},{8,16},{12,4},{16,24},{20,12},{24,32},{28,20},{32,40... | collective-permute-start | bytes 1769480 | tf_op jit(solution)/shard_map/ppermute | solution.py:39
  29.5 0.7 reshape.74.opcols
  30.2 0.6 reshape.75.odcols
  30.8 0.0 copy-done
  30.8 0.1 copy.11
  31.0 0.8 reshape.72.pcols
  31.8 0.9 copy.12
  32.7 0.8 reshape.73.dcols
  33.4 0.0 collective-permute-done.3
  33.4 0.0 collective-permute-start.6
  33.4 8.2 %plan.1.meta = s32[1056]{0:T(1024)} custom-call(s32[2]{0:T(128)} %pad_add_fusion.place_ref, s32[88]{0:T(128)} %constant.11.clone.table_ref, s32[6144]{0:T(1024)} %reshape.72.pcols, s32[6144]{0:T(1024)} %reshape.73.dcols, s32[96]{0:T(128)} %reshape.74.opcols, s32[96]{0:T(128)} %reshape.75.odcols, s32[512]{0:T(512)} %row_slot.1), custom_call_target="tpu_custom_call" | custom-call | flops 6000000000 | bytes 65536 | tf_op jit(solution)/shard_map/plan/pallas_call | solution.py:166
  41.7 3.0 %pack.3 = (bf16[8,3,128,128]{3,2,1,0:T(8,128)(2,1)}, bf16[6,3,128,128]{3,2,1,0:T(8,128)(2,1)}, bf16[2,3,128,128]{3,2,1,0:T(8,128)(2,1)}, bf16[2,3,128,128]{3,2,1,0:T(8,128)(2,1)}) custom-call(s32[2]{0:T(128)} %pad_add_fusion.place_ref, bf16[8,12,128,128]{3,2,1,0:T(8,128)(2,1)} %refs_1_.1), custom_call_target="tpu_custom_call" | custom-call | flops 2000000000 | bytes 786432 | tf_op jit(solution)/shard_map/pack/pallas_call | solution.py:64
  44.7 0.0 collective-permute-done.4
  44.7 2.8 %collective-permute-start.8 = (bf16[8,3,128,128]{3,2,1,0:T(8,128)(2,1)}, bf16[8,3,128,128]{3,2,1,0:T(8,128)(2,1)}, u32[]{:S(2)}, u32[]{:S(2)}) collective-permute-start(bf16[8,3,128,128]{3,2,1,0:T(8,128)(2,1)} %get-tuple-element.26), channel_id=1, source_target_pairs={{0,252},{4,8},{8,4},{12,16},{16,12},{20,24},{24,20},{28,32},{32,28... | collective-permute-start | bytes 2359304 | tf_op jit(solution)/shard_map/ppermute | solution.py:39
  47.5 0.0 collective-permute-done.6
  47.5 0.0 collective-permute-done.2
  47.5 0.0 collective-permute-done
  47.5 0.0 collective-permute-done.5
  47.6 10.5 %square_products.1 = bf16[4,8,3,128,128]{4,3,2,1,0:T(8,128)(2,1)} custom-call(s32[1056]{0:T(1024)} %plan.1.meta, bf16[8,12,128,128]{3,2,1,0:T(8,128)(2,1)} %refs_0_.3, bf16[24,128,128]{2,1,0:T(8,128)(2,1)} %bitcast.18, bf16[24,128,128]{2,1,0:T(8,128)(2,1)} %bitcast.3.refs_2_.refs_3_, bf16[24,128,128]{2,1,0:T(8,128)(2,1)} %bitcast.4.refs_3_.refs_4_, ...), custom_call_target="tpu_custom_call" | custom-call | flops 8000000000 | bytes 10616832 | tf_op jit(solution)/shard_map/square_products/pallas_call | solution.py:289
  58.0 5.7 %all-to-all-start = ((bf16[4,8,3,128,128]{4,3,2,1,0:T(8,128)(2,1)}), bf16[4,8,3,128,128]{4,3,2,1,0:T(8,128)(2,1)}, u32[]{:S(2)}, u32[]{:S(2)}) async-start(bf16[4,8,3,128,128]{4,3,2,1,0:T(8,128)(2,1)} %square_products.1), calls=%async_computation | async-start | bytes 6291456 | tf_op jit(solution)/shard_map/all_to_all | solution.py:384
  63.7 0.0 collective-permute-start.7
  63.7 0.0 collective-permute-done.8
  63.7 0.5 collective-permute-start.12
  64.2 0.0 collective-permute-start.9
  64.2 0.0 collective-permute-start.10
  64.3 1.4 collective-permute-start.11
  65.6 18.4 %collective-permute-done.10 = bf16[2,3,128,128]{3,2,1,0:T(8,128)(2,1)} collective-permute-done((bf16[2,3,128,128]{3,2,1,0:T(8,128)(2,1)S(1)}, bf16[2,3,128,128]{3,2,1,0:T(8,128)(2,1)}, u32[]{:S(2)}, u32[]{:S(2)}) %collective-permute-start.10) | collective-permute-done | bytes 196640 | tf_op jit(solution)/shard_map/ppermute | solution.py:39
  84.0 0.0 collective-permute-start.13
  84.0 3.7 %kept.1.kept_ref = bf16[2,8,3,128,128]{4,3,2,1,0:T(8,128)(2,1)} custom-call(s32[1056]{0:T(1024)} %plan.1.meta, bf16[8,12,128,128]{3,2,1,0:T(8,128)(2,1)} %refs_0_.3, bf16[8,12,128,128]{3,2,1,0:T(8,128)(2,1)} %refs_1_.1), custom_call_target="tpu_custom_call" | custom-call | flops 3000000000 | bytes 2097152 | tf_op jit(solution)/shard_map/kept/pallas_call | solution.py:209
  87.7 0.0 collective-permute-done.11
  87.7 0.0 collective-permute-done.13
  87.7 0.0 collective-permute-done.9
  87.7 0.0 collective-permute-done.7
  87.7 0.0 collective-permute-done.12
  87.7 15.4 %tangent_products.1 = bf16[4,8,3,128,128]{4,3,2,1,0:T(8,128)(2,1)} custom-call(s32[1056]{0:T(1024)} %plan.1.meta, bf16[8,12,128,128]{3,2,1,0:T(8,128)(2,1)} %refs_0_.3, bf16[8,12,128,128]{3,2,1,0:T(8,128)(2,1)} %refs_1_.1, bf16[24,128,128]{2,1,0:T(8,128)(2,1)} %bitcast.19, bf16[24,128,128]{2,1,0:T(8,128)(2,1)} %bitcast.3.refs_2_.refs_3_, ...), custom_call_target="tpu_custom_call" | custom-call | flops 12000000000 | bytes 14942208 | tf_op jit(solution)/shard_map/tangent_products/pallas_call | solution.py:289
  103.1 0.0 all-to-all-done.parts_ref
  103.1 5.7 %all-to-all-start.1 = ((bf16[4,8,3,128,128]{4,3,2,1,0:T(8,128)(2,1)}), bf16[4,8,3,128,128]{4,3,2,1,0:T(8,128)(2,1)}, u32[]{:S(2)}, u32[]{:S(2)}) async-start(bf16[4,8,3,128,128]{4,3,2,1,0:T(8,128)(2,1)} %tangent_products.1), calls=%async_computation.1 | async-start | bytes 6291456 | tf_op jit(solution)/shard_map/all_to_all | solution.py:391
  108.9 4.7 %finish.2 = bf16[8,3,128,128]{3,2,1,0:T(8,128)(2,1)} custom-call(s32[8]{0:T(128)} %branch_ref.3, bf16[4,8,3,128,128]{4,3,2,1,0:T(8,128)(2,1)} %all-to-all-done.parts_ref, bf16[2,8,3,128,128]{4,3,2,1,0:T(8,128)(2,1)} %kept.1.kept_ref), custom_call_target="tpu_custom_call" | custom-call | flops 4000000000 | bytes 5242880 | tf_op jit(solution)/shard_map/finish/pallas_call | solution.py:331
  113.6 31.9 %all-to-all-done.1.parts_ref = bf16[4,8,3,128,128]{4,3,2,1,0:T(8,128)(2,1)} async-done(((bf16[4,8,3,128,128]{4,3,2,1,0:T(8,128)(2,1)}), bf16[4,8,3,128,128]{4,3,2,1,0:T(8,128)(2,1)}, u32[]{:S(2)}, u32[]{:S(2)}) %all-to-all-start.1) | async-done | bytes 3145760 | tf_op jit(solution)/shard_map/all_to_all | solution.py:391
  145.5 4.7 %finish.3 = bf16[8,3,128,128]{3,2,1,0:T(8,128)(2,1)} custom-call(s32[8]{0:T(128)} %branch_ref.3, bf16[4,8,3,128,128]{4,3,2,1,0:T(8,128)(2,1)} %all-to-all-done.1.parts_ref, bf16[2,8,3,128,128]{4,3,2,1,0:T(8,128)(2,1)} %kept.1.kept_ref), custom_call_target="tpu_custom_call" | custom-call | flops 4000000000 | bytes 5242880 | tf_op jit(solution)/shard_map/finish/pallas_call | solution.py:331
  (7 shorter events, 0.0 us)
Async XLA Ops:
  1.2 28.3 %copy-start.1 = (s32[8,12]{1,0:T(8,128)S(1)}, s32[8,12]{1,0:T(8,128)}, u32[]{:S(2)}) copy-start(s32[8,12]{1,0:T(8,128)} %param.13) | copy-start | bytes 1156
  1.2 28.9 %copy-start.2 = (s32[8,12]{1,0:T(8,128)S(1)}, s32[8,12]{1,0:T(8,128)}, u32[]{:S(2)}) copy-start(s32[8,12]{1,0:T(8,128)} %param.14) | copy-start | bytes 1156
  1.2 29.6 %copy-start = (s32[512,12]{0,1:T(8,128)S(1)}, s32[512,12]{0,1:T(8,128)}, u32[]{:S(2)}) copy-start(s32[512,12]{0,1:T(8,128)} %param.11) | copy-start | bytes 73732
  4.4 19.7 %collective-permute-start.1 = (bf16[8,3,128,128]{3,2,1,0:T(8,128)(2,1)}, bf16[8,3,128,128]{3,2,1,0:T(8,128)(2,1)}, u32[]{:S(2)}, u32[]{:S(2)}) collective-permute-start(bf16[8,3,128,128]{3,2,1,0:T(8,128)(2,1)} %get-tuple-element.20), channel_id=1, source_target_pairs={{0,252},{4,8},{8,4},{12,16},{16,12},{20,24},{24,20},{28,32},{32,28... | collective-permute-start | bytes 2359304 | tf_op jit(solution)/shard_map/ppermute | solution.py:39
  12.0 21.4 %collective-permute-start.3 = (bf16[2,3,128,128]{3,2,1,0:T(8,128)(2,1)}, bf16[2,3,128,128]{3,2,1,0:T(8,128)(2,1)}, u32[]{:S(2)}, u32[]{:S(2)}) collective-permute-start(bf16[2,3,128,128]{3,2,1,0:T(8,128)(2,1)} %get-tuple-element.22), channel_id=1, source_target_pairs={{0,8},{4,252},{8,16},{12,4},{16,24},{20,12},{24,32},{28,20},{32,40... | collective-permute-start | bytes 589832 | tf_op jit(solution)/shard_map/ppermute | solution.py:39
  12.0 35.5 %collective-permute-start = (bf16[8,3,128,128]{3,2,1,0:T(8,128)(2,1)}, bf16[8,3,128,128]{3,2,1,0:T(8,128)(2,1)}, u32[]{:S(2)}, u32[]{:S(2)}) collective-permute-start(bf16[8,3,128,128]{3,2,1,0:T(8,128)(2,1)} %get-tuple-element.20), channel_id=1, source_target_pairs={{0,4},{4,0},{8,12},{12,8},{16,20},{20,16},{24,28},{28,24},{32,36},... | collective-permute-start | bytes 2359304 | tf_op jit(solution)/shard_map/ppermute | solution.py:39
  24.1 23.5 %collective-permute-start.5 = (bf16[8,3,128,128]{3,2,1,0:T(8,128)(2,1)}, bf16[8,3,128,128]{3,2,1,0:T(8,128)(2,1)}, u32[]{:S(2)}, u32[]{:S(2)}) collective-permute-start(bf16[8,3,128,128]{3,2,1,0:T(8,128)(2,1)} %collective-permute-done.1), channel_id=1, source_target_pairs={{0,4},{4,0},{8,12},{12,8},{16,20},{20,16},{24,28},{28,24},{32,36},... | collective-permute-start | bytes 2359304 | tf_op jit(solution)/shard_map/ppermute | solution.py:39
  24.1 20.6 %collective-permute-start.4 = (bf16[2,3,128,128]{3,2,1,0:T(8,128)(2,1)}, bf16[2,3,128,128]{3,2,1,0:T(8,128)(2,1)}, u32[]{:S(2)}, u32[]{:S(2)}) collective-permute-start(bf16[2,3,128,128]{3,2,1,0:T(8,128)(2,1)} %get-tuple-element.23), channel_id=1, source_target_pairs={{0,244},{4,16},{8,252},{12,24},{16,4},{20,32},{24,12},{28,40},{32,... | collective-permute-start | bytes 589832 | tf_op jit(solution)/shard_map/ppermute | solution.py:39
  26.8 20.8 %collective-permute-start.2 = (bf16[6,3,128,128]{3,2,1,0:T(8,128)(2,1)}, bf16[6,3,128,128]{3,2,1,0:T(8,128)(2,1)}, u32[]{:S(2)}, u32[]{:S(2)}) collective-permute-start(bf16[6,3,128,128]{3,2,1,0:T(8,128)(2,1)} %get-tuple-element.21), channel_id=1, source_target_pairs={{0,8},{4,252},{8,16},{12,4},{16,24},{20,12},{24,32},{28,20},{32,40... | collective-permute-start | bytes 1769480 | tf_op jit(solution)/shard_map/ppermute | solution.py:39
  33.4 14.1 %collective-permute-start.6 = (bf16[2,3,128,128]{3,2,1,0:T(8,128)(2,1)}, bf16[2,3,128,128]{3,2,1,0:T(8,128)(2,1)}, u32[]{:S(2)}, u32[]{:S(2)}) collective-permute-start(bf16[2,3,128,128]{3,2,1,0:T(8,128)(2,1)} %collective-permute-done.3), channel_id=1, source_target_pairs={{0,4},{4,0},{8,12},{12,8},{16,20},{20,16},{24,28},{28,24},{32,36},... | collective-permute-start | bytes 589832 | tf_op jit(solution)/shard_map/ppermute | solution.py:39
  44.7 19.0 %collective-permute-start.8 = (bf16[8,3,128,128]{3,2,1,0:T(8,128)(2,1)}, bf16[8,3,128,128]{3,2,1,0:T(8,128)(2,1)}, u32[]{:S(2)}, u32[]{:S(2)}) collective-permute-start(bf16[8,3,128,128]{3,2,1,0:T(8,128)(2,1)} %get-tuple-element.26), channel_id=1, source_target_pairs={{0,252},{4,8},{8,4},{12,16},{16,12},{20,24},{24,20},{28,32},{32,28... | collective-permute-start | bytes 2359304 | tf_op jit(solution)/shard_map/ppermute | solution.py:39
  58.0 6.2 %copy-start.3 = (bf16[2,3,128,128]{3,2,1,0:T(8,128)(2,1)S(1)}, bf16[2,3,128,128]{3,2,1,0:T(8,128)(2,1)}, u32[]{:S(2)}) copy-start(bf16[2,3,128,128]{3,2,1,0:T(8,128)(2,1)} %get-tuple-element.28) | copy-start | bytes 589828
  58.0 45.1 %all-to-all-start = ((bf16[4,8,3,128,128]{4,3,2,1,0:T(8,128)(2,1)}), bf16[4,8,3,128,128]{4,3,2,1,0:T(8,128)(2,1)}, u32[]{:S(2)}, u32[]{:S(2)}) async-start(bf16[4,8,3,128,128]{4,3,2,1,0:T(8,128)(2,1)} %square_products.1), calls=%async_computation | async-start | bytes 6291456 | tf_op jit(solution)/shard_map/all_to_all | solution.py:384
  63.7 24.0 %collective-permute-start.7 = (bf16[8,3,128,128]{3,2,1,0:T(8,128)(2,1)}, bf16[8,3,128,128]{3,2,1,0:T(8,128)(2,1)}, u32[]{:S(2)}, u32[]{:S(2)}) collective-permute-start(bf16[8,3,128,128]{3,2,1,0:T(8,128)(2,1)} %get-tuple-element.26), channel_id=1, source_target_pairs={{0,4},{4,0},{8,12},{12,8},{16,20},{20,16},{24,28},{28,24},{32,36},... | collective-permute-start | bytes 2359304 | tf_op jit(solution)/shard_map/ppermute | solution.py:39
  63.7 24.0 %collective-permute-start.12 = (bf16[8,3,128,128]{3,2,1,0:T(8,128)(2,1)}, bf16[8,3,128,128]{3,2,1,0:T(8,128)(2,1)}, u32[]{:S(2)}, u32[]{:S(2)}) collective-permute-start(bf16[8,3,128,128]{3,2,1,0:T(8,128)(2,1)} %collective-permute-done.8), channel_id=1, source_target_pairs={{0,4},{4,0},{8,12},{12,8},{16,20},{20,16},{24,28},{28,24},{32,36},... | collective-permute-start | bytes 2359304 | tf_op jit(solution)/shard_map/ppermute | solution.py:39
  64.2 23.5 %collective-permute-start.9 = (bf16[6,3,128,128]{3,2,1,0:T(8,128)(2,1)}, bf16[6,3,128,128]{3,2,1,0:T(8,128)(2,1)}, u32[]{:S(2)}, u32[]{:S(2)}) collective-permute-start(bf16[6,3,128,128]{3,2,1,0:T(8,128)(2,1)} %get-tuple-element.27), channel_id=1, source_target_pairs={{0,8},{4,252},{8,16},{12,4},{16,24},{20,12},{24,32},{28,20},{32,40... | collective-permute-start | bytes 1769480 | tf_op jit(solution)/shard_map/ppermute | solution.py:39
  64.2 19.8 %collective-permute-start.10 = (bf16[2,3,128,128]{3,2,1,0:T(8,128)(2,1)S(1)}, bf16[2,3,128,128]{3,2,1,0:T(8,128)(2,1)}, u32[]{:S(2)}, u32[]{:S(2)}) collective-permute-start(bf16[2,3,128,128]{3,2,1,0:T(8,128)(2,1)S(1)} %copy-done.3), channel_id=1, source_target_pairs={{0,8},{4,252},{8,16},{12,4},{16,24},{20,12},{24,32},{28,20},{32,40... | collective-permute-start | bytes 589832 | tf_op jit(solution)/shard_map/ppermute | solution.py:39
  64.3 23.4 %collective-permute-start.11 = (bf16[2,3,128,128]{3,2,1,0:T(8,128)(2,1)}, bf16[2,3,128,128]{3,2,1,0:T(8,128)(2,1)}, u32[]{:S(2)}, u32[]{:S(2)}) collective-permute-start(bf16[2,3,128,128]{3,2,1,0:T(8,128)(2,1)} %get-tuple-element.29), channel_id=1, source_target_pairs={{0,244},{4,16},{8,252},{12,24},{16,4},{20,32},{24,12},{28,40},{32,... | collective-permute-start | bytes 589832 | tf_op jit(solution)/shard_map/ppermute | solution.py:39
  84.0 3.7 %collective-permute-start.13 = (bf16[2,3,128,128]{3,2,1,0:T(8,128)(2,1)}, bf16[2,3,128,128]{3,2,1,0:T(8,128)(2,1)}, u32[]{:S(2)}, u32[]{:S(2)}) collective-permute-start(bf16[2,3,128,128]{3,2,1,0:T(8,128)(2,1)} %collective-permute-done.10), channel_id=1, source_target_pairs={{0,4},{4,0},{8,12},{12,8},{16,20},{20,16},{24,28},{28,24},{32,36},... | collective-permute-start | bytes 589832 | tf_op jit(solution)/shard_map/ppermute | solution.py:39
  103.1 42.4 %all-to-all-start.1 = ((bf16[4,8,3,128,128]{4,3,2,1,0:T(8,128)(2,1)}), bf16[4,8,3,128,128]{4,3,2,1,0:T(8,128)(2,1)}, u32[]{:S(2)}, u32[]{:S(2)}) async-start(bf16[4,8,3,128,128]{4,3,2,1,0:T(8,128)(2,1)} %tangent_products.1), calls=%async_computation.1 | async-start | bytes 6291456 | tf_op jit(solution)/shard_map/all_to_all | solution.py:391
where the time goes:
time: 153 us; the launch traced here: 150 us
  waiting for transfers between devices  62.2 us (41%)
  Pallas kernels  53.4 us (35%)
  starting transfers between devices  29.3 us (19%)
  local copies, waits for them, and re-layouts  3.89 us (3%)
    all_to_all x1, waiting for transfers between devices, step(): lax.all_to_all(tangent, 'rep', split_axis=0, concat_axis=0, tiled=True)  31.9 us
    ppermute x14, waiting for transfers between devices, swapped(): return lax.ppermute(value, 'rows', pairs)  30.3 us
    pallas_call x2, Pallas kernels, block_products(): pl.pallas_call(functools.partial(product_kernel, len(lefts), sizes, *wher...  25.8 us
    ppermute x14, starting transfers between devices, swapped(): return lax.ppermute(value, 'rows', pairs)  17.9 us
    pallas_call x2, Pallas kernels, finish(): pl.pallas_call(functools.partial(finish_kernel, rows), grid_spec=pltpu.Pr...  9.46 us
    pallas_call x1, Pallas kernels, planned(): pl.pallas_call(functools.partial(plan_kernel, lay, margin, window_rows),...  8.23 us
    pallas_call x2, Pallas kernels, packed(): pl.pallas_call(functools.partial(pack_kernel, far), in_specs=[pl.BlockSpe...  6.21 us
    all_to_all x1, starting transfers between devices, step(): lax.all_to_all(tangent, 'rep', split_axis=0, concat_axis=0, tiled=True)  5.75 us
  transfers between devices with their start and end apart: 16, of which 3 were waited for; matrix products, arithmetic and copies ran while one was open for 3% of the time, Pallas kernels for 30%

commit v1 on v0

v1 whole, which is shorter than its diff:
```python
import functools

import jax
import jax.numpy as jnp
import numpy as np
from jax import lax
from jax.experimental import pallas as pl
from jax.experimental.pallas import tpu as pltpu
from jax.sharding import PartitionSpec as P


SPREAD_ROWS = 3
GROUP = 8
VMEM_LIMIT = 67_000_000


def window_table(slab, margin):
    far = margin - 2 * slab
    sizes = (slab, slab, slab, slab - far, far, far, slab, far)
    own, in1, out1, near2, far2, out3, in2, in3 = np.cumsum((0,) + sizes[:-1])

    def run(start, count):
        return list(range(start, start + count))

    core0 = (
        run(out3, far) + run(near2, slab - far) + run(far2, far) + run(out1, slab)
        + run(own, slab) + run(in1, slab) + run(in2, slab) + run(in3, far)
    )
    core1 = (
        run(in3, far) + run(in2, slab) + run(in1, slab) + run(own, slab)
        + run(out1, slab) + run(far2, far) + run(near2, slab - far) + run(out3, far)
    )
    edge = [0] * (slab - far)
    return sizes, np.array(edge + core0 + edge + edge + core1 + edge, np.int32)


def swapped(value, even_step, odd_step):
    count = lax.axis_size("rows")
    pairs = [(i, (i + (odd_step if i % 2 else even_step)) % count) for i in range(count)]
    return lax.ppermute(value, "rows", pairs)


def pack_kernel(far, *refs):
    blocks, outs, (held, sems) = refs[:2], refs[2:10], refs[10:]
    slab, per = held.shape[1:3]
    core, rep = lax.axis_index("rows") % 2, lax.axis_index("rep")
    rest = slab - far
    loads = [
        pltpu.make_async_copy(block.at[:, pl.ds(rep * per, per)], held.at[n], sems.at[n, 4])
        for n, block in enumerate(blocks)
    ]
    for load in loads:
        load.start()
    stores = []
    for n, load in enumerate(loads):
        load.wait()
        cuts = (
            held.at[n],
            held.at[n, pl.ds(core * far, rest)],
            held.at[n, pl.ds((1 - core) * rest, far)],
            held.at[n, pl.ds(core * rest, far)],
        )
        for i, cut in enumerate(cuts):
            store = pltpu.make_async_copy(cut, outs[4 * n + i], sems.at[n, i])
            store.start()
            stores.append(store)
    for store in stores:
        store.wait()


def packed(p_blocks, d_blocks, per, far):
    slab, _, side, _ = p_blocks.shape
    dtype = p_blocks.dtype
    shapes = [(slab, per), (slab - far, per), (far, per), (far, per)] * 2
    outs = pl.pallas_call(
        functools.partial(pack_kernel, far),
        in_specs=[pl.BlockSpec(memory_space=pl.ANY)] * 2,
        out_specs=[pl.BlockSpec(memory_space=pl.ANY)] * 8,
        out_shape=[jax.ShapeDtypeStruct(s + (side, side), dtype) for s in shapes],
        scratch_shapes=[
            pltpu.VMEM((2, slab, per, side, side), dtype),
            pltpu.SemaphoreType.DMA((2, 5)),
        ],
        compiler_params=pltpu.CompilerParams(vmem_limit_bytes=VMEM_LIMIT),
        cost_estimate=pl.CostEstimate(flops=3_000_000_000, bytes_accessed=1 << 22, transcendentals=0),
        name="pack",
    )(p_blocks, d_blocks)
    return outs[:4], outs[4:]


class Lists:
    def __init__(self, slab, slots, per, n_lists, kept):
        self.slab, self.slots, self.per, self.n_lists = slab, slots, per, n_lists
        self.pitch = slots * per + GROUP
        self.counts = [n * slab for n in range(n_lists)]
        self.kept = n_lists * slab if kept else None
        base = n_lists * slab + (2 * slab * per if kept else 0)
        self.lists = [base + n * slab * self.pitch for n in range(n_lists)]
        self.size = base + n_lists * slab * self.pitch


def plan_kernel(lay, reach, window_rows, products, table, row_slot, *refs):
    n = 1 + max(max(product) for product in products)
    cols_hbm, outs = refs[:n], refs[n : 2 * n]
    meta = refs[2 * n]
    cols, inverse, (slot_of, sems) = refs[2 * n + 1 : 3 * n + 1], refs[3 * n + 1 : 4 * n + 1], refs[-2:]
    slab, slots, per = lay.slab, lay.slots, lay.per
    rows = row_slot.shape[0]
    index, rep = lax.axis_index("rows"), lax.axis_index("rep")
    row_start = index * slab
    slabs = rows // slab
    width = 2 * reach + 1
    table_base = (index % 2) * (width * slab)

    copies = []
    for which in range(n):
        for near in range(width):
            at = (index + near + slabs - reach) & (slabs - 1)
            copies.append(
                pltpu.make_async_copy(
                    cols_hbm[which].at[pl.ds(at * slab, slab)],
                    cols[which].at[pl.ds(near * slab, slab)],
                    sems.at[which * width + near],
                )
            )
    for copy in copies:
        copy.start()
    span = 2 * slots + SPREAD_ROWS
    for column in range(-span, slab + span):
        for inv in inverse + ((slot_of,) if lay.kept is not None else ()):
            inv[(row_start + column + rows) & (rows - 1)] = slots
    for copy in copies:
        copy.wait()
    relative = [(q ^ rep) * per for q in range(slots // per)]
    here = reach * slab

    def row(s, carry):
        for which in range(n):
            for j in range(slots):
                inverse[which][outs[which][s, j]] = relative[j // per] + j % per
        starts = [base + s * lay.pitch for base in lay.lists]
        ends = list(starts)
        lefts = sorted({product[0] for product in products})
        for k in range(slots):
            for left in lefts:
                offset = (row_slot[cols[left][here + s, k]] - row_start + here + rows) & (rows - 1)
                place = table[table_base + offset]
                code = (place << 4) + (k << 13)
                found = []
                for number, (which_left, right, out) in enumerate(products):
                    if which_left != left:
                        continue
                    for m in range(per):
                        target = inverse[out][cols[right][offset, rep * per + m]]
                        shift = (right if n > 1 else 0) * window_rows * per + m
                        found.append((number, target, code + (shift << 4) + target))
                for number, target, entry in found:
                    meta[ends[number]] = entry
                    ends[number] += jnp.where(target < slots, 1, 0)
        for number in range(len(products)):
            for u in range(GROUP):
                meta[ends[number] + u] = slots
            meta[lay.counts[number] + s] = ends[number] - starts[number]
        if lay.kept is not None:
            for which in range(n):
                for k in range(slots):
                    slot_of[cols[which][here + s, k]] = k
                for j in range(per):
                    at = lay.kept + (which * slab + s) * per + j
                    meta[at] = slot_of[outs[which][s, rep * per + j]]
                for k in range(slots):
                    slot_of[cols[which][here + s, k]] = slots
        for which in range(n):
            for j in range(slots):
                inverse[which][outs[which][s, j]] = slots
        return carry

    lax.fori_loop(0, slab, row, 0)


def planned(lay, reach, window_rows, products, table, row_slot, cols, outs):
    rows, slots = cols[0].shape
    n = len(cols)
    smem, any_spec = pl.BlockSpec(memory_space=pltpu.SMEM), pl.BlockSpec(memory_space=pl.ANY)
    width = 2 * reach + 1
    return pl.pallas_call(
        functools.partial(plan_kernel, lay, reach, window_rows, products),
        in_specs=[smem, smem] + [any_spec] * n + [smem] * n,
        out_specs=smem,
        out_shape=jax.ShapeDtypeStruct((lay.size,), jnp.int32),
        scratch_shapes=[pltpu.SMEM((width * lay.slab, slots), jnp.int32)] * n
        + [pltpu.SMEM((rows,), jnp.int32)] * (n + 1)
        + [pltpu.SemaphoreType.DMA((n * width,))],
        compiler_params=pltpu.CompilerParams(vmem_limit_bytes=VMEM_LIMIT),
        cost_estimate=pl.CostEstimate(flops=4_000_000_000, bytes_accessed=65536, transcendentals=0),
        name="plan",
    )(jnp.asarray(table), row_slot, *cols, *outs)


def kept_kernel(lay, meta, p_ref, d_ref, out_ref, held, sems, out_sem):
    slab, slots, per = lay.slab, lay.slots, lay.per
    loads = []
    for which, blocks in enumerate((p_ref, d_ref)):
        for s in range(slab):
            for j in range(per):
                n = (which * slab + s) * per + j
                k = meta[lay.kept + n]
                load = pltpu.make_async_copy(
                    blocks.at[s, jnp.minimum(k, slots - 1)], held.at[which, s, j], sems.at[n]
                )
                load.start()
                loads.append((load, k, which, s, j))
    for load, k, which, s, j in loads:
        load.wait()

        @pl.when(k == slots)
        def _():
            held[which, s, j] = jnp.zeros(held.shape[3:], held.dtype)

    store = pltpu.make_async_copy(held, out_ref, out_sem)
    store.start()
    store.wait()


def kept_blocks(lay, meta, p_blocks, d_blocks):
    slab, _, side, _ = p_blocks.shape
    shape = (2, slab, lay.per, side, side)
    return pl.pallas_call(
        functools.partial(kept_kernel, lay),
        in_specs=[pl.BlockSpec(memory_space=pltpu.SMEM)] + [pl.BlockSpec(memory_space=pl.ANY)] * 2,
        out_specs=pl.BlockSpec(memory_space=pl.ANY),
        out_shape=jax.ShapeDtypeStruct(shape, p_blocks.dtype),
        scratch_shapes=[
            pltpu.VMEM(shape, p_blocks.dtype),
            pltpu.SemaphoreType.DMA((2 * slab * lay.per,)),
            pltpu.SemaphoreType.DMA,
        ],
        compiler_params=pltpu.CompilerParams(vmem_limit_bytes=VMEM_LIMIT),
        cost_estimate=pl.CostEstimate(flops=3_000_000_000, bytes_accessed=1 << 21, transcendentals=0),
        name="kept",
    )(meta, p_blocks, d_blocks)


def product_kernel(lay, n_left, sizes, first, halves, meta, *refs):
    left_refs = refs[:n_left]
    pieces = refs[n_left : n_left + n_left * len(sizes)]
    out_refs, (window, total, sems) = refs[-3 - 2 * len(halves) : -3], refs[-3:]
    step = pl.program_id(0)
    row = first + step
    per = lay.per

    @pl.when(step == 0)
    def _():
        copies, base = [], 0
        for index, piece in enumerate(pieces):
            size = sizes[index % len(sizes)]
            copies.append(
                pltpu.make_async_copy(
                    piece, window.at[pl.ds(base * per, size * per)], sems.at[index]
                )
            )
            base += size
        for copy in copies:
            copy.start()
        for copy in copies:
            copy.wait()

    total[...] = jnp.zeros_like(total)
    for n in range(n_left):

        def add_group(group, carry):
            for u in range(GROUP):
                code = meta[lay.lists[n] + row * lay.pitch + group * GROUP + u]
                total[code & 15] += jnp.dot(
                    left_refs[n][0, code >> 13], window[(code >> 4) & 511],
                    preferred_element_type=jnp.float32,
                )
            return carry

        groups = (meta[lay.counts[n] + row] + GROUP - 1) // GROUP
        lax.fori_loop(0, groups, add_group, 0)

    def store(send_ref, keep_ref, order):
        for at, q in enumerate(order):
            ref = keep_ref if at < 2 else send_ref
            for j in range(per):
                ref[at % 2, 0, j] = total[q * per + j].astype(ref.dtype)

    half_rows = lay.slab // 2
    for index, half in enumerate(halves):
        refs_of = out_refs[2 * index], out_refs[2 * index + 1]
        if len(halves) == 1:
            store(*refs_of, HALF_ORDER[half])
        else:
            pl.when(row // half_rows == half)(
                functools.partial(store, *refs_of, HALF_ORDER[half])
            )


HALF_ORDER = ((0, 3, 1, 2), (0, 1, 3, 2))


def block_products(lay, lefts, windows, sizes, meta, halves):
    slab, slots, side, _ = lefts[0].shape
    per = lay.per
    pieces = [piece.reshape(-1, side, side) for window in windows for piece in window]
    rows_in = len(windows) * sum(sizes)
    dtype = lefts[0].dtype
    half_rows = slab // 2
    first, steps = halves[0] * half_rows, len(halves) * half_rows
    any_spec = pl.BlockSpec(memory_space=pl.ANY)
    out_specs = []
    for index in range(len(halves)):
        spec = pl.BlockSpec(
            (2, 1, per, side, side),
            lambda s, *_, low=index * half_rows: (
                0, jnp.clip(s - low, 0, half_rows - 1), 0, 0, 0,
            ),
        )
        out_specs += [spec, spec]
    return pl.pallas_call(
        functools.partial(product_kernel, lay, len(lefts), sizes, first, halves),
        grid_spec=pltpu.PrefetchScalarGridSpec(
            num_scalar_prefetch=1,
            grid=(steps,),
            in_specs=[
                pl.BlockSpec((1, slots, side, side), lambda s, *_: (first + s, 0, 0, 0))
            ] * len(lefts)
            + [any_spec] * len(pieces),
            out_specs=out_specs,
            scratch_shapes=[
                pltpu.VMEM((rows_in * per, side, side), dtype),
                pltpu.VMEM((slots + 1, side, side), jnp.float32),
                pltpu.SemaphoreType.DMA((len(pieces),)),
            ],
        ),
        out_shape=[jax.ShapeDtypeStruct((2, half_rows, per, side, side), jnp.bfloat16)]
        * (2 * len(halves)),
        compiler_params=pltpu.CompilerParams(
            dimension_semantics=("arbitrary",), vmem_limit_bytes=VMEM_LIMIT
        ),
        cost_estimate=pl.CostEstimate(
            flops=8_000_000_000,
            bytes_accessed=2 * (rows_in * per + 2 * slab * slots) * side * side,
            transcendentals=0,
        ),
    )(meta, *lefts, *pieces)


def met(value, flip):
    return lax.ppermute(value, "rep", [(i, i ^ flip) for i in range(lax.axis_size("rep"))])


def finish_kernel(rows, branch_ref, *refs):
    kept_ref, out_ref = refs[-2:]
    step = pl.program_id(0)
    half_steps = pl.num_programs(0) // 2

    def store(keep_ref, first_ref, second_ref):
        for s in range(rows):
            squaring = branch_ref[step * rows + s] == 1
            total = keep_ref[0, s].astype(jnp.float32) + first_ref[0, s].astype(jnp.float32)
            total = total + second_ref[s].astype(jnp.float32)
            kept = kept_ref[0, s].astype(jnp.float32)
            out_ref[s] = jnp.where(squaring, total, 2.0 * kept - total).astype(out_ref.dtype)

    for half in range(2):
        pl.when(step // half_steps == half)(
            functools.partial(store, *refs[3 * half : 3 * half + 3])
        )


def finish(halves, kept, which, branch):
    _, half_rows, per, side, _ = halves[0][0].shape
    slab = 2 * half_rows
    rows = 2
    half_steps = half_rows // rows
    in_specs = []
    for half in range(2):

        def at(s, *_, low=half * half_steps):
            return jnp.clip(s - low, 0, half_steps - 1)

        pair = pl.BlockSpec(
            (1, rows, per, side, side), lambda s, *_, at=at: (0, at(s), 0, 0, 0)
        )
        single = pl.BlockSpec((rows, per, side, side), lambda s, *_, at=at: (at(s), 0, 0, 0))
        in_specs += [pair, pair, single]
    in_specs.append(
        pl.BlockSpec((1, rows, per, side, side), lambda s, *_: (which, s, 0, 0, 0))
    )
    return pl.pallas_call(
        functools.partial(finish_kernel, rows),
        grid_spec=pltpu.PrefetchScalarGridSpec(
            num_scalar_prefetch=1,
            grid=(slab // rows,),
            in_specs=in_specs,
            out_specs=pl.BlockSpec((rows, per, side, side), lambda s, *_: (s, 0, 0, 0)),
        ),
        out_shape=jax.ShapeDtypeStruct((slab, per, side, side), jnp.bfloat16),
        compiler_params=pltpu.CompilerParams(
            dimension_semantics=("arbitrary",), vmem_limit_bytes=VMEM_LIMIT
        ),
        cost_estimate=pl.CostEstimate(flops=2_000_000_000, bytes_accessed=4 << 20, transcendentals=0),
        name="finish",
    )(branch, *halves[0], *halves[1], kept)


def pair_sum(keep, got):
    return (keep[1].astype(jnp.float32) + got[1].astype(jnp.float32)).astype(jnp.bfloat16)


def step(p_blocks, d_blocks, p_cols, d_cols, out_pcols, out_dcols, row_slot, branch):
    slab, slots, _, _ = p_blocks.shape
    per = slots // lax.axis_size("rep")
    margin = slots + 2 * SPREAD_ROWS
    reach = -(-margin // slab)
    far = margin - 2 * slab
    sizes, table = window_table(slab, margin)
    table = table * per
    window_rows = sum(sizes)

    def outer(pieces):
        part, near, rest, edge = pieces
        out1 = swapped(part, -1, 1)
        far2 = swapped(rest, 2, -2)
        near2 = swapped(near, 2, -2)
        out3 = swapped(edge, -3, 3)
        in1 = swapped(part, 1, -1)
        return part, in1, out1, near2, far2, out3

    def inner(pieces):
        return pieces + (swapped(pieces[2], 1, -1), swapped(pieces[4], 1, -1))

    p_pieces, d_pieces = packed(p_blocks, d_blocks, per, far)
    p_window = outer(p_pieces)
    d_window = outer(d_pieces)
    square_lay = Lists(slab, slots, per, 1, False)
    tangent_lay = Lists(slab, slots, per, 2, True)
    square_meta = planned(
        square_lay, reach, window_rows, ((0, 0, 0),), table, row_slot, (p_cols,), (out_pcols,)
    )
    p_window = inner(p_window)
    d_window = inner(d_window)
    square = block_products(square_lay, (p_blocks,), (p_window,), sizes, square_meta, (0, 1))
    square, later_slot = lax.optimization_barrier((square, row_slot))
    sent_a, keep_a, sent_b, keep_b = square
    first_a = met(sent_a, 1)
    first_b = met(sent_b, 3)

    tangent_meta = planned(
        tangent_lay, reach, window_rows, ((0, 1, 1), (1, 0, 1)), table, later_slot,
        (p_cols, d_cols), (out_pcols, out_dcols),
    )
    kept = kept_blocks(tangent_lay, tangent_meta, p_blocks, d_blocks)
    kept, meta_a = lax.optimization_barrier((kept, tangent_meta))
    lefts, windows = (p_blocks, d_blocks), (p_window, d_window)
    tsent_a, tkeep_a = block_products(tangent_lay, lefts, windows, sizes, meta_a, (0,))
    (tsent_a, tkeep_a), (first_a, first_b) = lax.optimization_barrier(
        ((tsent_a, tkeep_a), (first_a, first_b))
    )
    middle_a, middle_b = pair_sum(keep_a, first_a), pair_sum(keep_b, first_b)
    middle_a, middle_b, meta_b = lax.optimization_barrier((middle_a, middle_b, meta_a))
    second_a = met(middle_a, 3)
    second_b = met(middle_b, 1)
    tfirst_a = met(tsent_a, 1)
    tsent_b, tkeep_b = block_products(tangent_lay, lefts, windows, sizes, meta_b, (1,))
    tfirst_b = met(tsent_b, 3)
    tmiddle_a = pair_sum(tkeep_a, tfirst_a)
    tmiddle_b = pair_sum(tkeep_b, tfirst_b)
    tsecond_a = met(tmiddle_a, 3)
    tsecond_b = met(tmiddle_b, 1)
    next_p = finish(
        ((keep_a, first_a, second_a), (keep_b, first_b, second_b)), kept, 0, branch
    )
    next_d = finish(
        ((tkeep_a, tfirst_a, tsecond_a), (tkeep_b, tfirst_b, tsecond_b)), kept, 1, branch
    )
    return next_p, next_d


def solution(mesh):
    return jax.shard_map(
        step,
        mesh=mesh,
        in_specs=(
            P("rows", None, None, None),
            P("rows", None, None, None),
            P(),
            P(),
            P("rows", None),
            P("rows", None),
            P(),
            P("rows"),
        ),
        out_specs=(P("rows", "rep", None, None), P("rows", "rep", None, None)),
        check_vma=False,
    )
```

time: 153 us -> 156 us (1.020)
  waiting for transfers between devices: 62.2 us -> 47.4 us
  Pallas kernels: 53.4 us -> 62 us
  other arithmetic: 0.61 us -> 6.42 us
  starting transfers between devices: 29.3 us -> 34.1 us
    all_to_all x2 -> x0, waiting for transfers between devices: 31.9 us -> none  [the longest x1 31.9 us: step(): lax.all_to_all(tangent, 'rep', split_axis=0, concat_axis=0, tiled=True)]
    ppermute x0 -> x8, waiting for transfers between devices: none -> 22.1 us  [met(): lax.ppermute(value, 'rep', [(i, i ^ flip) for i in range(lax.axis_size('r...]
    ppermute x0 -> x8, starting transfers between devices: none -> 13.1 us  [met(): lax.ppermute(value, 'rep', [(i, i ^ flip) for i in range(lax.axis_size('r...]
    all_to_all x2 -> x0, starting transfers between devices: 11.4 us -> none  [the longest x1 5.75 us: step(): lax.all_to_all(tangent, 'rep', split_axis=0, concat_axis=0, tiled=True)]
    pallas_call x3 -> x5, Pallas kernels: 34.1 us -> 45.3 us  [the longest x3 33.1 us: block_products(): pl.pallas_call(functools.partial(product_kernel, lay, len(lefts), sizes,...]
    convert_element_type x0 -> x3, other arithmetic: none -> 6.42 us  [pair_sum(): (keep[1].astype(jnp.float32) + got[1].astype(jnp.float32)).astype(jnp.bfl...]
    ppermute x14, waiting for transfers between devices: 30.3 us -> 25.3 us  [swapped(): return lax.ppermute(value, 'rows', pairs)]
    pallas_call x2 -> x1, Pallas kernels: 6.21 us -> 3.03 us  [packed(): pl.pallas_call(functools.partial(pack_kernel, far), in_specs=[pl.BlockSpe...]
  transfers between devices with their start and end apart: 16 -> 22, of which waited for: 3 -> 9; matrix products, arithmetic and copies ran while one was open for 3% -> 4% of each run, Pallas kernels for 30% -> 35%
where the time goes in v1:
time: 156 us; the launch traced here: 154 us
  Pallas kernels  62 us (40%)
  waiting for transfers between devices  47.4 us (30%)
  starting transfers between devices  34.1 us (22%)
  other arithmetic  6.42 us (4%)
  local copies, waits for them, and re-layouts  3.41 us (2%)
    pallas_call x3, Pallas kernels, block_products(): pl.pallas_call(functools.partial(product_kernel, lay, len(lefts), sizes,...  33.1 us
    ppermute x14, waiting for transfers between devices, swapped(): return lax.ppermute(value, 'rows', pairs)  25.3 us
    ppermute x8, waiting for transfers between devices, met(): lax.ppermute(value, 'rep', [(i, i ^ flip) for i in range(lax.axis_size('r...  22.1 us
    ppermute x14, starting transfers between devices, swapped(): return lax.ppermute(value, 'rows', pairs)  20.9 us
    ppermute x8, starting transfers between devices, met(): lax.ppermute(value, 'rep', [(i, i ^ flip) for i in range(lax.axis_size('r...  13.1 us
    pallas_call x2, Pallas kernels, planned(): pl.pallas_call(functools.partial(plan_kernel, lay, reach, window_rows, pr...  12.2 us
    pallas_call x2, Pallas kernels, finish(): pl.pallas_call(functools.partial(finish_kernel, rows), grid_spec=pltpu.Pr...  9.77 us
    convert_element_type x3, other arithmetic, pair_sum(): (keep[1].astype(jnp.float32) + got[1].astype(jnp.float32)).astype(jnp.bfl...  6.42 us
  transfers between devices with their start and end apart: 22, of which 9 were waited for; matrix products, arithmetic and copies ran while one was open for 4% of the time, Pallas kernels for 35%

profile of v1, /device:TPU:8, one launch (start us, length us, event | category | flops | bytes accessed | tf_op | source)
XLA Modules:
  0.0 154.0 jit_solution(10494504708142424646)
XLA Ops:
  0.6 3.0 %pack.1 = (bf16[8,3,128,128]{3,2,1,0:T(8,128)(2,1)}, bf16[6,3,128,128]{3,2,1,0:T(8,128)(2,1)}, bf16[2,3,128,128]{3,2,1,0:T(8,128)(2,1)}, bf16[2,3,128,128]{3,2,1...) custom-call(bf16[8,12,128,128]{3,2,1,0:T(8,128)(2,1)} %refs_0_.9, ...), custom_call_target="tpu_custom_call" | custom-call | flops 3000000000 | bytes 4194304 | tf_op jit(solution)/shard_map/pack/pallas_call | solution.py:75
  3.7 7.6 %collective-permute-start.1 = (bf16[8,3,128,128]{3,2,1,0:T(8,128)(2,1)}, bf16[8,3,128,128]{3,2,1,0:T(8,128)(2,1)}, u32[]{:S(2)}, u32[]{:S(2)}) collective-permute-start(bf16[8,3,128,128]{3,2,1,0:T(8,128)(2,1)} %get-tuple-element.32), channel_id=1, source_target_pairs={{0,252},{4,8},{8,4},{12,16},{16,12},{20,24},{24,20},{28,32},{32,28... | collective-permute-start | bytes 2359304 | tf_op jit(solution)/shard_map/ppermute | solution.py:40
  11.3 0.2 collective-permute-start
  11.5 5.3 %collective-permute-start.8 = (bf16[8,3,128,128]{3,2,1,0:T(8,128)(2,1)}, bf16[8,3,128,128]{3,2,1,0:T(8,128)(2,1)}, u32[]{:S(2)}, u32[]{:S(2)}) collective-permute-start(bf16[8,3,128,128]{3,2,1,0:T(8,128)(2,1)} %get-tuple-element.43), channel_id=1, source_target_pairs={{0,252},{4,8},{8,4},{12,16},{16,12},{20,24},{24,20},{28,32},{32,28... | collective-permute-start | bytes 2359304 | tf_op jit(solution)/shard_map/ppermute | solution.py:40
  16.7 6.6 %collective-permute-done.1 = bf16[8,3,128,128]{3,2,1,0:T(8,128)(2,1)} collective-permute-done((bf16[8,3,128,128]{3,2,1,0:T(8,128)(2,1)}, bf16[8,3,128,128]{3,2,1,0:T(8,128)(2,1)}, u32[]{:S(2)}, u32[]{:S(2)}) %collective-permute-start.1) | collective-permute-done | bytes 786464 | tf_op jit(solution)/shard_map/ppermute | solution.py:40
  23.4 0.0 collective-permute-start.5
  23.4 2.7 %collective-permute-start.4 = (bf16[2,3,128,128]{3,2,1,0:T(8,128)(2,1)}, bf16[2,3,128,128]{3,2,1,0:T(8,128)(2,1)}, u32[]{:S(2)}, u32[]{:S(2)}) collective-permute-start(bf16[2,3,128,128]{3,2,1,0:T(8,128)(2,1)} %get-tuple-element.35), channel_id=1, source_target_pairs={{0,244},{4,16},{8,252},{12,24},{16,4},{20,32},{24,12},{28,40},{32,... | collective-permute-start | bytes 589832 | tf_op jit(solution)/shard_map/ppermute | solution.py:40
  26.0 0.0 collective-permute-done.3
  26.0 2.8 %collective-permute-start.2 = (bf16[6,3,128,128]{3,2,1,0:T(8,128)(2,1)}, bf16[6,3,128,128]{3,2,1,0:T(8,128)(2,1)}, u32[]{:S(2)}, u32[]{:S(2)}) collective-permute-start(bf16[6,3,128,128]{3,2,1,0:T(8,128)(2,1)} %get-tuple-element.33), channel_id=1, source_target_pairs={{0,8},{4,252},{8,16},{12,4},{16,24},{20,12},{24,32},{28,20},{32,40... | collective-permute-start | bytes 1769480 | tf_op jit(solution)/shard_map/ppermute | solution.py:40
  28.8 11.8 %collective-permute-done.4 = bf16[2,3,128,128]{3,2,1,0:T(8,128)(2,1)} collective-permute-done((bf16[2,3,128,128]{3,2,1,0:T(8,128)(2,1)}, bf16[2,3,128,128]{3,2,1,0:T(8,128)(2,1)}, u32[]{:S(2)}, u32[]{:S(2)}) %collective-permute-start.4) | collective-permute-done | bytes 196640 | tf_op jit(solution)/shard_map/ppermute | solution.py:40
  40.6 0.0 collective-permute-start.10
  40.6 0.9 copy.11.refs_0_
  41.5 1.6 %copy.13.refs_1_ = s32[512,12]{1,0:T(8,128)} copy(s32[512,12]{0,1:T(8,128)} %param.12) | data formatting | bytes 49152 | tf_op args[3]
  43.1 6.8 %collective-permute-done.10 = bf16[2,3,128,128]{3,2,1,0:T(8,128)(2,1)} collective-permute-done((bf16[2,3,128,128]{3,2,1,0:T(8,128)(2,1)}, bf16[2,3,128,128]{3,2,1,0:T(8,128)(2,1)}, u32[]{:S(2)}, u32[]{:S(2)}) %collective-permute-start.10) | collective-permute-done | bytes 196640 | tf_op jit(solution)/shard_map/ppermute | solution.py:40
  49.9 0.0 collective-permute-start.6
  49.9 4.4 %plan.2.meta = s32[360]{0:T(512)} custom-call(s32[112]{0:T(128)} %constant.2.clone.table, s32[512]{0:T(512)} %row_slot.2, s32[512,12]{1,0:T(8,128)} %copy.11.refs_0_, s32[8,12]{1,0:T(8,128)} %refs_2_.1), custom_call_target="tpu_custom_call" | custom-call | flops 4000000000 | bytes 65536 | tf_op jit(solution)/shard_map/plan/pallas_call | solution.py:186
  54.3 0.6 collective-permute-start.7
  54.9 0.0 collective-permute-done.2
  54.9 0.0 collective-permute-start.9
  54.9 0.0 collective-permute-done
  54.9 1.4 collective-permute-start.11
  56.3 0.0 collective-permute-done.5
  56.3 0.5 collective-permute-start.12
  56.8 11.8 %shard_map.104 = (bf16[2,4,3,128,128]{4,3,2,1,0:T(8,128)(2,1)}, bf16[2,4,3,128,128]{4,3,2,1,0:T(8,128)(2,1)}, bf16[2,4,3,128,128]{4,3,2,1,0:T(8,128)(2,1)}, bf16[2,4,3,128,128]{4,3,2,1,0:T(8,128)(2,1)}) custom-call(s32[360]{0:T(512)} %plan.2.meta, bf16[8,12,128,128]{3,2,1,0:T(8,128)(2,1)} %refs_0_.9, bf16[24,128,128]{2,1,0:T(8,128)(2,1)} %bitcast.24, ...), custom_call_target="tpu_custom_call" | custom-call | flops 8000000000 | bytes 10616832 | tf_op jit(solution)/shard_map/pallas_call | solution.py:321
  68.7 7.8 %plan.3.meta = s32[768]{0:T(1024)} custom-call(s32[112]{0:T(128)} %constant.2.clone.table, s32[512]{0:T(512)} %row_slot.2, s32[512,12]{1,0:T(8,128)} %copy.11.refs_0_, s32[512,12]{1,0:T(8,128)} %copy.13.refs_1_, s32[8,12]{1,0:T(8,128)} %refs_2_.1, s32[8,12]{1,0:T(8,128)} %refs_3_.1), custom_call_target="tpu_custom_call" | custom-call | flops 4000000000 | bytes 65536 | tf_op jit(solution)/shard_map/plan/pallas_call | solution.py:186
  76.5 0.9 collective-permute-start.14
  77.4 1.6 %collective-permute-start.15 = (bf16[2,4,3,128,128]{4,3,2,1,0:T(8,128)(2,1)}, bf16[2,4,3,128,128]{4,3,2,1,0:T(8,128)(2,1)}, u32[]{:S(2)}, u32[]{:S(2)}) collective-permute-start(bf16[2,4,3,128,128]{4,3,2,1,0:T(8,128)(2,1)} %get-tuple-element.50), channel_id=1, source_target_pairs={{0,3},{1,2},{2,1},{3,0},{4,7},{5,6},{6,5},{7,4},{8,11},{9,10},{10,... | collective-permute-start | bytes 2359304 | tf_op jit(solution)/shard_map/ppermute | solution.py:351
  79.0 3.9 %kept.1.refs_6_ = bf16[2,8,3,128,128]{4,3,2,1,0:T(8,128)(2,1)} custom-call(s32[768]{0:T(1024)} %plan.3.meta, bf16[8,12,128,128]{3,2,1,0:T(8,128)(2,1)} %refs_0_.9, bf16[8,12,128,128]{3,2,1,0:T(8,128)(2,1)} %refs_1_.8), custom_call_target="tpu_custom_call" | custom-call | flops 3000000000 | bytes 2097152 | tf_op jit(solution)/shard_map/kept/pallas_call | solution.py:228
  82.9 10.5 %shard_map.105 = (bf16[2,4,3,128,128]{4,3,2,1,0:T(8,128)(2,1)}, bf16[2,4,3,128,128]{4,3,2,1,0:T(8,128)(2,1)}) custom-call(s32[768]{0:T(1024)} %plan.3.meta, bf16[8,12,128,128]{3,2,1,0:T(8,128)(2,1)} %refs_0_.9, bf16[8,12,128,128]{3,2,1,0:T(8,128)(2,1)} %refs_1_.8, bf16[24,128,128]{2,1,0:T(8,128)(2,1)} %bitcast.25, ...), custom_call_target="tpu_custom_call" | custom-call | flops 8000000000 | bytes 14942208 | tf_op jit(solution)/shard_map/pallas_call | solution.py:321
  93.4 2.6 %collective-permute-done.14.refs_1_ = bf16[2,4,3,128,128]{4,3,2,1,0:T(8,128)(2,1)} collective-permute-done((bf16[2,4,3,128,128]{4,3,2,1,0:T(8,128)(2,1)}, bf16[2,4,3,128,128]{4,3,2,1,0:T(8,128)(2,1)}, u32[]{:S(2)}, u32[]{:S(2)}) %collective-permute-start.14) | collective-permute-done | bytes 786464 | tf_op jit(solution)/shard_map/ppermute | solution.py:351
  96.0 0.8 collective-permute-done.15.refs_4_
  96.8 2.6 %fusion = (bf16[4,3,128,128]{3,2,1,0:T(8,128)(2,1)}, bf16[4,3,128,128]{3,2,1,0:T(8,128)(2,1)}) fusion(bf16[2,4,3,128,128]{4,3,2,1,0:T(8,128)(2,1)} %collective-permute-done.14.refs_1_, bf16[2,4,3,128,128]{4,3,2,1,0:T(8,128)(2,1)} %get-tuple-element.40.refs_0_, bf16[2,4,3,128,128]{4,3,2,1,0:T(8,128)(2,1)} %collective-permute-done.15.refs_4_, ...), kind=kLoop, calls=%fused_computation.4 | loop fusion | flops 1572864 | bytes 2359296 | tf_op jit(solution)/shard_map/convert_element_type | solution.py:410
  99.4 2.1 %collective-permute-start.18 = (bf16[2,4,3,128,128]{4,3,2,1,0:T(8,128)(2,1)}, bf16[2,4,3,128,128]{4,3,2,1,0:T(8,128)(2,1)}, u32[]{:S(2)}, u32[]{:S(2)}) collective-permute-start(bf16[2,4,3,128,128]{4,3,2,1,0:T(8,128)(2,1)} %get-tuple-element.58), channel_id=1, source_target_pairs={{0,1},{1,0},{2,3},{3,2},{4,5},{5,4},{6,7},{7,6},{8,9},{9,8},{10,11... | collective-permute-start | bytes 2359304 | tf_op jit(solution)/shard_map/ppermute | solution.py:351
  101.5 10.8 %shard_map.106 = (bf16[2,4,3,128,128]{4,3,2,1,0:T(8,128)(2,1)}, bf16[2,4,3,128,128]{4,3,2,1,0:T(8,128)(2,1)}) custom-call(s32[768]{0:T(1024)} %plan.3.meta, bf16[8,12,128,128]{3,2,1,0:T(8,128)(2,1)} %refs_0_.9, bf16[8,12,128,128]{3,2,1,0:T(8,128)(2,1)} %refs_1_.8, bf16[24,128,128]{2,1,0:T(8,128)(2,1)} %bitcast.26, ...), custom_call_target="tpu_custom_call" | custom-call | flops 8000000000 | bytes 14942208 | tf_op jit(solution)/shard_map/pallas_call | solution.py:321
  112.3 2.1 %collective-permute-start.20 = (bf16[2,4,3,128,128]{4,3,2,1,0:T(8,128)(2,1)}, bf16[2,4,3,128,128]{4,3,2,1,0:T(8,128)(2,1)S(1)}, u32[]{:S(2)}, u32[]{:S(2)}) collective-permute-start(bf16[2,4,3,128,128]{4,3,2,1,0:T(8,128)(2,1)} %get-tuple-element.61), channel_id=1, source_target_pairs={{0,3},{1,2},{2,1},{3,0},{4,7},{5,6},{6,5},{7,4},{8,11},{9,10},{10,... | collective-permute-start | bytes 2359304 | tf_op jit(solution)/shard_map/ppermute | solution.py:351
  114.4 0.1 collective-permute-start.16
  114.5 1.6 %collective-permute-start.17 = (bf16[4,3,128,128]{3,2,1,0:T(8,128)(2,1)}, bf16[4,3,128,128]{3,2,1,0:T(8,128)(2,1)}, u32[]{:S(2)}, u32[]{:S(2)}) collective-permute-start(bf16[4,3,128,128]{3,2,1,0:T(8,128)(2,1)} %get-tuple-element.55), channel_id=1, source_target_pairs={{0,1},{1,0},{2,3},{3,2},{4,5},{5,4},{6,7},{7,6},{8,9},{9,8},{10,11... | collective-permute-start | bytes 1179656 | tf_op jit(solution)/shard_map/ppermute | solution.py:351
  116.1 3.2 %collective-permute-done.18.refs_1_ = bf16[2,4,3,128,128]{4,3,2,1,0:T(8,128)(2,1)} collective-permute-done((bf16[2,4,3,128,128]{4,3,2,1,0:T(8,128)(2,1)}, bf16[2,4,3,128,128]{4,3,2,1,0:T(8,128)(2,1)}, u32[]{:S(2)}, u32[]{:S(2)}) %collective-permute-start.18) | collective-permute-done | bytes 786464 | tf_op jit(solution)/shard_map/ppermute | solution.py:351
  119.2 2.0 %fusion.2 = bf16[4,3,128,128]{3,2,1,0:T(8,128)(2,1)} fusion(bf16[2,4,3,128,128]{4,3,2,1,0:T(8,128)(2,1)} %collective-permute-done.18.refs_1_, bf16[2,4,3,128,128]{4,3,2,1,0:T(8,128)(2,1)} %get-tuple-element.57.refs_0_), kind=kLoop, calls=%fused_computation.6 | loop fusion | flops 786432 | bytes 1179648 | tf_op jit(solution)/shard_map/convert_element_type | solution.py:410
  121.2 3.0 %collective-permute-start.19 = (bf16[4,3,128,128]{3,2,1,0:T(8,128)(2,1)}, bf16[4,3,128,128]{3,2,1,0:T(8,128)(2,1)}, u32[]{:S(2)}, u32[]{:S(2)}) collective-permute-start(bf16[4,3,128,128]{3,2,1,0:T(8,128)(2,1)} %fusion.2), channel_id=1, source_target_pairs={{0,3},{1,2},{2,1},{3,0},{4,7},{5,6},{6,5},{7,4},{8,11},{9,10},{10,... | collective-permute-start | bytes 1179656 | tf_op jit(solution)/shard_map/ppermute | solution.py:351
  124.2 8.8 %collective-permute-done.20.refs_4_ = bf16[2,4,3,128,128]{4,3,2,1,0:T(8,128)(2,1)S(1)} collective-permute-done((bf16[2,4,3,128,128]{4,3,2,1,0:T(8,128)(2,1)}, bf16[2,4,3,128,128]{4,3,2,1,0:T(8,128)(2,1)S(1)}, u32[]{:S(2)}, u32[]{:S(2)}) %collective-permute-start.20) | collective-permute-done | bytes 786464 | tf_op jit(solution)/shard_map/ppermute | solution.py:351
  133.0 0.9 copy-done
  133.9 1.9 %fusion.3 = bf16[4,3,128,128]{3,2,1,0:T(8,128)(2,1)} fusion(bf16[2,4,3,128,128]{4,3,2,1,0:T(8,128)(2,1)S(1)} %collective-permute-done.20.refs_4_, bf16[2,4,3,128,128]{4,3,2,1,0:T(8,128)(2,1)} %get-tuple-element.60.refs_3_), kind=kLoop, calls=%fused_computation.7 | loop fusion | flops 786432 | bytes 1179648 | tf_op jit(solution)/shard_map/convert_element_type | solution.py:410
  135.8 1.7 %collective-permute-start.21 = (bf16[4,3,128,128]{3,2,1,0:T(8,128)(2,1)}, bf16[4,3,128,128]{3,2,1,0:T(8,128)(2,1)}, u32[]{:S(2)}, u32[]{:S(2)}) collective-permute-start(bf16[4,3,128,128]{3,2,1,0:T(8,128)(2,1)} %fusion.3), channel_id=1, source_target_pairs={{0,1},{1,0},{2,3},{3,2},{4,5},{5,4},{6,7},{7,6},{8,9},{9,8},{10,11... | collective-permute-start | bytes 1179656 | tf_op jit(solution)/shard_map/ppermute | solution.py:351
  137.5 4.1 %collective-permute-done.16.refs_2_ = bf16[4,3,128,128]{3,2,1,0:T(8,128)(2,1)} collective-permute-done((bf16[4,3,128,128]{3,2,1,0:T(8,128)(2,1)}, bf16[4,3,128,128]{3,2,1,0:T(8,128)(2,1)}, u32[]{:S(2)}, u32[]{:S(2)}) %collective-permute-start.16) | collective-permute-done | bytes 393248 | tf_op jit(solution)/shard_map/ppermute | solution.py:351
  141.5 4.9 %finish.2 = bf16[8,3,128,128]{3,2,1,0:T(8,128)(2,1)} custom-call(s32[8]{0:T(128)} %branch_ref.3, bf16[2,4,3,128,128]{4,3,2,1,0:T(8,128)(2,1)} %get-tuple-element.40.refs_0_, bf16[2,4,3,128,128]{4,3,2,1,0:T(8,128)(2,1)} %collective-permute-done.14.refs_1_, bf16[4,3,128,128]{3,2,1,0:T(8,128)(2,1)} %collective-permute-done.16.refs_2_, ...), custom_call_target="tpu_custom_call" | custom-call | flops 2000000000 | bytes 4194304 | tf_op jit(solution)/shard_map/finish/pallas_call | solution.py:392
  146.4 2.7 %collective-permute-done.19.refs_2_ = bf16[4,3,128,128]{3,2,1,0:T(8,128)(2,1)} collective-permute-done((bf16[4,3,128,128]{3,2,1,0:T(8,128)(2,1)}, bf16[4,3,128,128]{3,2,1,0:T(8,128)(2,1)}, u32[]{:S(2)}, u32[]{:S(2)}) %collective-permute-start.19) | collective-permute-done | bytes 393248 | tf_op jit(solution)/shard_map/ppermute | solution.py:351
  149.2 4.9 %finish.3 = bf16[8,3,128,128]{3,2,1,0:T(8,128)(2,1)} custom-call(s32[8]{0:T(128)} %branch_ref.3, bf16[2,4,3,128,128]{4,3,2,1,0:T(8,128)(2,1)} %get-tuple-element.57.refs_0_, bf16[2,4,3,128,128]{4,3,2,1,0:T(8,128)(2,1)} %collective-permute-done.18.refs_1_, bf16[4,3,128,128]{3,2,1,0:T(8,128)(2,1)} %collective-permute-done.19.refs_2_, ...), custom_call_target="tpu_custom_call" | custom-call | flops 2000000000 | bytes 4194304 | tf_op jit(solution)/shard_map/finish/pallas_call | solution.py:392
  (14 shorter events, 0.0 us)
Async XLA Ops:
  0.6 40.0 %copy-start.1 = (s32[512,12]{0,1:T(8,128)S(1)}, s32[512,12]{0,1:T(8,128)}, u32[]{:S(2)}) copy-start(s32[512,12]{0,1:T(8,128)} %param.11) | copy-start | bytes 73732
  3.7 19.7 %collective-permute-start.1 = (bf16[8,3,128,128]{3,2,1,0:T(8,128)(2,1)}, bf16[8,3,128,128]{3,2,1,0:T(8,128)(2,1)}, u32[]{:S(2)}, u32[]{:S(2)}) collective-permute-start(bf16[8,3,128,128]{3,2,1,0:T(8,128)(2,1)} %get-tuple-element.32), channel_id=1, source_target_pairs={{0,252},{4,8},{8,4},{12,16},{16,12},{20,24},{24,20},{28,32},{32,28... | collective-permute-start | bytes 2359304 | tf_op jit(solution)/shard_map/ppermute | solution.py:40
  11.3 14.8 %collective-permute-start.3 = (bf16[2,3,128,128]{3,2,1,0:T(8,128)(2,1)}, bf16[2,3,128,128]{3,2,1,0:T(8,128)(2,1)}, u32[]{:S(2)}, u32[]{:S(2)}) collective-permute-start(bf16[2,3,128,128]{3,2,1,0:T(8,128)(2,1)} %get-tuple-element.34), channel_id=1, source_target_pairs={{0,8},{4,252},{8,16},{12,4},{16,24},{20,12},{24,32},{28,20},{32,40... | collective-permute-start | bytes 589832 | tf_op jit(solution)/shard_map/ppermute | solution.py:40
  11.3 43.7 %collective-permute-start = (bf16[8,3,128,128]{3,2,1,0:T(8,128)(2,1)}, bf16[8,3,128,128]{3,2,1,0:T(8,128)(2,1)}, u32[]{:S(2)}, u32[]{:S(2)}) collective-permute-start(bf16[8,3,128,128]{3,2,1,0:T(8,128)(2,1)} %get-tuple-element.32), channel_id=1, source_target_pairs={{0,4},{4,0},{8,12},{12,8},{16,20},{20,16},{24,28},{28,24},{32,36},... | collective-permute-start | bytes 2359304 | tf_op jit(solution)/shard_map/ppermute | solution.py:40
  11.5 44.8 %collective-permute-start.8 = (bf16[8,3,128,128]{3,2,1,0:T(8,128)(2,1)}, bf16[8,3,128,128]{3,2,1,0:T(8,128)(2,1)}, u32[]{:S(2)}, u32[]{:S(2)}) collective-permute-start(bf16[8,3,128,128]{3,2,1,0:T(8,128)(2,1)} %get-tuple-element.43), channel_id=1, source_target_pairs={{0,252},{4,8},{8,4},{12,16},{16,12},{20,24},{24,20},{28,32},{32,28... | collective-permute-start | bytes 2359304 | tf_op jit(solution)/shard_map/ppermute | solution.py:40
  23.4 33.0 %collective-permute-start.5 = (bf16[8,3,128,128]{3,2,1,0:T(8,128)(2,1)}, bf16[8,3,128,128]{3,2,1,0:T(8,128)(2,1)}, u32[]{:S(2)}, u32[]{:S(2)}) collective-permute-start(bf16[8,3,128,128]{3,2,1,0:T(8,128)(2,1)} %collective-permute-done.1), channel_id=1, source_target_pairs={{0,4},{4,0},{8,12},{12,8},{16,20},{20,16},{24,28},{28,24},{32,36},... | collective-permute-start | bytes 2359304 | tf_op jit(solution)/shard_map/ppermute | solution.py:40
  23.4 17.3 %collective-permute-start.4 = (bf16[2,3,128,128]{3,2,1,0:T(8,128)(2,1)}, bf16[2,3,128,128]{3,2,1,0:T(8,128)(2,1)}, u32[]{:S(2)}, u32[]{:S(2)}) collective-permute-start(bf16[2,3,128,128]{3,2,1,0:T(8,128)(2,1)} %get-tuple-element.35), channel_id=1, source_target_pairs={{0,244},{4,16},{8,252},{12,24},{16,4},{20,32},{24,12},{28,40},{32,... | collective-permute-start | bytes 589832 | tf_op jit(solution)/shard_map/ppermute | solution.py:40
  26.0 28.9 %collective-permute-start.2 = (bf16[6,3,128,128]{3,2,1,0:T(8,128)(2,1)}, bf16[6,3,128,128]{3,2,1,0:T(8,128)(2,1)}, u32[]{:S(2)}, u32[]{:S(2)}) collective-permute-start(bf16[6,3,128,128]{3,2,1,0:T(8,128)(2,1)} %get-tuple-element.33), channel_id=1, source_target_pairs={{0,8},{4,252},{8,16},{12,4},{16,24},{20,12},{24,32},{28,20},{32,40... | collective-permute-start | bytes 1769480 | tf_op jit(solution)/shard_map/ppermute | solution.py:40
  40.6 9.3 %collective-permute-start.10 = (bf16[2,3,128,128]{3,2,1,0:T(8,128)(2,1)}, bf16[2,3,128,128]{3,2,1,0:T(8,128)(2,1)}, u32[]{:S(2)}, u32[]{:S(2)}) collective-permute-start(bf16[2,3,128,128]{3,2,1,0:T(8,128)(2,1)} %get-tuple-element.45), channel_id=1, source_target_pairs={{0,8},{4,252},{8,16},{12,4},{16,24},{20,12},{24,32},{28,20},{32,40... | collective-permute-start | bytes 589832 | tf_op jit(solution)/shard_map/ppermute | solution.py:40
  49.9 4.4 %collective-permute-start.6 = (bf16[2,3,128,128]{3,2,1,0:T(8,128)(2,1)}, bf16[2,3,128,128]{3,2,1,0:T(8,128)(2,1)}, u32[]{:S(2)}, u32[]{:S(2)}) collective-permute-start(bf16[2,3,128,128]{3,2,1,0:T(8,128)(2,1)} %collective-permute-done.3), channel_id=1, source_target_pairs={{0,4},{4,0},{8,12},{12,8},{16,20},{20,16},{24,28},{28,24},{32,36},... | collective-permute-start | bytes 589832 | tf_op jit(solution)/shard_map/ppermute | solution.py:40
  54.3 28.6 %collective-permute-start.7 = (bf16[8,3,128,128]{3,2,1,0:T(8,128)(2,1)}, bf16[8,3,128,128]{3,2,1,0:T(8,128)(2,1)}, u32[]{:S(2)}, u32[]{:S(2)}) collective-permute-start(bf16[8,3,128,128]{3,2,1,0:T(8,128)(2,1)} %get-tuple-element.43), channel_id=1, source_target_pairs={{0,4},{4,0},{8,12},{12,8},{16,20},{20,16},{24,28},{28,24},{32,36},... | collective-permute-start | bytes 2359304 | tf_op jit(solution)/shard_map/ppermute | solution.py:40
  54.9 27.9 %collective-permute-start.9 = (bf16[6,3,128,128]{3,2,1,0:T(8,128)(2,1)}, bf16[6,3,128,128]{3,2,1,0:T(8,128)(2,1)}, u32[]{:S(2)}, u32[]{:S(2)}) collective-permute-start(bf16[6,3,128,128]{3,2,1,0:T(8,128)(2,1)} %get-tuple-element.44), channel_id=1, source_target_pairs={{0,8},{4,252},{8,16},{12,4},{16,24},{20,12},{24,32},{28,20},{32,40... | collective-permute-start | bytes 1769480 | tf_op jit(solution)/shard_map/ppermute | solution.py:40
  54.9 21.5 %collective-permute-start.11 = (bf16[2,3,128,128]{3,2,1,0:T(8,128)(2,1)}, bf16[2,3,128,128]{3,2,1,0:T(8,128)(2,1)}, u32[]{:S(2)}, u32[]{:S(2)}) collective-permute-start(bf16[2,3,128,128]{3,2,1,0:T(8,128)(2,1)} %get-tuple-element.46), channel_id=1, source_target_pairs={{0,244},{4,16},{8,252},{12,24},{16,4},{20,32},{24,12},{28,40},{32,... | collective-permute-start | bytes 589832 | tf_op jit(solution)/shard_map/ppermute | solution.py:40
  56.3 21.1 %collective-permute-start.13 = (bf16[2,3,128,128]{3,2,1,0:T(8,128)(2,1)}, bf16[2,3,128,128]{3,2,1,0:T(8,128)(2,1)}, u32[]{:S(2)}, u32[]{:S(2)}) collective-permute-start(bf16[2,3,128,128]{3,2,1,0:T(8,128)(2,1)} %collective-permute-done.10), channel_id=1, source_target_pairs={{0,4},{4,0},{8,12},{12,8},{16,20},{20,16},{24,28},{28,24},{32,36},... | collective-permute-start | bytes 589832 | tf_op jit(solution)/shard_map/ppermute | solution.py:40
  56.3 26.6 %collective-permute-start.12 = (bf16[8,3,128,128]{3,2,1,0:T(8,128)(2,1)}, bf16[8,3,128,128]{3,2,1,0:T(8,128)(2,1)}, u32[]{:S(2)}, u32[]{:S(2)}) collective-permute-start(bf16[8,3,128,128]{3,2,1,0:T(8,128)(2,1)} %collective-permute-done.8), channel_id=1, source_target_pairs={{0,4},{4,0},{8,12},{12,8},{16,20},{20,16},{24,28},{28,24},{32,36},... | collective-permute-start | bytes 2359304 | tf_op jit(solution)/shard_map/ppermute | solution.py:40
  76.5 19.5 %collective-permute-start.14 = (bf16[2,4,3,128,128]{4,3,2,1,0:T(8,128)(2,1)}, bf16[2,4,3,128,128]{4,3,2,1,0:T(8,128)(2,1)}, u32[]{:S(2)}, u32[]{:S(2)}) collective-permute-start(bf16[2,4,3,128,128]{4,3,2,1,0:T(8,128)(2,1)} %get-tuple-element.49), channel_id=1, source_target_pairs={{0,1},{1,0},{2,3},{3,2},{4,5},{5,4},{6,7},{7,6},{8,9},{9,8},{10,11... | collective-permute-start | bytes 2359304 | tf_op jit(solution)/shard_map/ppermute | solution.py:351
  77.4 19.4 %collective-permute-start.15 = (bf16[2,4,3,128,128]{4,3,2,1,0:T(8,128)(2,1)}, bf16[2,4,3,128,128]{4,3,2,1,0:T(8,128)(2,1)}, u32[]{:S(2)}, u32[]{:S(2)}) collective-permute-start(bf16[2,4,3,128,128]{4,3,2,1,0:T(8,128)(2,1)} %get-tuple-element.50), channel_id=1, source_target_pairs={{0,3},{1,2},{2,1},{3,0},{4,7},{5,6},{6,5},{7,4},{8,11},{9,10},{10,... | collective-permute-start | bytes 2359304 | tf_op jit(solution)/shard_map/ppermute | solution.py:351
  99.4 19.8 %collective-permute-start.18 = (bf16[2,4,3,128,128]{4,3,2,1,0:T(8,128)(2,1)}, bf16[2,4,3,128,128]{4,3,2,1,0:T(8,128)(2,1)}, u32[]{:S(2)}, u32[]{:S(2)}) collective-permute-start(bf16[2,4,3,128,128]{4,3,2,1,0:T(8,128)(2,1)} %get-tuple-element.58), channel_id=1, source_target_pairs={{0,1},{1,0},{2,3},{3,2},{4,5},{5,4},{6,7},{7,6},{8,9},{9,8},{10,11... | collective-permute-start | bytes 2359304 | tf_op jit(solution)/shard_map/ppermute | solution.py:351
  112.3 20.7 %collective-permute-start.20 = (bf16[2,4,3,128,128]{4,3,2,1,0:T(8,128)(2,1)}, bf16[2,4,3,128,128]{4,3,2,1,0:T(8,128)(2,1)S(1)}, u32[]{:S(2)}, u32[]{:S(2)}) collective-permute-start(bf16[2,4,3,128,128]{4,3,2,1,0:T(8,128)(2,1)} %get-tuple-element.61), channel_id=1, source_target_pairs={{0,3},{1,2},{2,1},{3,0},{4,7},{5,6},{6,5},{7,4},{8,11},{9,10},{10,... | collective-permute-start | bytes 2359304 | tf_op jit(solution)/shard_map/ppermute | solution.py:351
  114.4 27.1 %collective-permute-start.16 = (bf16[4,3,128,128]{3,2,1,0:T(8,128)(2,1)}, bf16[4,3,128,128]{3,2,1,0:T(8,128)(2,1)}, u32[]{:S(2)}, u32[]{:S(2)}) collective-permute-start(bf16[4,3,128,128]{3,2,1,0:T(8,128)(2,1)} %get-tuple-element.54), channel_id=1, source_target_pairs={{0,3},{1,2},{2,1},{3,0},{4,7},{5,6},{6,5},{7,4},{8,11},{9,10},{10,... | collective-permute-start | bytes 1179656 | tf_op jit(solution)/shard_map/ppermute | solution.py:351
  114.5 27.0 %collective-permute-start.17 = (bf16[4,3,128,128]{3,2,1,0:T(8,128)(2,1)}, bf16[4,3,128,128]{3,2,1,0:T(8,128)(2,1)}, u32[]{:S(2)}, u32[]{:S(2)}) collective-permute-start(bf16[4,3,128,128]{3,2,1,0:T(8,128)(2,1)} %get-tuple-element.55), channel_id=1, source_target_pairs={{0,1},{1,0},{2,3},{3,2},{4,5},{5,4},{6,7},{7,6},{8,9},{9,8},{10,11... | collective-permute-start | bytes 1179656 | tf_op jit(solution)/shard_map/ppermute | solution.py:351
  121.2 28.0 %collective-permute-start.19 = (bf16[4,3,128,128]{3,2,1,0:T(8,128)(2,1)}, bf16[4,3,128,128]{3,2,1,0:T(8,128)(2,1)}, u32[]{:S(2)}, u32[]{:S(2)}) collective-permute-start(bf16[4,3,128,128]{3,2,1,0:T(8,128)(2,1)} %fusion.2), channel_id=1, source_target_pairs={{0,3},{1,2},{2,1},{3,0},{4,7},{5,6},{6,5},{7,4},{8,11},{9,10},{10,... | collective-permute-start | bytes 1179656 | tf_op jit(solution)/shard_map/ppermute | solution.py:351
  133.0 0.9 copy-start
  135.8 13.4 %collective-permute-start.21 = (bf16[4,3,128,128]{3,2,1,0:T(8,128)(2,1)}, bf16[4,3,128,128]{3,2,1,0:T(8,128)(2,1)}, u32[]{:S(2)}, u32[]{:S(2)}) collective-permute-start(bf16[4,3,128,128]{3,2,1,0:T(8,128)(2,1)} %fusion.3), channel_id=1, source_target_pairs={{0,1},{1,0},{2,3},{3,2},{4,5},{5,4},{6,7},{7,6},{8,9},{9,8},{10,11... | collective-permute-start | bytes 1179656 | tf_op jit(solution)/shard_map/ppermute | solution.py:351

commit v2 on v1

--- a/solution.py
+++ b/solution.py
@@ -11,6 +11,7 @@
 
 SPREAD_ROWS = 3
 GROUP = 8
+BATCH = 2
 VMEM_LIMIT = 67_000_000
 
 
@@ -89,14 +90,12 @@
 
 
 class Lists:
-    def __init__(self, slab, slots, per, n_lists, kept):
-        self.slab, self.slots, self.per, self.n_lists = slab, slots, per, n_lists
-        self.pitch = slots * per + GROUP
-        self.counts = [n * slab for n in range(n_lists)]
-        self.kept = n_lists * slab if kept else None
-        base = n_lists * slab + (2 * slab * per if kept else 0)
-        self.lists = [base + n * slab * self.pitch for n in range(n_lists)]
-        self.size = base + n_lists * slab * self.pitch
+    def __init__(self, slab, slots, per, n_products, kept):
+        self.slab, self.slots, self.per = slab, slots, per
+        self.pitch = n_products * slots * per + GROUP
+        self.kept = slab if kept else None
+        self.list = slab + (2 * slab * per if kept else 0)
+        self.size = self.list + slab * self.pitch
 
 
 def plan_kernel(lay, reach, window_rows, products, table, row_slot, *refs):
@@ -138,29 +137,29 @@
         for which in range(n):
             for j in range(slots):
                 inverse[which][outs[which][s, j]] = relative[j // per] + j % per
-        starts = [base + s * lay.pitch for base in lay.lists]
-        ends = list(starts)
+        start = lay.list + s * lay.pitch
+        end = start
         lefts = sorted({product[0] for product in products})
-        for k in range(slots):
-            for left in lefts:
-                offset = (row_slot[cols[left][here + s, k]] - row_start + here + rows) & (rows - 1)
-                place = table[table_base + offset]
-                code = (place << 4) + (k << 13)
-                found = []
-                for number, (which_left, right, out) in enumerate(products):
-                    if which_left != left:
-                        continue
-                    for m in range(per):
-                        target = inverse[out][cols[right][offset, rep * per + m]]
-                        shift = (right if n > 1 else 0) * window_rows * per + m
-                        found.append((number, target, code + (shift << 4) + target))
-                for number, target, entry in found:
-                    meta[ends[number]] = entry
-                    ends[number] += jnp.where(target < slots, 1, 0)
-        for number in range(len(products)):
-            for u in range(GROUP):
-                meta[ends[number] + u] = slots
-            meta[lay.counts[number] + s] = ends[number] - starts[number]
+        for first in range(0, slots, BATCH):
+            found = []
+            for k in range(first, min(first + BATCH, slots)):
+                for left in lefts:
+                    column = cols[left][here + s, k]
+                    offset = (row_slot[column] - row_start + here + rows) & (rows - 1)
+                    code = (table[table_base + offset] << 4) + ((left * slots + k) << 13)
+                    for which_left, right, out in products:
+                        if which_left != left:
+                            continue
+                        base = right * window_rows * per if n > 1 else 0
+                        for m in range(per):
+                            target = inverse[out][cols[right][offset, rep * per + m]]
+                            found.append((target, code + ((base + m) << 4)))
+            for target, entry in found:
+                meta[end] = entry + target
+                end += jnp.where(target < slots, 1, 0)
+        for u in range(GROUP):
+            meta[end + u] = slots
+        meta[s] = end - start
         if lay.kept is not None:
             for which in range(n):
                 for k in range(slots):
@@ -241,104 +240,103 @@
     )(meta, p_blocks, d_blocks)
 
 
-def product_kernel(lay, n_left, sizes, first, halves, meta, *refs):
+def product_kernel(lay, n_left, sizes, meta, *refs):
     left_refs = refs[:n_left]
     pieces = refs[n_left : n_left + n_left * len(sizes)]
-    out_refs, (window, total, sems) = refs[-3 - 2 * len(halves) : -3], refs[-3:]
-    step = pl.program_id(0)
-    row = first + step
-    per = lay.per
-
-    @pl.when(step == 0)
-    def _():
-        copies, base = [], 0
-        for index, piece in enumerate(pieces):
-            size = sizes[index % len(sizes)]
-            copies.append(
-                pltpu.make_async_copy(
-                    piece, window.at[pl.ds(base * per, size * per)], sems.at[index]
-                )
+    outs, stages = refs[-12:-8], refs[-8:-4]
+    left, window, total, sems = refs[-4:]
+    slab, slots, per = lay.slab, lay.slots, lay.per
+    half_rows = slab // 2
+    window_sem, left_sem, out_sem = 0, len(pieces), len(pieces) + slab * n_left
+
+    def left_copy(row, n):
+        return pltpu.make_async_copy(
+            left_refs[n].at[row], left.at[row, pl.ds(n * slots, slots)],
+            sems.at[left_sem + row * n_left + n],
+        )
+
+    copies, base = [], 0
+    for index, piece in enumerate(pieces):
+        size = sizes[index % len(sizes)]
+        copies.append(
+            pltpu.make_async_copy(
+                piece, window.at[pl.ds(base * per, size * per)], sems.at[window_sem + index]
             )
-            base += size
-        for copy in copies:
-            copy.start()
-        for copy in copies:
-            copy.wait()
-
-    total[...] = jnp.zeros_like(total)
-    for n in range(n_left):
-
-        def add_group(group, carry):
-            for u in range(GROUP):
-                code = meta[lay.lists[n] + row * lay.pitch + group * GROUP + u]
-                total[code & 15] += jnp.dot(
-                    left_refs[n][0, code >> 13], window[(code >> 4) & 511],
-                    preferred_element_type=jnp.float32,
-                )
+        )
+        base += size
+    for copy in copies:
+        copy.start()
+    for row in range(slab):
+        for n in range(n_left):
+            left_copy(row, n).start()
+    for copy in copies:
+        copy.wait()
+
+    def out_copy(half, row, which):
+        number = 2 * half + which
+        return pltpu.make_async_copy(
+            stages[number].at[:, row], outs[number].at[:, row],
+            sems.at[out_sem + (half * half_rows + row) * 2 + which],
+        )
+
+    for half in range(2):
+
+        def one_row(local_row, carry):
+            row = half * half_rows + local_row
+            for n in range(n_left):
+                left_copy(row, n).wait()
+            total[...] = jnp.zeros_like(total)
+
+            def add_group(group, inner):
+                for u in range(GROUP):
+                    code = meta[lay.list + row * lay.pitch + group * GROUP + u]
+                    total[code & 15] += jnp.dot(
+                        left[row, code >> 13], window[(code >> 4) & 511],
+                        preferred_element_type=jnp.float32,
+                    )
+                return inner
+
+            lax.fori_loop(0, (meta[row] + GROUP - 1) // GROUP, add_group, 0)
+            for at, q in enumerate(HALF_ORDER[half]):
+                stage = stages[2 * half + (1 if at < 2 else 0)]
+                for j in range(per):
+                    stage[at % 2, local_row, j] = total[q * per + j].astype(stage.dtype)
+            for which in range(2):
+                out_copy(half, local_row, which).start()
             return carry
 
-        groups = (meta[lay.counts[n] + row] + GROUP - 1) // GROUP
-        lax.fori_loop(0, groups, add_group, 0)
-
-    def store(send_ref, keep_ref, order):
-        for at, q in enumerate(order):
-            ref = keep_ref if at < 2 else send_ref
-            for j in range(per):
-                ref[at % 2, 0, j] = total[q * per + j].astype(ref.dtype)
-
-    half_rows = lay.slab // 2
-    for index, half in enumerate(halves):
-        refs_of = out_refs[2 * index], out_refs[2 * index + 1]
-        if len(halves) == 1:
-            store(*refs_of, HALF_ORDER[half])
-        else:
-            pl.when(row // half_rows == half)(
-                functools.partial(store, *refs_of, HALF_ORDER[half])
-            )
+        lax.fori_loop(0, half_rows, one_row, 0)
+    for half in range(2):
+        for row in range(half_rows):
+            for which in range(2):
+                out_copy(half, row, which).wait()
 
 
 HALF_ORDER = ((0, 3, 1, 2), (0, 1, 3, 2))
 
 
-def block_products(lay, lefts, windows, sizes, meta, halves):
+def block_products(lay, lefts, windows, sizes, meta):
     slab, slots, side, _ = lefts[0].shape
     per = lay.per
     pieces = [piece.reshape(-1, side, side) for window in windows for piece in window]
     rows_in = len(windows) * sum(sizes)
     dtype = lefts[0].dtype
-    half_rows = slab // 2
-    first, steps = halves[0] * half_rows, len(halves) * half_rows
     any_spec = pl.BlockSpec(memory_space=pl.ANY)
-    out_specs = []
-    for index in range(len(halves)):
-        spec = pl.BlockSpec(
-            (2, 1, per, side, side),
-            lambda s, *_, low=index * half_rows: (
-                0, jnp.clip(s - low, 0, half_rows - 1), 0, 0, 0,
-            ),
-        )
-        out_specs += [spec, spec]
+    out_shape = (2, slab // 2, per, side, side)
     return pl.pallas_call(
-        functools.partial(product_kernel, lay, len(lefts), sizes, first, halves),
-        grid_spec=pltpu.PrefetchScalarGridSpec(
-            num_scalar_prefetch=1,
-            grid=(steps,),
-            in_specs=[
-                pl.BlockSpec((1, slots, side, side), lambda s, *_: (first + s, 0, 0, 0))
-            ] * len(lefts)
-            + [any_spec] * len(pieces),
-            out_specs=out_specs,
-            scratch_shapes=[
-                pltpu.VMEM((rows_in * per, side, side), dtype),
-                pltpu.VMEM((slots + 1, side, side), jnp.float32),
-                pltpu.SemaphoreType.DMA((len(pieces),)),
-            ],
-        ),
-        out_shape=[jax.ShapeDtypeStruct((2, half_rows, per, side, side), jnp.bfloat16)]
-        * (2 * len(halves)),
-        compiler_params=pltpu.CompilerParams(
-            dimension_semantics=("arbitrary",), vmem_limit_bytes=VMEM_LIMIT
-        ),
+        functools.partial(product_kernel, lay, len(lefts), sizes),
+        in_specs=[pl.BlockSpec(memory_space=pltpu.SMEM)]
+        + [any_spec] * (len(lefts) + len(pieces)),
+        out_specs=[any_spec] * 4,
+        scratch_shapes=[pltpu.VMEM(out_shape, jnp.bfloat16)] * 4
+        + [
+            pltpu.VMEM((slab, len(lefts) * slots, side, side), dtype),
+            pltpu.VMEM((rows_in * per, side, side), dtype),
+            pltpu.VMEM((slots + 1, side, side), jnp.float32),
+            pltpu.SemaphoreType.DMA((len(pieces) + slab * len(lefts) + 2 * slab,)),
+        ],
+        out_shape=[jax.ShapeDtypeStruct(out_shape, jnp.bfloat16)] * 4,
+        compiler_params=pltpu.CompilerParams(vmem_limit_bytes=VMEM_LIMIT),
         cost_estimate=pl.CostEstimate(
             flops=8_000_000_000,
             bytes_accessed=2 * (rows_in * per + 2 * slab * slots) * side * side,
@@ -351,56 +349,62 @@
     return lax.ppermute(value, "rep", [(i, i ^ flip) for i in range(lax.axis_size("rep"))])
 
 
-def finish_kernel(rows, branch_ref, *refs):
-    kept_ref, out_ref = refs[-2:]
-    step = pl.program_id(0)
-    half_steps = pl.num_programs(0) // 2
-
-    def store(keep_ref, first_ref, second_ref):
-        for s in range(rows):
-            squaring = branch_ref[step * rows + s] == 1
-            total = keep_ref[0, s].astype(jnp.float32) + first_ref[0, s].astype(jnp.float32)
-            total = total + second_ref[s].astype(jnp.float32)
-            kept = kept_ref[0, s].astype(jnp.float32)
-            out_ref[s] = jnp.where(squaring, total, 2.0 * kept - total).astype(out_ref.dtype)
-
+def finish_kernel(which, branch_ref, *refs):
+    sources, (kept_ref, out_ref) = refs[:6], refs[6:8]
+    parts, kept, out, sems = refs[8:]
+    half_rows = out.shape[1]
+    loads = []
     for half in range(2):
-        pl.when(step // half_steps == half)(
-            functools.partial(store, *refs[3 * half : 3 * half + 3])
+        for i in range(3):
+            source = sources[3 * half + i]
+            loads.append(
+                pltpu.make_async_copy(
+                    source if i == 2 else source.at[0], parts.at[half, i], sems.at[half, i]
+                )
+            )
+        rows = pl.ds(half * half_rows, half_rows)
+        loads.append(
+            pltpu.make_async_copy(kept_ref.at[which, rows], kept.at[half], sems.at[half, 3])
         )
+    for load in loads:
+        load.start()
+    stores = []
+    for half in range(2):
+        for load in loads[4 * half : 4 * half + 4]:
+            load.wait()
+        for row in range(half_rows):
+            squaring = branch_ref[half * half_rows + row] == 1
+            total = parts[half, 0, row].astype(jnp.float32) + parts[half, 1, row].astype(jnp.float32)
+            total = total + parts[half, 2, row].astype(jnp.float32)
+            twice = 2.0 * kept[half, row].astype(jnp.float32)
+            out[half, row] = jnp.where(squaring, total, twice - total).astype(out.dtype)
+            store = pltpu.make_async_copy(
+                out.at[half, row], out_ref.at[half * half_rows + row],
+                sems.at[half, 4 + row],
+            )
+            store.start()
+            stores.append(store)
+    for store in stores:
+        store.wait()
 
 
 def finish(halves, kept, which, branch):
     _, half_rows, per, side, _ = halves[0][0].shape
-    slab = 2 * half_rows
-    rows = 2
-    half_steps = half_rows // rows
-    in_specs = []
-    for half in range(2):
-
-        def at(s, *_, low=half * half_steps):
-            return jnp.clip(s - low, 0, half_steps - 1)
-
-        pair = pl.BlockSpec(
-            (1, rows, per, side, side), lambda s, *_, at=at: (0, at(s), 0, 0, 0)
-        )
-        single = pl.BlockSpec((rows, per, side, side), lambda s, *_, at=at: (at(s), 0, 0, 0))
-        in_specs += [pair, pair, single]
-    in_specs.append(
-        pl.BlockSpec((1, rows, per, side, side), lambda s, *_: (which, s, 0, 0, 0))
-    )
+    dtype = jnp.bfloat16
+    any_spec = pl.BlockSpec(memory_space=pl.ANY)
+    half = (half_rows, per, side, side)
     return pl.pallas_call(
-        functools.partial(finish_kernel, rows),
-        grid_spec=pltpu.PrefetchScalarGridSpec(
-            num_scalar_prefetch=1,
-            grid=(slab // rows,),
-            in_specs=in_specs,
-            out_specs=pl.BlockSpec((rows, per, side, side), lambda s, *_: (s, 0, 0, 0)),
-        ),
-        out_shape=jax.ShapeDtypeStruct((slab, per, side, side), jnp.bfloat16),
-        compiler_params=pltpu.CompilerParams(
-            dimension_semantics=("arbitrary",), vmem_limit_bytes=VMEM_LIMIT
-        ),
+        functools.partial(finish_kernel, which),
+        in_specs=[pl.BlockSpec(memory_space=pltpu.SMEM)] + [any_spec] * 7,
+        out_specs=any_spec,
+        out_shape=jax.ShapeDtypeStruct((2 * half_rows, per, side, side), dtype),
+        scratch_shapes=[
+            pltpu.VMEM((2, 3) + half, dtype),
+            pltpu.VMEM((2,) + half, dtype),
+            pltpu.VMEM((2,) + half, dtype),
+            pltpu.SemaphoreType.DMA((2, 4 + half_rows)),
+        ],
+        compiler_params=pltpu.CompilerParams(vmem_limit_bytes=VMEM_LIMIT),
         cost_estimate=pl.CostEstimate(flops=2_000_000_000, bytes_accessed=4 << 20, transcendentals=0),
         name="finish",
     )(branch, *halves[0], *halves[1], kept)
@@ -440,36 +444,29 @@
     square_meta = planned(
         square_lay, reach, window_rows, ((0, 0, 0),), table, row_slot, (p_cols,), (out_pcols,)
     )
+    tangent_meta = planned(
+        tangent_lay, reach, window_rows, ((0, 1, 1), (1, 0, 1)), table, row_slot,
+        (p_cols, d_cols), (out_pcols, out_dcols),
+    )
     p_window = inner(p_window)
     d_window = inner(d_window)
-    square = block_products(square_lay, (p_blocks,), (p_window,), sizes, square_meta, (0, 1))
-    square, later_slot = lax.optimization_barrier((square, row_slot))
-    sent_a, keep_a, sent_b, keep_b = square
+    sent_a, keep_a, sent_b, keep_b = block_products(
+        square_lay, (p_blocks,), (p_window,), sizes, square_meta
+    )
     first_a = met(sent_a, 1)
     first_b = met(sent_b, 3)
-
-    tangent_meta = planned(
-        tangent_lay, reach, window_rows, ((0, 1, 1), (1, 0, 1)), table, later_slot,
-        (p_cols, d_cols), (out_pcols, out_dcols),
-    )
-    kept = kept_blocks(tangent_lay, tangent_meta, p_blocks, d_blocks)
-    kept, meta_a = lax.optimization_barrier((kept, tangent_meta))
-    lefts, windows = (p_blocks, d_blocks), (p_window, d_window)
-    tsent_a, tkeep_a = block_products(tangent_lay, lefts, windows, sizes, meta_a, (0,))
-    (tsent_a, tkeep_a), (first_a, first_b) = lax.optimization_barrier(
-        ((tsent_a, tkeep_a), (first_a, first_b))
-    )
-    middle_a, middle_b = pair_sum(keep_a, first_a), pair_sum(keep_b, first_b)
-    middle_a, middle_b, meta_b = lax.optimization_barrier((middle_a, middle_b, meta_a))
-    second_a = met(middle_a, 3)
-    second_b = met(middle_b, 1)
+    keep_a, kept_meta = lax.optimization_barrier((keep_a, tangent_meta))
+    kept = kept_blocks(tangent_lay, kept_meta, p_blocks, d_blocks)
+    kept, tangent_meta = lax.optimization_barrier((kept, tangent_meta))
+    tsent_a, tkeep_a, tsent_b, tkeep_b = block_products(
+        tangent_lay, (p_blocks, d_blocks), (p_window, d_window), sizes, tangent_meta,
+    )
     tfirst_a = met(tsent_a, 1)
-    tsent_b, tkeep_b = block_products(tangent_lay, lefts, windows, sizes, meta_b, (1,))
     tfirst_b = met(tsent_b, 3)
-    tmiddle_a = pair_sum(tkeep_a, tfirst_a)
-    tmiddle_b = pair_sum(tkeep_b, tfirst_b)
-    tsecond_a = met(tmiddle_a, 3)
-    tsecond_b = met(tmiddle_b, 1)
+    second_a = met(pair_sum(keep_a, first_a), 3)
+    second_b = met(pair_sum(keep_b, first_b), 1)
+    tsecond_a = met(pair_sum(tkeep_a, tfirst_a), 3)
+    tsecond_b = met(pair_sum(tkeep_b, tfirst_b), 1)
     next_p = finish(
         ((keep_a, first_a, second_a), (keep_b, first_b, second_b)), kept, 0, branch
     )

time: 156 us -> 133 us (0.85)
  Pallas kernels: 62 us -> 48.6 us
  waiting for transfers between devices: 47.4 us -> 40.3 us
  starting transfers between devices: 34.1 us -> 31.7 us
    pallas_call x5 -> x4, Pallas kernels: 42.9 us -> 29.7 us  [the longest x2 22.7 us: block_products(): pl.pallas_call(functools.partial(product_kernel, lay, len(lefts), sizes),...]
    ppermute x8, waiting for transfers between devices: 22.1 us -> 18.3 us  [met(): lax.ppermute(value, 'rep', [(i, i ^ flip) for i in range(lax.axis_size('r...]
    ppermute x14, waiting for transfers between devices: 25.3 us -> 21.9 us  [swapped(): return lax.ppermute(value, 'rows', pairs)]
    ppermute x14, starting transfers between devices: 20.9 us -> 19.2 us  [swapped(): return lax.ppermute(value, 'rows', pairs)]
    convert_element_type x3 -> x4, other arithmetic: 6.42 us -> 5.54 us  [pair_sum(): (keep[1].astype(jnp.float32) + got[1].astype(jnp.float32)).astype(jnp.bfl...]
    unnamed x6 -> x12, local copies, waits for them, and re-layouts: 3.41 us -> 3.25 us
  transfers between devices with their start and end apart: 22 -> 22, of which waited for: 9 -> 6; matrix products, arithmetic and copies ran while one was open for 4% -> 6% of each run, Pallas kernels for 35% -> 32%
where the time goes in v2:
time: 133 us; the launch traced here: 130 us
  Pallas kernels  48.6 us (37%)
  waiting for transfers between devices  40.3 us (30%)
  starting transfers between devices  31.7 us (24%)
  other arithmetic  5.54 us (4%)
  local copies, waits for them, and re-layouts  3.25 us (2%)
    pallas_call x2, Pallas kernels, block_products(): pl.pallas_call(functools.partial(product_kernel, lay, len(lefts), sizes),...  22.7 us
    ppermute x14, waiting for transfers between devices, swapped(): return lax.ppermute(value, 'rows', pairs)  21.9 us
    ppermute x14, starting transfers between devices, swapped(): return lax.ppermute(value, 'rows', pairs)  19.2 us
    ppermute x8, waiting for transfers between devices, met(): lax.ppermute(value, 'rep', [(i, i ^ flip) for i in range(lax.axis_size('r...  18.3 us
    ppermute x8, starting transfers between devices, met(): lax.ppermute(value, 'rep', [(i, i ^ flip) for i in range(lax.axis_size('r...  12.5 us
    pallas_call x2, Pallas kernels, planned(): pl.pallas_call(functools.partial(plan_kernel, lay, reach, window_rows, pr...  12.2 us
    pallas_call x2, Pallas kernels, finish(): pl.pallas_call(functools.partial(finish_kernel, which), in_specs=[pl.Bloc...  7.02 us
    convert_element_type x4, other arithmetic, pair_sum(): (keep[1].astype(jnp.float32) + got[1].astype(jnp.float32)).astype(jnp.bfl...  5.54 us
  transfers between devices with their start and end apart: 22, of which 6 were waited for; matrix products, arithmetic and copies ran while one was open for 6% of the time, Pallas kernels for 32%

profile of v2, /device:TPU:8, one launch (start us, length us, event | category | flops | bytes accessed | tf_op | source)
XLA Modules:
  0.0 130.4 jit_solution(1379423141458431313)
XLA Ops:
  0.6 3.0 %pack.1 = (bf16[8,3,128,128]{3,2,1,0:T(8,128)(2,1)}, bf16[6,3,128,128]{3,2,1,0:T(8,128)(2,1)}, bf16[2,3,128,128]{3,2,1,0:T(8,128)(2,1)}, bf16[2,3,128,128]{3,2,1...) custom-call(bf16[8,12,128,128]{3,2,1,0:T(8,128)(2,1)} %refs_0_.7, ...), custom_call_target="tpu_custom_call" | custom-call | flops 3000000000 | bytes 4194304 | tf_op jit(solution)/shard_map/pack/pallas_call | solution.py:76
  3.7 7.6 %collective-permute-start.1 = (bf16[8,3,128,128]{3,2,1,0:T(8,128)(2,1)}, bf16[8,3,128,128]{3,2,1,0:T(8,128)(2,1)}, u32[]{:S(2)}, u32[]{:S(2)}) collective-permute-start(bf16[8,3,128,128]{3,2,1,0:T(8,128)(2,1)} %get-tuple-element.22), channel_id=1, source_target_pairs={{0,252},{4,8},{8,4},{12,16},{16,12},{20,24},{24,20},{28,32},{32,28... | collective-permute-start | bytes 2359304 | tf_op jit(solution)/shard_map/ppermute | solution.py:41
  11.2 0.0 collective-permute-start.3
  11.2 2.3 %collective-permute-start.4 = (bf16[2,3,128,128]{3,2,1,0:T(8,128)(2,1)}, bf16[2,3,128,128]{3,2,1,0:T(8,128)(2,1)}, u32[]{:S(2)}, u32[]{:S(2)}) collective-permute-start(bf16[2,3,128,128]{3,2,1,0:T(8,128)(2,1)} %get-tuple-element.25), channel_id=1, source_target_pairs={{0,244},{4,16},{8,252},{12,24},{16,4},{20,32},{24,12},{28,40},{32,... | collective-permute-start | bytes 589832 | tf_op jit(solution)/shard_map/ppermute | solution.py:41
  13.5 3.2 %collective-permute-start.12 = (bf16[8,3,128,128]{3,2,1,0:T(8,128)(2,1)}, bf16[8,3,128,128]{3,2,1,0:T(8,128)(2,1)}, u32[]{:S(2)}, u32[]{:S(2)}) collective-permute-start(bf16[8,3,128,128]{3,2,1,0:T(8,128)(2,1)} %get-tuple-element.34), channel_id=1, source_target_pairs={{0,252},{4,8},{8,4},{12,16},{16,12},{20,24},{24,20},{28,32},{32,28... | collective-permute-start | bytes 2359304 | tf_op jit(solution)/shard_map/ppermute | solution.py:41
  16.7 10.8 %collective-permute-done.1 = bf16[8,3,128,128]{3,2,1,0:T(8,128)(2,1)} collective-permute-done((bf16[8,3,128,128]{3,2,1,0:T(8,128)(2,1)}, bf16[8,3,128,128]{3,2,1,0:T(8,128)(2,1)}, u32[]{:S(2)}, u32[]{:S(2)}) %collective-permute-start.1) | collective-permute-done | bytes 786464 | tf_op jit(solution)/shard_map/ppermute | solution.py:41
  27.6 0.9 copy.11.refs_0_
  28.4 1.6 %copy.13.refs_1_ = s32[512,12]{1,0:T(8,128)} copy(s32[512,12]{0,1:T(8,128)} %param.12) | data formatting | bytes 49152 | tf_op args[3]
  30.1 0.1 collective-permute-start.14
  30.1 4.5 %plan.2.meta = s32[360]{0:T(512)} custom-call(s32[112]{0:T(128)} %constant.2.clone.table, s32[512]{0:T(512)} %row_slot.3, s32[512,12]{1,0:T(8,128)} %copy.11.refs_0_, s32[8,12]{1,0:T(8,128)} %refs_2_.1), custom_call_target="tpu_custom_call" | custom-call | flops 4000000000 | bytes 65536 | tf_op jit(solution)/shard_map/plan/pallas_call | solution.py:185
  34.6 11.1 %collective-permute-done.14 = bf16[2,3,128,128]{3,2,1,0:T(8,128)(2,1)} collective-permute-done((bf16[2,3,128,128]{3,2,1,0:T(8,128)(2,1)}, bf16[2,3,128,128]{3,2,1,0:T(8,128)(2,1)}, u32[]{:S(2)}, u32[]{:S(2)}) %collective-permute-start.14) | collective-permute-done | bytes 196640 | tf_op jit(solution)/shard_map/ppermute | solution.py:41
  45.7 0.0 collective-permute-start.6
  45.7 7.7 %plan.3.meta = s32[696]{0:T(1024)} custom-call(s32[112]{0:T(128)} %constant.2.clone.table, s32[512]{0:T(512)} %row_slot.3, s32[512,12]{1,0:T(8,128)} %copy.11.refs_0_, s32[512,12]{1,0:T(8,128)} %copy.13.refs_1_, s32[8,12]{1,0:T(8,128)} %refs_2_.1, s32[8,12]{1,0:T(8,128)} %refs_3_.1), custom_call_target="tpu_custom_call" | custom-call | flops 4000000000 | bytes 65536 | tf_op jit(solution)/shard_map/plan/pallas_call | solution.py:185
  53.5 0.0 collective-permute-done.6
  53.5 0.6 collective-permute-start.11
  54.0 0.0 collective-permute-done.2
  54.0 0.0 collective-permute-start.13
  54.0 0.0 collective-permute-done
  54.0 1.6 %collective-permute-start.15 = (bf16[2,3,128,128]{3,2,1,0:T(8,128)(2,1)}, bf16[2,3,128,128]{3,2,1,0:T(8,128)(2,1)}, u32[]{:S(2)}, u32[]{:S(2)}) collective-permute-start(bf16[2,3,128,128]{3,2,1,0:T(8,128)(2,1)} %get-tuple-element.37), channel_id=1, source_target_pairs={{0,244},{4,16},{8,252},{12,24},{16,4},{20,32},{24,12},{28,40},{32,... | collective-permute-start | bytes 589832 | tf_op jit(solution)/shard_map/ppermute | solution.py:41
  55.6 0.0 collective-permute-done.12
  55.6 3.8 %collective-permute-start.17 = (bf16[2,3,128,128]{3,2,1,0:T(8,128)(2,1)}, bf16[2,3,128,128]{3,2,1,0:T(8,128)(2,1)}, u32[]{:S(2)}, u32[]{:S(2)}) collective-permute-start(bf16[2,3,128,128]{3,2,1,0:T(8,128)(2,1)} %collective-permute-done.14), channel_id=1, source_target_pairs={{0,4},{4,0},{8,12},{12,8},{16,20},{20,16},{24,28},{28,24},{32,36},... | collective-permute-start | bytes 589832 | tf_op jit(solution)/shard_map/ppermute | solution.py:41
  59.4 0.0 collective-permute-done.5
  59.4 0.1 collective-permute-start.16
  59.5 9.3 %shard_map.104 = (bf16[2,4,3,128,128]{4,3,2,1,0:T(8,128)(2,1)}, bf16[2,4,3,128,128]{4,3,2,1,0:T(8,128)(2,1)}, bf16[2,4,3,128,128]{4,3,2,1,0:T(8,128)(2,1)}, bf16[2,4,3,128,128]{4,3,2,1,0:T(8,128)(2,1)}) custom-call(s32[360]{0:T(512)} %plan.2.meta, bf16[8,12,128,128]{3,2,1,0:T(8,128)(2,1)} %refs_0_.7, bf16[24,128,128]{2,1,0:T(8,128)(2,1)} %bitcast.24, ...), custom_call_target="tpu_custom_call" | custom-call | flops 8000000000 | bytes 10616832 | tf_op jit(solution)/shard_map/pallas_call | solution.py:326
  68.8 3.7 %kept.1.refs_6_ = bf16[2,8,3,128,128]{4,3,2,1,0:T(8,128)(2,1)} custom-call(s32[696]{0:T(1024)} %plan.3.meta, bf16[8,12,128,128]{3,2,1,0:T(8,128)(2,1)} %refs_0_.7, bf16[8,12,128,128]{3,2,1,0:T(8,128)(2,1)} %refs_1_.6), custom_call_target="tpu_custom_call" | custom-call | flops 3000000000 | bytes 2097152 | tf_op jit(solution)/shard_map/kept/pallas_call | solution.py:227
  72.5 0.0 collective-permute-done.15
  72.5 1.1 collective-permute-start.7
  73.7 0.0 collective-permute-done.17
  73.7 1.2 collective-permute-start.9
  74.8 0.0 collective-permute-done.13
  74.8 13.4 %shard_map.105 = (bf16[2,4,3,128,128]{4,3,2,1,0:T(8,128)(2,1)}, bf16[2,4,3,128,128]{4,3,2,1,0:T(8,128)(2,1)}, bf16[2,4,3,128,128]{4,3,2,1,0:T(8,128)(2,1)}, bf16[2,4,3,128,128]{4,3,2,1,0:T(8,128)(2,1)}) custom-call(s32[696]{0:T(1024)} %plan.3.meta, bf16[8,12,128,128]{3,2,1,0:T(8,128)(2,1)} %refs_0_.7, bf16[8,12,128,128]{3,2,1,0:T(8,128)(2,1)} %refs_1_.6, ...), custom_call_target="tpu_custom_call" | custom-call | flops 8000000000 | bytes 14942208 | tf_op jit(solution)/shard_map/pallas_call | solution.py:326
  88.3 1.7 %collective-permute-start.18 = (bf16[2,4,3,128,128]{4,3,2,1,0:T(8,128)(2,1)}, bf16[2,4,3,128,128]{4,3,2,1,0:T(8,128)(2,1)S(1)}, u32[]{:S(2)}, u32[]{:S(2)}) collective-permute-start(bf16[2,4,3,128,128]{4,3,2,1,0:T(8,128)(2,1)} %get-tuple-element.39), channel_id=1, source_target_pairs={{0,1},{1,0},{2,3},{3,2},{4,5},{5,4},{6,7},{7,6},{8,9},{9,8},{10,11... | collective-permute-start | bytes 2359304 | tf_op jit(solution)/shard_map/ppermute | solution.py:349
  89.9 2.0 %collective-permute-start.20 = (bf16[2,4,3,128,128]{4,3,2,1,0:T(8,128)(2,1)}, bf16[2,4,3,128,128]{4,3,2,1,0:T(8,128)(2,1)S(1)}, u32[]{:S(2)}, u32[]{:S(2)}) collective-permute-start(bf16[2,4,3,128,128]{4,3,2,1,0:T(8,128)(2,1)} %get-tuple-element.41), channel_id=1, source_target_pairs={{0,3},{1,2},{2,1},{3,0},{4,7},{5,6},{6,5},{7,4},{8,11},{9,10},{10,... | collective-permute-start | bytes 2359304 | tf_op jit(solution)/shard_map/ppermute | solution.py:349
  92.0 1.2 collective-permute-done.7.refs_1_
  93.1 1.2 fusion
  94.4 0.9 collective-permute-start.8
  95.2 1.2 fusion.1
  96.5 2.3 %collective-permute-start.10 = (bf16[4,3,128,128]{3,2,1,0:T(8,128)(2,1)S(1)}, bf16[4,3,128,128]{3,2,1,0:T(8,128)(2,1)}, u32[]{:S(2)}, u32[]{:S(2)}) collective-permute-start(bf16[4,3,128,128]{3,2,1,0:T(8,128)(2,1)S(1)} %fusion.1), channel_id=1, source_target_pairs={{0,1},{1,0},{2,3},{3,2},{4,5},{5,4},{6,7},{7,6},{8,9},{9,8},{10,11... | collective-permute-start | bytes 1179656 | tf_op jit(solution)/shard_map/ppermute | solution.py:349
  98.8 11.1 %collective-permute-done.18.refs_1_ = bf16[2,4,3,128,128]{4,3,2,1,0:T(8,128)(2,1)S(1)} collective-permute-done((bf16[2,4,3,128,128]{4,3,2,1,0:T(8,128)(2,1)}, bf16[2,4,3,128,128]{4,3,2,1,0:T(8,128)(2,1)S(1)}, u32[]{:S(2)}, u32[]{:S(2)}) %collective-permute-start.18) | collective-permute-done | bytes 786464 | tf_op jit(solution)/shard_map/ppermute | solution.py:349
  109.9 2.1 %fusion.2 = bf16[4,3,128,128]{3,2,1,0:T(8,128)(2,1)} fusion(bf16[2,4,3,128,128]{4,3,2,1,0:T(8,128)(2,1)S(1)} %collective-permute-done.18.refs_1_, bf16[2,4,3,128,128]{4,3,2,1,0:T(8,128)(2,1)} %get-tuple-element.38.refs_0_), kind=kLoop, calls=%fused_computation.6 | loop fusion | flops 786432 | bytes 1179648 | tf_op jit(solution)/shard_map/convert_element_type | solution.py:414
  112.0 0.8 collective-permute-start.19
  112.8 1.0 fusion.3
  113.8 2.6 %collective-permute-start.21 = (bf16[4,3,128,128]{3,2,1,0:T(8,128)(2,1)}, bf16[4,3,128,128]{3,2,1,0:T(8,128)(2,1)}, u32[]{:S(2)}, u32[]{:S(2)}) collective-permute-start(bf16[4,3,128,128]{3,2,1,0:T(8,128)(2,1)} %fusion.3), channel_id=1, source_target_pairs={{0,1},{1,0},{2,3},{3,2},{4,5},{5,4},{6,7},{7,6},{8,9},{9,8},{10,11... | collective-permute-start | bytes 1179656 | tf_op jit(solution)/shard_map/ppermute | solution.py:349
  116.3 2.7 %collective-permute-done.8.refs_2_ = bf16[4,3,128,128]{3,2,1,0:T(8,128)(2,1)S(1)} collective-permute-done((bf16[4,3,128,128]{3,2,1,0:T(8,128)(2,1)S(1)}, bf16[4,3,128,128]{3,2,1,0:T(8,128)(2,1)S(1)}, u32[]{:S(2)}, u32[]{:S(2)}) %collective-permute-start.8) | collective-permute-done | bytes 393248 | tf_op jit(solution)/shard_map/ppermute | solution.py:349
  119.0 0.7 copy-done.4
  119.8 3.5 %finish.2 = bf16[8,3,128,128]{3,2,1,0:T(8,128)(2,1)} custom-call(s32[8]{0:T(128)} %branch_ref.3, bf16[2,4,3,128,128]{4,3,2,1,0:T(8,128)(2,1)} %get-tuple-element.27.refs_0_, bf16[2,4,3,128,128]{4,3,2,1,0:T(8,128)(2,1)} %collective-permute-done.7.refs_1_, bf16[4,3,128,128]{3,2,1,0:T(8,128)(2,1)} %copy-done.4, ...), custom_call_target="tpu_custom_call" | custom-call | flops 2000000000 | bytes 4194304 | tf_op jit(solution)/shard_map/finish/pallas_call | solution.py:396
  123.3 3.4 %collective-permute-done.19.refs_2_ = bf16[4,3,128,128]{3,2,1,0:T(8,128)(2,1)} collective-permute-done((bf16[4,3,128,128]{3,2,1,0:T(8,128)(2,1)}, bf16[4,3,128,128]{3,2,1,0:T(8,128)(2,1)}, u32[]{:S(2)}, u32[]{:S(2)}) %collective-permute-start.19) | collective-permute-done | bytes 393248 | tf_op jit(solution)/shard_map/ppermute | solution.py:349
  126.7 3.5 %finish.3 = bf16[8,3,128,128]{3,2,1,0:T(8,128)(2,1)} custom-call(s32[8]{0:T(128)} %branch_ref.3, bf16[2,4,3,128,128]{4,3,2,1,0:T(8,128)(2,1)} %get-tuple-element.38.refs_0_, bf16[2,4,3,128,128]{4,3,2,1,0:T(8,128)(2,1)} %copy-done.1, bf16[4,3,128,128]{3,2,1,0:T(8,128)(2,1)} %collective-permute-done.19.refs_2_, ...), custom_call_target="tpu_custom_call" | custom-call | flops 2000000000 | bytes 4194304 | tf_op jit(solution)/shard_map/finish/pallas_call | solution.py:396
  (20 shorter events, 0.0 us)
Async XLA Ops:
  0.6 26.9 %copy-start.3 = (s32[512,12]{0,1:T(8,128)S(1)}, s32[512,12]{0,1:T(8,128)}, u32[]{:S(2)}) copy-start(s32[512,12]{0,1:T(8,128)} %param.11) | copy-start | bytes 73732
  3.7 23.9 %collective-permute-start.1 = (bf16[8,3,128,128]{3,2,1,0:T(8,128)(2,1)}, bf16[8,3,128,128]{3,2,1,0:T(8,128)(2,1)}, u32[]{:S(2)}, u32[]{:S(2)}) collective-permute-start(bf16[8,3,128,128]{3,2,1,0:T(8,128)(2,1)} %get-tuple-element.22), channel_id=1, source_target_pairs={{0,252},{4,8},{8,4},{12,16},{16,12},{20,24},{24,20},{28,32},{32,28... | collective-permute-start | bytes 2359304 | tf_op jit(solution)/shard_map/ppermute | solution.py:41
  11.2 18.8 %collective-permute-start.3 = (bf16[2,3,128,128]{3,2,1,0:T(8,128)(2,1)}, bf16[2,3,128,128]{3,2,1,0:T(8,128)(2,1)}, u32[]{:S(2)}, u32[]{:S(2)}) collective-permute-start(bf16[2,3,128,128]{3,2,1,0:T(8,128)(2,1)} %get-tuple-element.24), channel_id=1, source_target_pairs={{0,8},{4,252},{8,16},{12,4},{16,24},{20,12},{24,32},{28,20},{32,40... | collective-permute-start | bytes 589832 | tf_op jit(solution)/shard_map/ppermute | solution.py:41
  11.2 18.8 %collective-permute-start.4 = (bf16[2,3,128,128]{3,2,1,0:T(8,128)(2,1)}, bf16[2,3,128,128]{3,2,1,0:T(8,128)(2,1)}, u32[]{:S(2)}, u32[]{:S(2)}) collective-permute-start(bf16[2,3,128,128]{3,2,1,0:T(8,128)(2,1)} %get-tuple-element.25), channel_id=1, source_target_pairs={{0,244},{4,16},{8,252},{12,24},{16,4},{20,32},{24,12},{28,40},{32,... | collective-permute-start | bytes 589832 | tf_op jit(solution)/shard_map/ppermute | solution.py:41
  13.5 40.5 %collective-permute-start = (bf16[8,3,128,128]{3,2,1,0:T(8,128)(2,1)}, bf16[8,3,128,128]{3,2,1,0:T(8,128)(2,1)}, u32[]{:S(2)}, u32[]{:S(2)}) collective-permute-start(bf16[8,3,128,128]{3,2,1,0:T(8,128)(2,1)} %get-tuple-element.22), channel_id=1, source_target_pairs={{0,4},{4,0},{8,12},{12,8},{16,20},{20,16},{24,28},{28,24},{32,36},... | collective-permute-start | bytes 2359304 | tf_op jit(solution)/shard_map/ppermute | solution.py:41
  13.5 42.1 %collective-permute-start.12 = (bf16[8,3,128,128]{3,2,1,0:T(8,128)(2,1)}, bf16[8,3,128,128]{3,2,1,0:T(8,128)(2,1)}, u32[]{:S(2)}, u32[]{:S(2)}) collective-permute-start(bf16[8,3,128,128]{3,2,1,0:T(8,128)(2,1)} %get-tuple-element.34), channel_id=1, source_target_pairs={{0,252},{4,8},{8,4},{12,16},{16,12},{20,24},{24,20},{28,32},{32,28... | collective-permute-start | bytes 2359304 | tf_op jit(solution)/shard_map/ppermute | solution.py:41
  27.6 31.9 %collective-permute-start.5 = (bf16[8,3,128,128]{3,2,1,0:T(8,128)(2,1)}, bf16[8,3,128,128]{3,2,1,0:T(8,128)(2,1)}, u32[]{:S(2)}, u32[]{:S(2)}) collective-permute-start(bf16[8,3,128,128]{3,2,1,0:T(8,128)(2,1)} %collective-permute-done.1), channel_id=1, source_target_pairs={{0,4},{4,0},{8,12},{12,8},{16,20},{20,16},{24,28},{28,24},{32,36},... | collective-permute-start | bytes 2359304 | tf_op jit(solution)/shard_map/ppermute | solution.py:41
  30.0 24.0 %collective-permute-start.2 = (bf16[6,3,128,128]{3,2,1,0:T(8,128)(2,1)}, bf16[6,3,128,128]{3,2,1,0:T(8,128)(2,1)}, u32[]{:S(2)}, u32[]{:S(2)}) collective-permute-start(bf16[6,3,128,128]{3,2,1,0:T(8,128)(2,1)} %get-tuple-element.23), channel_id=1, source_target_pairs={{0,8},{4,252},{8,16},{12,4},{16,24},{20,12},{24,32},{28,20},{32,40... | collective-permute-start | bytes 1769480 | tf_op jit(solution)/shard_map/ppermute | solution.py:41
  30.1 15.6 %collective-permute-start.14 = (bf16[2,3,128,128]{3,2,1,0:T(8,128)(2,1)}, bf16[2,3,128,128]{3,2,1,0:T(8,128)(2,1)}, u32[]{:S(2)}, u32[]{:S(2)}) collective-permute-start(bf16[2,3,128,128]{3,2,1,0:T(8,128)(2,1)} %get-tuple-element.36), channel_id=1, source_target_pairs={{0,8},{4,252},{8,16},{12,4},{16,24},{20,12},{24,32},{28,20},{32,40... | collective-permute-start | bytes 589832 | tf_op jit(solution)/shard_map/ppermute | solution.py:41
  45.7 7.8 %collective-permute-start.6 = (bf16[2,3,128,128]{3,2,1,0:T(8,128)(2,1)}, bf16[2,3,128,128]{3,2,1,0:T(8,128)(2,1)}, u32[]{:S(2)}, u32[]{:S(2)}) collective-permute-start(bf16[2,3,128,128]{3,2,1,0:T(8,128)(2,1)} %collective-permute-done.3), channel_id=1, source_target_pairs={{0,4},{4,0},{8,12},{12,8},{16,20},{20,16},{24,28},{28,24},{32,36},... | collective-permute-start | bytes 589832 | tf_op jit(solution)/shard_map/ppermute | solution.py:41
  53.5 21.3 %collective-permute-start.11 = (bf16[8,3,128,128]{3,2,1,0:T(8,128)(2,1)}, bf16[8,3,128,128]{3,2,1,0:T(8,128)(2,1)}, u32[]{:S(2)}, u32[]{:S(2)}) collective-permute-start(bf16[8,3,128,128]{3,2,1,0:T(8,128)(2,1)} %get-tuple-element.34), channel_id=1, source_target_pairs={{0,4},{4,0},{8,12},{12,8},{16,20},{20,16},{24,28},{28,24},{32,36},... | collective-permute-start | bytes 2359304 | tf_op jit(solution)/shard_map/ppermute | solution.py:41
  54.0 20.8 %collective-permute-start.13 = (bf16[6,3,128,128]{3,2,1,0:T(8,128)(2,1)}, bf16[6,3,128,128]{3,2,1,0:T(8,128)(2,1)}, u32[]{:S(2)}, u32[]{:S(2)}) collective-permute-start(bf16[6,3,128,128]{3,2,1,0:T(8,128)(2,1)} %get-tuple-element.35), channel_id=1, source_target_pairs={{0,8},{4,252},{8,16},{12,4},{16,24},{20,12},{24,32},{28,20},{32,40... | collective-permute-start | bytes 1769480 | tf_op jit(solution)/shard_map/ppermute | solution.py:41
  54.0 18.5 %collective-permute-start.15 = (bf16[2,3,128,128]{3,2,1,0:T(8,128)(2,1)}, bf16[2,3,128,128]{3,2,1,0:T(8,128)(2,1)}, u32[]{:S(2)}, u32[]{:S(2)}) collective-permute-start(bf16[2,3,128,128]{3,2,1,0:T(8,128)(2,1)} %get-tuple-element.37), channel_id=1, source_target_pairs={{0,244},{4,16},{8,252},{12,24},{16,4},{20,32},{24,12},{28,40},{32,... | collective-permute-start | bytes 589832 | tf_op jit(solution)/shard_map/ppermute | solution.py:41
  55.6 18.1 %collective-permute-start.17 = (bf16[2,3,128,128]{3,2,1,0:T(8,128)(2,1)}, bf16[2,3,128,128]{3,2,1,0:T(8,128)(2,1)}, u32[]{:S(2)}, u32[]{:S(2)}) collective-permute-start(bf16[2,3,128,128]{3,2,1,0:T(8,128)(2,1)} %collective-permute-done.14), channel_id=1, source_target_pairs={{0,4},{4,0},{8,12},{12,8},{16,20},{20,16},{24,28},{28,24},{32,36},... | collective-permute-start | bytes 589832 | tf_op jit(solution)/shard_map/ppermute | solution.py:41
  59.4 15.4 %collective-permute-start.16 = (bf16[8,3,128,128]{3,2,1,0:T(8,128)(2,1)}, bf16[8,3,128,128]{3,2,1,0:T(8,128)(2,1)}, u32[]{:S(2)}, u32[]{:S(2)}) collective-permute-start(bf16[8,3,128,128]{3,2,1,0:T(8,128)(2,1)} %collective-permute-done.12), channel_id=1, source_target_pairs={{0,4},{4,0},{8,12},{12,8},{16,20},{20,16},{24,28},{28,24},{32,36},... | collective-permute-start | bytes 2359304 | tf_op jit(solution)/shard_map/ppermute | solution.py:41
  72.5 20.6 %collective-permute-start.7 = (bf16[2,4,3,128,128]{4,3,2,1,0:T(8,128)(2,1)}, bf16[2,4,3,128,128]{4,3,2,1,0:T(8,128)(2,1)}, u32[]{:S(2)}, u32[]{:S(2)}) collective-permute-start(bf16[2,4,3,128,128]{4,3,2,1,0:T(8,128)(2,1)} %get-tuple-element.28), channel_id=1, source_target_pairs={{0,1},{1,0},{2,3},{3,2},{4,5},{5,4},{6,7},{7,6},{8,9},{9,8},{10,11... | collective-permute-start | bytes 2359304 | tf_op jit(solution)/shard_map/ppermute | solution.py:349
  73.7 21.6 %collective-permute-start.9 = (bf16[2,4,3,128,128]{4,3,2,1,0:T(8,128)(2,1)}, bf16[2,4,3,128,128]{4,3,2,1,0:T(8,128)(2,1)}, u32[]{:S(2)}, u32[]{:S(2)}) collective-permute-start(bf16[2,4,3,128,128]{4,3,2,1,0:T(8,128)(2,1)} %get-tuple-element.30), channel_id=1, source_target_pairs={{0,3},{1,2},{2,1},{3,0},{4,7},{5,6},{6,5},{7,4},{8,11},{9,10},{10,... | collective-permute-start | bytes 2359304 | tf_op jit(solution)/shard_map/ppermute | solution.py:349
  88.3 24.5 %copy-start = (bf16[2,4,3,128,128]{4,3,2,1,0:T(8,128)(2,1)S(1)}, bf16[2,4,3,128,128]{4,3,2,1,0:T(8,128)(2,1)}, u32[]{:S(2)}) copy-start(bf16[2,4,3,128,128]{4,3,2,1,0:T(8,128)(2,1)} %get-tuple-element.40.refs_3_) | copy-start | bytes 2359300
  88.3 21.6 %collective-permute-start.18 = (bf16[2,4,3,128,128]{4,3,2,1,0:T(8,128)(2,1)}, bf16[2,4,3,128,128]{4,3,2,1,0:T(8,128)(2,1)S(1)}, u32[]{:S(2)}, u32[]{:S(2)}) collective-permute-start(bf16[2,4,3,128,128]{4,3,2,1,0:T(8,128)(2,1)} %get-tuple-element.39), channel_id=1, source_target_pairs={{0,1},{1,0},{2,3},{3,2},{4,5},{5,4},{6,7},{7,6},{8,9},{9,8},{10,11... | collective-permute-start | bytes 2359304 | tf_op jit(solution)/shard_map/ppermute | solution.py:349
  89.9 22.8 %collective-permute-start.20 = (bf16[2,4,3,128,128]{4,3,2,1,0:T(8,128)(2,1)}, bf16[2,4,3,128,128]{4,3,2,1,0:T(8,128)(2,1)S(1)}, u32[]{:S(2)}, u32[]{:S(2)}) collective-permute-start(bf16[2,4,3,128,128]{4,3,2,1,0:T(8,128)(2,1)} %get-tuple-element.41), channel_id=1, source_target_pairs={{0,3},{1,2},{2,1},{3,0},{4,7},{5,6},{6,5},{7,4},{8,11},{9,10},{10,... | collective-permute-start | bytes 2359304 | tf_op jit(solution)/shard_map/ppermute | solution.py:349
  94.4 24.6 %collective-permute-start.8 = (bf16[4,3,128,128]{3,2,1,0:T(8,128)(2,1)S(1)}, bf16[4,3,128,128]{3,2,1,0:T(8,128)(2,1)S(1)}, u32[]{:S(2)}, u32[]{:S(2)}) collective-permute-start(bf16[4,3,128,128]{3,2,1,0:T(8,128)(2,1)S(1)} %fusion), channel_id=1, source_target_pairs={{0,3},{1,2},{2,1},{3,0},{4,7},{5,6},{6,5},{7,4},{8,11},{9,10},{10,... | collective-permute-start | bytes 1179656 | tf_op jit(solution)/shard_map/ppermute | solution.py:349
  96.5 23.3 %collective-permute-start.10 = (bf16[4,3,128,128]{3,2,1,0:T(8,128)(2,1)S(1)}, bf16[4,3,128,128]{3,2,1,0:T(8,128)(2,1)}, u32[]{:S(2)}, u32[]{:S(2)}) collective-permute-start(bf16[4,3,128,128]{3,2,1,0:T(8,128)(2,1)S(1)} %fusion.1), channel_id=1, source_target_pairs={{0,1},{1,0},{2,3},{3,2},{4,5},{5,4},{6,7},{7,6},{8,9},{9,8},{10,11... | collective-permute-start | bytes 1179656 | tf_op jit(solution)/shard_map/ppermute | solution.py:349
  109.9 9.1 %copy-start.1 = (bf16[2,4,3,128,128]{4,3,2,1,0:T(8,128)(2,1)}, bf16[2,4,3,128,128]{4,3,2,1,0:T(8,128)(2,1)S(1)}, u32[]{:S(2)}) copy-start(bf16[2,4,3,128,128]{4,3,2,1,0:T(8,128)(2,1)S(1)} %collective-permute-done.18.refs_1_) | copy-start | bytes 2359300
  112.0 14.7 %collective-permute-start.19 = (bf16[4,3,128,128]{3,2,1,0:T(8,128)(2,1)}, bf16[4,3,128,128]{3,2,1,0:T(8,128)(2,1)}, u32[]{:S(2)}, u32[]{:S(2)}) collective-permute-start(bf16[4,3,128,128]{3,2,1,0:T(8,128)(2,1)} %fusion.2), channel_id=1, source_target_pairs={{0,3},{1,2},{2,1},{3,0},{4,7},{5,6},{6,5},{7,4},{8,11},{9,10},{10,... | collective-permute-start | bytes 1179656 | tf_op jit(solution)/shard_map/ppermute | solution.py:349
  112.8 6.2 %copy-start.2 = (bf16[2,4,3,128,128]{4,3,2,1,0:T(8,128)(2,1)}, bf16[2,4,3,128,128]{4,3,2,1,0:T(8,128)(2,1)S(1)}, u32[]{:S(2)}) copy-start(bf16[2,4,3,128,128]{4,3,2,1,0:T(8,128)(2,1)S(1)} %collective-permute-done.20.refs_4_) | copy-start | bytes 2359300
  113.8 12.9 %collective-permute-start.21 = (bf16[4,3,128,128]{3,2,1,0:T(8,128)(2,1)}, bf16[4,3,128,128]{3,2,1,0:T(8,128)(2,1)}, u32[]{:S(2)}, u32[]{:S(2)}) collective-permute-start(bf16[4,3,128,128]{3,2,1,0:T(8,128)(2,1)} %fusion.3), channel_id=1, source_target_pairs={{0,1},{1,0},{2,3},{3,2},{4,5},{5,4},{6,7},{7,6},{8,9},{9,8},{10,11... | collective-permute-start | bytes 1179656 | tf_op jit(solution)/shard_map/ppermute | solution.py:349
  119.0 0.7 copy-start.4

commit v3 on v2

--- a/solution.py
+++ b/solution.py
@@ -98,42 +98,23 @@
         self.size = self.list + slab * self.pitch
 
 
-def plan_kernel(lay, reach, window_rows, products, table, row_slot, *refs):
-    n = 1 + max(max(product) for product in products)
-    cols_hbm, outs = refs[:n], refs[n : 2 * n]
-    meta = refs[2 * n]
-    cols, inverse, (slot_of, sems) = refs[2 * n + 1 : 3 * n + 1], refs[3 * n + 1 : 4 * n + 1], refs[-2:]
+def plan_kernel(lay, reach, window_rows, products, n, table, row_slot, *refs):
+    cols, outs, meta = refs[:n], refs[n : 2 * n], refs[2 * n]
+    inverse, slot_of = refs[2 * n + 1 : 3 * n + 1], refs[-1]
     slab, slots, per = lay.slab, lay.slots, lay.per
     rows = row_slot.shape[0]
     index, rep = lax.axis_index("rows"), lax.axis_index("rep")
     row_start = index * slab
-    slabs = rows // slab
-    width = 2 * reach + 1
-    table_base = (index % 2) * (width * slab)
-
-    copies = []
-    for which in range(n):
-        for near in range(width):
-            at = (index + near + slabs - reach) & (slabs - 1)
-            copies.append(
-                pltpu.make_async_copy(
-                    cols_hbm[which].at[pl.ds(at * slab, slab)],
-                    cols[which].at[pl.ds(near * slab, slab)],
-                    sems.at[which * width + near],
-                )
-            )
-    for copy in copies:
-        copy.start()
+    here = reach * slab
+    table_base = (index % 2) * (2 * here + slab)
     span = 2 * slots + SPREAD_ROWS
     for column in range(-span, slab + span):
         for inv in inverse + ((slot_of,) if lay.kept is not None else ()):
             inv[(row_start + column + rows) & (rows - 1)] = slots
-    for copy in copies:
-        copy.wait()
     relative = [(q ^ rep) * per for q in range(slots // per)]
-    here = reach * slab
 
     def row(s, carry):
+        own = row_start + s
         for which in range(n):
             for j in range(slots):
                 inverse[which][outs[which][s, j]] = relative[j // per] + j % per
@@ -144,15 +125,15 @@
             found = []
             for k in range(first, min(first + BATCH, slots)):
                 for left in lefts:
-                    column = cols[left][here + s, k]
-                    offset = (row_slot[column] - row_start + here + rows) & (rows - 1)
+                    stored = row_slot[cols[left][k, own]]
+                    offset = (stored - row_start + here + rows) & (rows - 1)
                     code = (table[table_base + offset] << 4) + ((left * slots + k) << 13)
                     for which_left, right, out in products:
                         if which_left != left:
                             continue
                         base = right * window_rows * per if n > 1 else 0
                         for m in range(per):
-                            target = inverse[out][cols[right][offset, rep * per + m]]
+                            target = inverse[out][cols[right][rep * per + m, stored]]
                             found.append((target, code + ((base + m) << 4)))
             for target, entry in found:
                 meta[end] = entry + target
@@ -163,12 +144,12 @@
         if lay.kept is not None:
             for which in range(n):
                 for k in range(slots):
-                    slot_of[cols[which][here + s, k]] = k
+                    slot_of[cols[which][k, own]] = k
                 for j in range(per):
                     at = lay.kept + (which * slab + s) * per + j
                     meta[at] = slot_of[outs[which][s, rep * per + j]]
                 for k in range(slots):
-                    slot_of[cols[which][here + s, k]] = slots
+                    slot_of[cols[which][k, own]] = slots
         for which in range(n):
             for j in range(slots):
                 inverse[which][outs[which][s, j]] = slots
@@ -178,22 +159,19 @@
 
 
 def planned(lay, reach, window_rows, products, table, row_slot, cols, outs):
-    rows, slots = cols[0].shape
     n = len(cols)
-    smem, any_spec = pl.BlockSpec(memory_space=pltpu.SMEM), pl.BlockSpec(memory_space=pl.ANY)
-    width = 2 * reach + 1
+    rows = row_slot.shape[0]
+    smem = pl.BlockSpec(memory_space=pltpu.SMEM)
     return pl.pallas_call(
-        functools.partial(plan_kernel, lay, reach, window_rows, products),
-        in_specs=[smem, smem] + [any_spec] * n + [smem] * n,
+        functools.partial(plan_kernel, lay, reach, window_rows, products, n),
+        in_specs=[smem] * (2 + 2 * n),
         out_specs=smem,
         out_shape=jax.ShapeDtypeStruct((lay.size,), jnp.int32),
-        scratch_shapes=[pltpu.SMEM((width * lay.slab, slots), jnp.int32)] * n
-        + [pltpu.SMEM((rows,), jnp.int32)] * (n + 1)
-        + [pltpu.SemaphoreType.DMA((n * width,))],
+        scratch_shapes=[pltpu.SMEM((rows,), jnp.int32)] * (n + 1),
         compiler_params=pltpu.CompilerParams(vmem_limit_bytes=VMEM_LIMIT),
         cost_estimate=pl.CostEstimate(flops=4_000_000_000, bytes_accessed=65536, transcendentals=0),
         name="plan",
-    )(jnp.asarray(table), row_slot, *cols, *outs)
+    )(jnp.asarray(table), row_slot, *(ids.T for ids in cols), *outs)
 
 
 def kept_kernel(lay, meta, p_ref, d_ref, out_ref, held, sems, out_sem):
@@ -444,10 +422,6 @@
     square_meta = planned(
         square_lay, reach, window_rows, ((0, 0, 0),), table, row_slot, (p_cols,), (out_pcols,)
     )
-    tangent_meta = planned(
-        tangent_lay, reach, window_rows, ((0, 1, 1), (1, 0, 1)), table, row_slot,
-        (p_cols, d_cols), (out_pcols, out_dcols),
-    )
     p_window = inner(p_window)
     d_window = inner(d_window)
     sent_a, keep_a, sent_b, keep_b = block_products(
@@ -455,12 +429,16 @@
     )
     first_a = met(sent_a, 1)
     first_b = met(sent_b, 3)
-    keep_a, kept_meta = lax.optimization_barrier((keep_a, tangent_meta))
-    kept = kept_blocks(tangent_lay, kept_meta, p_blocks, d_blocks)
-    kept, tangent_meta = lax.optimization_barrier((kept, tangent_meta))
+    keep_a, later_slot = lax.optimization_barrier((keep_a, row_slot))
+    tangent_meta = planned(
+        tangent_lay, reach, window_rows, ((0, 1, 1), (1, 0, 1)), table, later_slot,
+        (p_cols, d_cols), (out_pcols, out_dcols),
+    )
     tsent_a, tkeep_a, tsent_b, tkeep_b = block_products(
         tangent_lay, (p_blocks, d_blocks), (p_window, d_window), sizes, tangent_meta,
     )
+    tkeep_a, kept_meta = lax.optimization_barrier((tkeep_a, tangent_meta))
+    kept = kept_blocks(tangent_lay, kept_meta, p_blocks, d_blocks)
     tfirst_a = met(tsent_a, 1)
     tfirst_b = met(tsent_b, 3)
     second_a = met(pair_sum(keep_a, first_a), 3)

time: 133 us -> 147 us (1.11)
  waiting for transfers between devices: 40.3 us -> 54.5 us
  local copies, waits for them, and re-layouts: 3.25 us -> 0.03 us
  other arithmetic: 5.54 us -> 7.36 us
  starting transfers between devices: 31.7 us -> 33.4 us
    ppermute x8, waiting for transfers between devices: 18.3 us -> 26.7 us  [met(): lax.ppermute(value, 'rep', [(i, i ^ flip) for i in range(lax.axis_size('r...]
    ppermute x14, waiting for transfers between devices: 21.9 us -> 27.8 us  [swapped(): return lax.ppermute(value, 'rows', pairs)]
    unnamed x12 -> x10, local copies, waits for them, and re-layouts: 3.25 us -> 0.03 us
    convert_element_type x4, other arithmetic: 5.54 us -> 7.36 us  [pair_sum(): (keep[1].astype(jnp.float32) + got[1].astype(jnp.float32)).astype(jnp.bfl...]
    ppermute x14, starting transfers between devices: 19.2 us -> 20.7 us  [swapped(): return lax.ppermute(value, 'rows', pairs)]
  transfers between devices with their start and end apart: 22 -> 22, of which waited for: 6 -> 6; matrix products, arithmetic and copies ran while one was open for 6% -> 5% of each run, Pallas kernels for 32% -> 20%
where the time goes in v3:
time: 147 us; the launch traced here: 144 us
  waiting for transfers between devices  54.5 us (37%)
  Pallas kernels  48.2 us (33%)
  starting transfers between devices  33.4 us (23%)
  other arithmetic  7.36 us (5%)
    ppermute x14, waiting for transfers between devices, swapped(): return lax.ppermute(value, 'rows', pairs)  27.8 us
    ppermute x8, waiting for transfers between devices, met(): lax.ppermute(value, 'rep', [(i, i ^ flip) for i in range(lax.axis_size('r...  26.7 us
    pallas_call x2, Pallas kernels, block_products(): pl.pallas_call(functools.partial(product_kernel, lay, len(lefts), sizes),...  22.7 us
    ppermute x14, starting transfers between devices, swapped(): return lax.ppermute(value, 'rows', pairs)  20.7 us
    ppermute x8, starting transfers between devices, met(): lax.ppermute(value, 'rep', [(i, i ^ flip) for i in range(lax.axis_size('r...  12.7 us
    pallas_call x2, Pallas kernels, planned(): pl.pallas_call(functools.partial(plan_kernel, lay, reach, window_rows, pr...  11.8 us
    convert_element_type x4, other arithmetic, pair_sum(): (keep[1].astype(jnp.float32) + got[1].astype(jnp.float32)).astype(jnp.bfl...  7.36 us
    pallas_call x2, Pallas kernels, finish(): pl.pallas_call(functools.partial(finish_kernel, which), in_specs=[pl.Bloc...  7.03 us
  transfers between devices with their start and end apart: 22, of which 6 were waited for; matrix products, arithmetic and copies ran while one was open for 5% of the time, Pallas kernels for 20%

profile of v3, /device:TPU:8, one launch (start us, length us, event | category | flops | bytes accessed | tf_op | source)
XLA Modules:
  0.0 144.5 jit_solution(13561012573105209358)
XLA Ops:
  0.6 3.0 %pack.1 = (bf16[8,3,128,128]{3,2,1,0:T(8,128)(2,1)}, bf16[6,3,128,128]{3,2,1,0:T(8,128)(2,1)}, bf16[2,3,128,128]{3,2,1,0:T(8,128)(2,1)}, bf16[2,3,128,128]{3,2,1...) custom-call(bf16[8,12,128,128]{3,2,1,0:T(8,128)(2,1)} %p_ref.1, ...), custom_call_target="tpu_custom_call" | custom-call | flops 3000000000 | bytes 4194304 | tf_op jit(solution)/shard_map/pack/pallas_call | solution.py:76
  3.6 7.6 %collective-permute-start.1 = (bf16[8,3,128,128]{3,2,1,0:T(8,128)(2,1)}, bf16[8,3,128,128]{3,2,1,0:T(8,128)(2,1)}, u32[]{:S(2)}, u32[]{:S(2)}) collective-permute-start(bf16[8,3,128,128]{3,2,1,0:T(8,128)(2,1)} %get-tuple-element.22), channel_id=1, source_target_pairs={{0,252},{4,8},{8,4},{12,16},{16,12},{20,24},{24,20},{28,32},{32,28... | collective-permute-start | bytes 2359304 | tf_op jit(solution)/shard_map/ppermute | solution.py:41
  11.2 0.2 collective-permute-start
  11.4 5.3 %collective-permute-start.12 = (bf16[8,3,128,128]{3,2,1,0:T(8,128)(2,1)}, bf16[8,3,128,128]{3,2,1,0:T(8,128)(2,1)}, u32[]{:S(2)}, u32[]{:S(2)}) collective-permute-start(bf16[8,3,128,128]{3,2,1,0:T(8,128)(2,1)} %get-tuple-element.32), channel_id=1, source_target_pairs={{0,252},{4,8},{8,4},{12,16},{16,12},{20,24},{24,20},{28,32},{32,28... | collective-permute-start | bytes 2359304 | tf_op jit(solution)/shard_map/ppermute | solution.py:41
  16.7 6.6 %collective-permute-done.1 = bf16[8,3,128,128]{3,2,1,0:T(8,128)(2,1)} collective-permute-done((bf16[8,3,128,128]{3,2,1,0:T(8,128)(2,1)}, bf16[8,3,128,128]{3,2,1,0:T(8,128)(2,1)}, u32[]{:S(2)}, u32[]{:S(2)}) %collective-permute-start.1) | collective-permute-done | bytes 786464 | tf_op jit(solution)/shard_map/ppermute | solution.py:41
  23.3 2.7 %collective-permute-start.4 = (bf16[2,3,128,128]{3,2,1,0:T(8,128)(2,1)}, bf16[2,3,128,128]{3,2,1,0:T(8,128)(2,1)}, u32[]{:S(2)}, u32[]{:S(2)}) collective-permute-start(bf16[2,3,128,128]{3,2,1,0:T(8,128)(2,1)} %get-tuple-element.25), channel_id=1, source_target_pairs={{0,244},{4,16},{8,252},{12,24},{16,4},{20,32},{24,12},{28,40},{32,... | collective-permute-start | bytes 589832 | tf_op jit(solution)/shard_map/ppermute | solution.py:41
  26.0 2.8 %collective-permute-start.2 = (bf16[6,3,128,128]{3,2,1,0:T(8,128)(2,1)}, bf16[6,3,128,128]{3,2,1,0:T(8,128)(2,1)}, u32[]{:S(2)}, u32[]{:S(2)}) collective-permute-start(bf16[6,3,128,128]{3,2,1,0:T(8,128)(2,1)} %get-tuple-element.23), channel_id=1, source_target_pairs={{0,8},{4,252},{8,16},{12,4},{16,24},{20,12},{24,32},{28,20},{32,40... | collective-permute-start | bytes 1769480 | tf_op jit(solution)/shard_map/ppermute | solution.py:41
  28.8 11.8 %collective-permute-done.4 = bf16[2,3,128,128]{3,2,1,0:T(8,128)(2,1)} collective-permute-done((bf16[2,3,128,128]{3,2,1,0:T(8,128)(2,1)}, bf16[2,3,128,128]{3,2,1,0:T(8,128)(2,1)}, u32[]{:S(2)}, u32[]{:S(2)}) %collective-permute-start.4) | collective-permute-done | bytes 196640 | tf_op jit(solution)/shard_map/ppermute | solution.py:41
  40.6 0.0 collective-permute-start.14
  40.6 9.3 %collective-permute-done.14 = bf16[2,3,128,128]{3,2,1,0:T(8,128)(2,1)} collective-permute-done((bf16[2,3,128,128]{3,2,1,0:T(8,128)(2,1)}, bf16[2,3,128,128]{3,2,1,0:T(8,128)(2,1)}, u32[]{:S(2)}, u32[]{:S(2)}) %collective-permute-start.14) | collective-permute-done | bytes 196640 | tf_op jit(solution)/shard_map/ppermute | solution.py:41
  49.9 0.0 collective-permute-start.6
  49.9 4.2 %plan.2.meta = s32[360]{0:T(512)} custom-call(s32[112]{0:T(128)} %constant.2.clone.table, s32[512]{0:T(512)} %row_slot.2, s32[12,512]{1,0:T(8,128)} %bitcast.29, s32[8,12]{1,0:T(8,128)} %refs_2_.1), custom_call_target="tpu_custom_call" | custom-call | flops 4000000000 | bytes 65536 | tf_op jit(solution)/shard_map/plan/pallas_call | solution.py:165
  54.1 0.0 collective-permute-done.6
  54.1 0.6 collective-permute-start.11
  54.7 1.1 collective-permute-start.15
  55.7 0.0 collective-permute-done
  55.7 0.0 collective-permute-start.13
  55.7 0.2 collective-permute-start.17
  56.0 0.0 collective-permute-done.5
  56.0 0.4 collective-permute-start.16
  56.4 9.2 %shard_map.104 = (bf16[2,4,3,128,128]{4,3,2,1,0:T(8,128)(2,1)}, bf16[2,4,3,128,128]{4,3,2,1,0:T(8,128)(2,1)}, bf16[2,4,3,128,128]{4,3,2,1,0:T(8,128)(2,1)}, bf16[2,4,3,128,128]{4,3,2,1,0:T(8,128)(2,1)}) custom-call(s32[360]{0:T(512)} %plan.2.meta, bf16[8,12,128,128]{3,2,1,0:T(8,128)(2,1)} %p_ref.1, bf16[24,128,128]{2,1,0:T(8,128)(2,1)} %bitcast.26, ...), custom_call_target="tpu_custom_call" | custom-call | flops 8000000000 | bytes 10616832 | tf_op jit(solution)/shard_map/pallas_call | solution.py:304
  65.6 7.6 %plan.3.meta = s32[696]{0:T(1024)} custom-call(s32[112]{0:T(128)} %constant.2.clone.table, s32[512]{0:T(512)} %row_slot.2, s32[12,512]{1,0:T(8,128)} %bitcast.30, s32[12,512]{1,0:T(8,128)} %bitcast.31, s32[8,12]{1,0:T(8,128)} %refs_2_.1, s32[8,12]{1,0:T(8,128)} %refs_3_.1), custom_call_target="tpu_custom_call" | custom-call | flops 4000000000 | bytes 65536 | tf_op jit(solution)/shard_map/plan/pallas_call | solution.py:165
  73.2 0.0 collective-permute-done.17
  73.2 0.0 collective-permute-done.13
  73.3 13.4 %shard_map.105 = (bf16[2,4,3,128,128]{4,3,2,1,0:T(8,128)(2,1)}, bf16[2,4,3,128,128]{4,3,2,1,0:T(8,128)(2,1)}, bf16[2,4,3,128,128]{4,3,2,1,0:T(8,128)(2,1)}, bf16[2,4,3,128,128]{4,3,2,1,0:T(8,128)(2,1)}) custom-call(s32[696]{0:T(1024)} %plan.3.meta, bf16[8,12,128,128]{3,2,1,0:T(8,128)(2,1)} %p_ref.1, bf16[8,12,128,128]{3,2,1,0:T(8,128)(2,1)} %d_ref.1, ...), custom_call_target="tpu_custom_call" | custom-call | flops 8000000000 | bytes 14942208 | tf_op jit(solution)/shard_map/pallas_call | solution.py:304
  86.7 1.5 %collective-permute-start.18 = (bf16[2,4,3,128,128]{4,3,2,1,0:T(8,128)(2,1)}, bf16[2,4,3,128,128]{4,3,2,1,0:T(8,128)(2,1)S(1)}, u32[]{:S(2)}, u32[]{:S(2)}) collective-permute-start(bf16[2,4,3,128,128]{4,3,2,1,0:T(8,128)(2,1)} %get-tuple-element.39), channel_id=1, source_target_pairs={{0,1},{1,0},{2,3},{3,2},{4,5},{5,4},{6,7},{7,6},{8,9},{9,8},{10,11... | collective-permute-start | bytes 2359304 | tf_op jit(solution)/shard_map/ppermute | solution.py:327
  88.2 1.9 %collective-permute-start.20 = (bf16[2,4,3,128,128]{4,3,2,1,0:T(8,128)(2,1)}, bf16[2,4,3,128,128]{4,3,2,1,0:T(8,128)(2,1)S(1)}, u32[]{:S(2)}, u32[]{:S(2)}) collective-permute-start(bf16[2,4,3,128,128]{4,3,2,1,0:T(8,128)(2,1)} %get-tuple-element.41), channel_id=1, source_target_pairs={{0,3},{1,2},{2,1},{3,0},{4,7},{5,6},{6,5},{7,4},{8,11},{9,10},{10,... | collective-permute-start | bytes 2359304 | tf_op jit(solution)/shard_map/ppermute | solution.py:327
  90.1 0.9 collective-permute-start.7
  91.0 0.4 collective-permute-start.9
  91.5 16.0 %collective-permute-done.18.refs_1_ = bf16[2,4,3,128,128]{4,3,2,1,0:T(8,128)(2,1)S(1)} collective-permute-done((bf16[2,4,3,128,128]{4,3,2,1,0:T(8,128)(2,1)}, bf16[2,4,3,128,128]{4,3,2,1,0:T(8,128)(2,1)S(1)}, u32[]{:S(2)}, u32[]{:S(2)}) %collective-permute-start.18) | collective-permute-done | bytes 786464 | tf_op jit(solution)/shard_map/ppermute | solution.py:327
  107.4 2.1 %fusion.2 = bf16[4,3,128,128]{3,2,1,0:T(8,128)(2,1)} fusion(bf16[2,4,3,128,128]{4,3,2,1,0:T(8,128)(2,1)S(1)} %collective-permute-done.18.refs_1_, bf16[2,4,3,128,128]{4,3,2,1,0:T(8,128)(2,1)} %get-tuple-element.38.refs_0_), kind=kLoop, calls=%fused_computation.6 | loop fusion | flops 786432 | bytes 1179648 | tf_op jit(solution)/shard_map/convert_element_type | solution.py:392
  109.5 1.3 collective-permute-start.19
  110.9 0.0 collective-permute-done.20.refs_4_
  110.9 2.1 %fusion.3 = bf16[4,3,128,128]{3,2,1,0:T(8,128)(2,1)} fusion(bf16[2,4,3,128,128]{4,3,2,1,0:T(8,128)(2,1)S(1)} %collective-permute-done.20.refs_4_, bf16[2,4,3,128,128]{4,3,2,1,0:T(8,128)(2,1)} %get-tuple-element.40.refs_3_), kind=kLoop, calls=%fused_computation.7 | loop fusion | flops 786432 | bytes 1179648 | tf_op jit(solution)/shard_map/convert_element_type | solution.py:392
  113.0 2.6 %collective-permute-start.21 = (bf16[4,3,128,128]{3,2,1,0:T(8,128)(2,1)}, bf16[4,3,128,128]{3,2,1,0:T(8,128)(2,1)}, u32[]{:S(2)}, u32[]{:S(2)}) collective-permute-start(bf16[4,3,128,128]{3,2,1,0:T(8,128)(2,1)} %fusion.3), channel_id=1, source_target_pairs={{0,1},{1,0},{2,3},{3,2},{4,5},{5,4},{6,7},{7,6},{8,9},{9,8},{10,11... | collective-permute-start | bytes 1179656 | tf_op jit(solution)/shard_map/ppermute | solution.py:327
  115.6 8.7 %collective-permute-done.7.refs_1_ = bf16[2,4,3,128,128]{4,3,2,1,0:T(8,128)(2,1)S(1)} collective-permute-done((bf16[2,4,3,128,128]{4,3,2,1,0:T(8,128)(2,1)}, bf16[2,4,3,128,128]{4,3,2,1,0:T(8,128)(2,1)S(1)}, u32[]{:S(2)}, u32[]{:S(2)}) %collective-permute-start.7) | collective-permute-done | bytes 786464 | tf_op jit(solution)/shard_map/ppermute | solution.py:327
  124.3 2.1 %fusion = bf16[4,3,128,128]{3,2,1,0:T(8,128)(2,1)} fusion(bf16[2,4,3,128,128]{4,3,2,1,0:T(8,128)(2,1)S(1)} %collective-permute-done.7.refs_1_, bf16[2,4,3,128,128]{4,3,2,1,0:T(8,128)(2,1)} %get-tuple-element.27.refs_0_), kind=kLoop, calls=%fused_computation.4 | loop fusion | flops 786432 | bytes 1179648 | tf_op jit(solution)/shard_map/convert_element_type | solution.py:392
  126.4 1.3 collective-permute-start.8
  127.7 0.0 collective-permute-done.9.refs_4_
  127.7 1.0 fusion.1
  128.8 0.0 copy-done.2
  128.8 2.7 %collective-permute-start.10 = (bf16[4,3,128,128]{3,2,1,0:T(8,128)(2,1)}, bf16[4,3,128,128]{3,2,1,0:T(8,128)(2,1)}, u32[]{:S(2)}, u32[]{:S(2)}) collective-permute-start(bf16[4,3,128,128]{3,2,1,0:T(8,128)(2,1)} %fusion.1), channel_id=1, source_target_pairs={{0,1},{1,0},{2,3},{3,2},{4,5},{5,4},{6,7},{7,6},{8,9},{9,8},{10,11... | collective-permute-start | bytes 1179656 | tf_op jit(solution)/shard_map/ppermute | solution.py:327
  131.5 3.7 %kept.1.refs_6_ = bf16[2,8,3,128,128]{4,3,2,1,0:T(8,128)(2,1)} custom-call(s32[696]{0:T(1024)} %plan.3.meta, bf16[8,12,128,128]{3,2,1,0:T(8,128)(2,1)} %p_ref.1, bf16[8,12,128,128]{3,2,1,0:T(8,128)(2,1)} %d_ref.1), custom_call_target="tpu_custom_call" | custom-call | flops 3000000000 | bytes 2097152 | tf_op jit(solution)/shard_map/kept/pallas_call | solution.py:205
  135.2 0.0 collective-permute-done.19.refs_2_
  135.2 0.0 collective-permute-done.21.refs_5_
  135.2 3.5 %finish.3 = bf16[8,3,128,128]{3,2,1,0:T(8,128)(2,1)} custom-call(s32[8]{0:T(128)} %branch_ref.3, bf16[2,4,3,128,128]{4,3,2,1,0:T(8,128)(2,1)} %get-tuple-element.38.refs_0_, bf16[2,4,3,128,128]{4,3,2,1,0:T(8,128)(2,1)} %copy-done.3, bf16[4,3,128,128]{3,2,1,0:T(8,128)(2,1)} %collective-permute-done.19.refs_2_, ...), custom_call_target="tpu_custom_call" | custom-call | flops 2000000000 | bytes 4194304 | tf_op jit(solution)/shard_map/finish/pallas_call | solution.py:374
  138.7 2.0 %collective-permute-done.8.refs_2_ = bf16[4,3,128,128]{3,2,1,0:T(8,128)(2,1)} collective-permute-done((bf16[4,3,128,128]{3,2,1,0:T(8,128)(2,1)}, bf16[4,3,128,128]{3,2,1,0:T(8,128)(2,1)}, u32[]{:S(2)}, u32[]{:S(2)}) %collective-permute-start.8) | collective-permute-done | bytes 393248 | tf_op jit(solution)/shard_map/ppermute | solution.py:327
  140.8 3.5 %finish.2 = bf16[8,3,128,128]{3,2,1,0:T(8,128)(2,1)} custom-call(s32[8]{0:T(128)} %branch_ref.3, bf16[2,4,3,128,128]{4,3,2,1,0:T(8,128)(2,1)} %get-tuple-element.27.refs_0_, bf16[2,4,3,128,128]{4,3,2,1,0:T(8,128)(2,1)} %copy-done.1, bf16[4,3,128,128]{3,2,1,0:T(8,128)(2,1)} %collective-permute-done.8.refs_2_, ...), custom_call_target="tpu_custom_call" | custom-call | flops 2000000000 | bytes 4194304 | tf_op jit(solution)/shard_map/finish/pallas_call | solution.py:374
  (18 shorter events, 0.0 us)
Async XLA Ops:
  3.6 19.7 %collective-permute-start.1 = (bf16[8,3,128,128]{3,2,1,0:T(8,128)(2,1)}, bf16[8,3,128,128]{3,2,1,0:T(8,128)(2,1)}, u32[]{:S(2)}, u32[]{:S(2)}) collective-permute-start(bf16[8,3,128,128]{3,2,1,0:T(8,128)(2,1)} %get-tuple-element.22), channel_id=1, source_target_pairs={{0,252},{4,8},{8,4},{12,16},{16,12},{20,24},{24,20},{28,32},{32,28... | collective-permute-start | bytes 2359304 | tf_op jit(solution)/shard_map/ppermute | solution.py:41
  11.2 14.8 %collective-permute-start.3 = (bf16[2,3,128,128]{3,2,1,0:T(8,128)(2,1)}, bf16[2,3,128,128]{3,2,1,0:T(8,128)(2,1)}, u32[]{:S(2)}, u32[]{:S(2)}) collective-permute-start(bf16[2,3,128,128]{3,2,1,0:T(8,128)(2,1)} %get-tuple-element.24), channel_id=1, source_target_pairs={{0,8},{4,252},{8,16},{12,4},{16,24},{20,12},{24,32},{28,20},{32,40... | collective-permute-start | bytes 589832 | tf_op jit(solution)/shard_map/ppermute | solution.py:41
  11.2 44.5 %collective-permute-start = (bf16[8,3,128,128]{3,2,1,0:T(8,128)(2,1)}, bf16[8,3,128,128]{3,2,1,0:T(8,128)(2,1)}, u32[]{:S(2)}, u32[]{:S(2)}) collective-permute-start(bf16[8,3,128,128]{3,2,1,0:T(8,128)(2,1)} %get-tuple-element.22), channel_id=1, source_target_pairs={{0,4},{4,0},{8,12},{12,8},{16,20},{20,16},{24,28},{28,24},{32,36},... | collective-permute-start | bytes 2359304 | tf_op jit(solution)/shard_map/ppermute | solution.py:41
  11.4 44.3 %collective-permute-start.12 = (bf16[8,3,128,128]{3,2,1,0:T(8,128)(2,1)}, bf16[8,3,128,128]{3,2,1,0:T(8,128)(2,1)}, u32[]{:S(2)}, u32[]{:S(2)}) collective-permute-start(bf16[8,3,128,128]{3,2,1,0:T(8,128)(2,1)} %get-tuple-element.32), channel_id=1, source_target_pairs={{0,252},{4,8},{8,4},{12,16},{16,12},{20,24},{24,20},{28,32},{32,28... | collective-permute-start | bytes 2359304 | tf_op jit(solution)/shard_map/ppermute | solution.py:41
  23.3 32.7 %collective-permute-start.5 = (bf16[8,3,128,128]{3,2,1,0:T(8,128)(2,1)}, bf16[8,3,128,128]{3,2,1,0:T(8,128)(2,1)}, u32[]{:S(2)}, u32[]{:S(2)}) collective-permute-start(bf16[8,3,128,128]{3,2,1,0:T(8,128)(2,1)} %collective-permute-done.1), channel_id=1, source_target_pairs={{0,4},{4,0},{8,12},{12,8},{16,20},{20,16},{24,28},{28,24},{32,36},... | collective-permute-start | bytes 2359304 | tf_op jit(solution)/shard_map/ppermute | solution.py:41
  23.3 17.3 %collective-permute-start.4 = (bf16[2,3,128,128]{3,2,1,0:T(8,128)(2,1)}, bf16[2,3,128,128]{3,2,1,0:T(8,128)(2,1)}, u32[]{:S(2)}, u32[]{:S(2)}) collective-permute-start(bf16[2,3,128,128]{3,2,1,0:T(8,128)(2,1)} %get-tuple-element.25), channel_id=1, source_target_pairs={{0,244},{4,16},{8,252},{12,24},{16,4},{20,32},{24,12},{28,40},{32,... | collective-permute-start | bytes 589832 | tf_op jit(solution)/shard_map/ppermute | solution.py:41
  26.0 28.7 %collective-permute-start.2 = (bf16[6,3,128,128]{3,2,1,0:T(8,128)(2,1)}, bf16[6,3,128,128]{3,2,1,0:T(8,128)(2,1)}, u32[]{:S(2)}, u32[]{:S(2)}) collective-permute-start(bf16[6,3,128,128]{3,2,1,0:T(8,128)(2,1)} %get-tuple-element.23), channel_id=1, source_target_pairs={{0,8},{4,252},{8,16},{12,4},{16,24},{20,12},{24,32},{28,20},{32,40... | collective-permute-start | bytes 1769480 | tf_op jit(solution)/shard_map/ppermute | solution.py:41
  40.6 9.3 %collective-permute-start.14 = (bf16[2,3,128,128]{3,2,1,0:T(8,128)(2,1)}, bf16[2,3,128,128]{3,2,1,0:T(8,128)(2,1)}, u32[]{:S(2)}, u32[]{:S(2)}) collective-permute-start(bf16[2,3,128,128]{3,2,1,0:T(8,128)(2,1)} %get-tuple-element.34), channel_id=1, source_target_pairs={{0,8},{4,252},{8,16},{12,4},{16,24},{20,12},{24,32},{28,20},{32,40... | collective-permute-start | bytes 589832 | tf_op jit(solution)/shard_map/ppermute | solution.py:41
  49.9 4.2 %collective-permute-start.6 = (bf16[2,3,128,128]{3,2,1,0:T(8,128)(2,1)}, bf16[2,3,128,128]{3,2,1,0:T(8,128)(2,1)}, u32[]{:S(2)}, u32[]{:S(2)}) collective-permute-start(bf16[2,3,128,128]{3,2,1,0:T(8,128)(2,1)} %collective-permute-done.3), channel_id=1, source_target_pairs={{0,4},{4,0},{8,12},{12,8},{16,20},{20,16},{24,28},{28,24},{32,36},... | collective-permute-start | bytes 589832 | tf_op jit(solution)/shard_map/ppermute | solution.py:41
  54.1 19.2 %collective-permute-start.11 = (bf16[8,3,128,128]{3,2,1,0:T(8,128)(2,1)}, bf16[8,3,128,128]{3,2,1,0:T(8,128)(2,1)}, u32[]{:S(2)}, u32[]{:S(2)}) collective-permute-start(bf16[8,3,128,128]{3,2,1,0:T(8,128)(2,1)} %get-tuple-element.32), channel_id=1, source_target_pairs={{0,4},{4,0},{8,12},{12,8},{16,20},{20,16},{24,28},{28,24},{32,36},... | collective-permute-start | bytes 2359304 | tf_op jit(solution)/shard_map/ppermute | solution.py:41
  54.7 18.5 %collective-permute-start.15 = (bf16[2,3,128,128]{3,2,1,0:T(8,128)(2,1)}, bf16[2,3,128,128]{3,2,1,0:T(8,128)(2,1)}, u32[]{:S(2)}, u32[]{:S(2)}) collective-permute-start(bf16[2,3,128,128]{3,2,1,0:T(8,128)(2,1)} %get-tuple-element.35), channel_id=1, source_target_pairs={{0,244},{4,16},{8,252},{12,24},{16,4},{20,32},{24,12},{28,40},{32,... | collective-permute-start | bytes 589832 | tf_op jit(solution)/shard_map/ppermute | solution.py:41
  55.7 17.5 %collective-permute-start.13 = (bf16[6,3,128,128]{3,2,1,0:T(8,128)(2,1)}, bf16[6,3,128,128]{3,2,1,0:T(8,128)(2,1)}, u32[]{:S(2)}, u32[]{:S(2)}) collective-permute-start(bf16[6,3,128,128]{3,2,1,0:T(8,128)(2,1)} %get-tuple-element.33), channel_id=1, source_target_pairs={{0,8},{4,252},{8,16},{12,4},{16,24},{20,12},{24,32},{28,20},{32,40... | collective-permute-start | bytes 1769480 | tf_op jit(solution)/shard_map/ppermute | solution.py:41
  55.7 17.5 %collective-permute-start.17 = (bf16[2,3,128,128]{3,2,1,0:T(8,128)(2,1)}, bf16[2,3,128,128]{3,2,1,0:T(8,128)(2,1)}, u32[]{:S(2)}, u32[]{:S(2)}) collective-permute-start(bf16[2,3,128,128]{3,2,1,0:T(8,128)(2,1)} %collective-permute-done.14), channel_id=1, source_target_pairs={{0,4},{4,0},{8,12},{12,8},{16,20},{20,16},{24,28},{28,24},{32,36},... | collective-permute-start | bytes 589832 | tf_op jit(solution)/shard_map/ppermute | solution.py:41
  56.0 17.3 %collective-permute-start.16 = (bf16[8,3,128,128]{3,2,1,0:T(8,128)(2,1)}, bf16[8,3,128,128]{3,2,1,0:T(8,128)(2,1)}, u32[]{:S(2)}, u32[]{:S(2)}) collective-permute-start(bf16[8,3,128,128]{3,2,1,0:T(8,128)(2,1)} %collective-permute-done.12), channel_id=1, source_target_pairs={{0,4},{4,0},{8,12},{12,8},{16,20},{20,16},{24,28},{28,24},{32,36},... | collective-permute-start | bytes 2359304 | tf_op jit(solution)/shard_map/ppermute | solution.py:41
  86.7 41.0 %copy-start = (bf16[2,4,3,128,128]{4,3,2,1,0:T(8,128)(2,1)S(1)}, bf16[2,4,3,128,128]{4,3,2,1,0:T(8,128)(2,1)}, u32[]{:S(2)}) copy-start(bf16[2,4,3,128,128]{4,3,2,1,0:T(8,128)(2,1)} %get-tuple-element.29.refs_3_) | copy-start | bytes 2359300
  86.7 20.7 %collective-permute-start.18 = (bf16[2,4,3,128,128]{4,3,2,1,0:T(8,128)(2,1)}, bf16[2,4,3,128,128]{4,3,2,1,0:T(8,128)(2,1)S(1)}, u32[]{:S(2)}, u32[]{:S(2)}) collective-permute-start(bf16[2,4,3,128,128]{4,3,2,1,0:T(8,128)(2,1)} %get-tuple-element.39), channel_id=1, source_target_pairs={{0,1},{1,0},{2,3},{3,2},{4,5},{5,4},{6,7},{7,6},{8,9},{9,8},{10,11... | collective-permute-start | bytes 2359304 | tf_op jit(solution)/shard_map/ppermute | solution.py:327
  88.2 22.7 %collective-permute-start.20 = (bf16[2,4,3,128,128]{4,3,2,1,0:T(8,128)(2,1)}, bf16[2,4,3,128,128]{4,3,2,1,0:T(8,128)(2,1)S(1)}, u32[]{:S(2)}, u32[]{:S(2)}) collective-permute-start(bf16[2,4,3,128,128]{4,3,2,1,0:T(8,128)(2,1)} %get-tuple-element.41), channel_id=1, source_target_pairs={{0,3},{1,2},{2,1},{3,0},{4,7},{5,6},{6,5},{7,4},{8,11},{9,10},{10,... | collective-permute-start | bytes 2359304 | tf_op jit(solution)/shard_map/ppermute | solution.py:327
  90.1 34.1 %collective-permute-start.7 = (bf16[2,4,3,128,128]{4,3,2,1,0:T(8,128)(2,1)}, bf16[2,4,3,128,128]{4,3,2,1,0:T(8,128)(2,1)S(1)}, u32[]{:S(2)}, u32[]{:S(2)}) collective-permute-start(bf16[2,4,3,128,128]{4,3,2,1,0:T(8,128)(2,1)} %get-tuple-element.28), channel_id=1, source_target_pairs={{0,1},{1,0},{2,3},{3,2},{4,5},{5,4},{6,7},{7,6},{8,9},{9,8},{10,11... | collective-permute-start | bytes 2359304 | tf_op jit(solution)/shard_map/ppermute | solution.py:327
  91.0 36.7 %collective-permute-start.9 = (bf16[2,4,3,128,128]{4,3,2,1,0:T(8,128)(2,1)}, bf16[2,4,3,128,128]{4,3,2,1,0:T(8,128)(2,1)S(1)}, u32[]{:S(2)}, u32[]{:S(2)}) collective-permute-start(bf16[2,4,3,128,128]{4,3,2,1,0:T(8,128)(2,1)} %get-tuple-element.30), channel_id=1, source_target_pairs={{0,3},{1,2},{2,1},{3,0},{4,7},{5,6},{6,5},{7,4},{8,11},{9,10},{10,... | collective-permute-start | bytes 2359304 | tf_op jit(solution)/shard_map/ppermute | solution.py:327
  107.4 21.3 %copy-start.3 = (bf16[2,4,3,128,128]{4,3,2,1,0:T(8,128)(2,1)}, bf16[2,4,3,128,128]{4,3,2,1,0:T(8,128)(2,1)S(1)}, u32[]{:S(2)}) copy-start(bf16[2,4,3,128,128]{4,3,2,1,0:T(8,128)(2,1)S(1)} %collective-permute-done.18.refs_1_) | copy-start | bytes 2359300
  109.5 25.7 %collective-permute-start.19 = (bf16[4,3,128,128]{3,2,1,0:T(8,128)(2,1)}, bf16[4,3,128,128]{3,2,1,0:T(8,128)(2,1)}, u32[]{:S(2)}, u32[]{:S(2)}) collective-permute-start(bf16[4,3,128,128]{3,2,1,0:T(8,128)(2,1)} %fusion.2), channel_id=1, source_target_pairs={{0,3},{1,2},{2,1},{3,0},{4,7},{5,6},{6,5},{7,4},{8,11},{9,10},{10,... | collective-permute-start | bytes 1179656 | tf_op jit(solution)/shard_map/ppermute | solution.py:327
  110.9 17.9 %copy-start.4 = (bf16[2,4,3,128,128]{4,3,2,1,0:T(8,128)(2,1)}, bf16[2,4,3,128,128]{4,3,2,1,0:T(8,128)(2,1)S(1)}, u32[]{:S(2)}) copy-start(bf16[2,4,3,128,128]{4,3,2,1,0:T(8,128)(2,1)S(1)} %collective-permute-done.20.refs_4_) | copy-start | bytes 2359300
  113.0 22.2 %collective-permute-start.21 = (bf16[4,3,128,128]{3,2,1,0:T(8,128)(2,1)}, bf16[4,3,128,128]{3,2,1,0:T(8,128)(2,1)}, u32[]{:S(2)}, u32[]{:S(2)}) collective-permute-start(bf16[4,3,128,128]{3,2,1,0:T(8,128)(2,1)} %fusion.3), channel_id=1, source_target_pairs={{0,1},{1,0},{2,3},{3,2},{4,5},{5,4},{6,7},{7,6},{8,9},{9,8},{10,11... | collective-permute-start | bytes 1179656 | tf_op jit(solution)/shard_map/ppermute | solution.py:327
  124.3 4.5 %copy-start.1 = (bf16[2,4,3,128,128]{4,3,2,1,0:T(8,128)(2,1)}, bf16[2,4,3,128,128]{4,3,2,1,0:T(8,128)(2,1)S(1)}, u32[]{:S(2)}) copy-start(bf16[2,4,3,128,128]{4,3,2,1,0:T(8,128)(2,1)S(1)} %collective-permute-done.7.refs_1_) | copy-start | bytes 2359300
  126.4 14.4 %collective-permute-start.8 = (bf16[4,3,128,128]{3,2,1,0:T(8,128)(2,1)}, bf16[4,3,128,128]{3,2,1,0:T(8,128)(2,1)}, u32[]{:S(2)}, u32[]{:S(2)}) collective-permute-start(bf16[4,3,128,128]{3,2,1,0:T(8,128)(2,1)} %fusion), channel_id=1, source_target_pairs={{0,3},{1,2},{2,1},{3,0},{4,7},{5,6},{6,5},{7,4},{8,11},{9,10},{10,... | collective-permute-start | bytes 1179656 | tf_op jit(solution)/shard_map/ppermute | solution.py:327
  127.7 1.0 copy-start.2
  128.8 12.0 %collective-permute-start.10 = (bf16[4,3,128,128]{3,2,1,0:T(8,128)(2,1)}, bf16[4,3,128,128]{3,2,1,0:T(8,128)(2,1)}, u32[]{:S(2)}, u32[]{:S(2)}) collective-permute-start(bf16[4,3,128,128]{3,2,1,0:T(8,128)(2,1)} %fusion.1), channel_id=1, source_target_pairs={{0,1},{1,0},{2,3},{3,2},{4,5},{5,4},{6,7},{7,6},{8,9},{9,8},{10,11... | collective-permute-start | bytes 1179656 | tf_op jit(solution)/shard_map/ppermute | solution.py:327

commit v4 on v3

--- a/solution.py
+++ b/solution.py
@@ -10,7 +10,7 @@
 
 
 SPREAD_ROWS = 3
-GROUP = 8
+GROUPS = (16, 32)
 BATCH = 2
 VMEM_LIMIT = 67_000_000
 
@@ -92,7 +92,8 @@
 class Lists:
     def __init__(self, slab, slots, per, n_products, kept):
         self.slab, self.slots, self.per = slab, slots, per
-        self.pitch = n_products * slots * per + GROUP
+        self.group = GROUPS[n_products - 1]
+        self.pitch = n_products * slots * per + self.group
         self.kept = slab if kept else None
         self.list = slab + (2 * slab * per if kept else 0)
         self.size = self.list + slab * self.pitch
@@ -138,7 +139,7 @@
             for target, entry in found:
                 meta[end] = entry + target
                 end += jnp.where(target < slots, 1, 0)
-        for u in range(GROUP):
+        for u in range(lay.group):
             meta[end + u] = slots
         meta[s] = end - start
         if lay.kept is not None:
@@ -266,15 +267,15 @@
             total[...] = jnp.zeros_like(total)
 
             def add_group(group, inner):
-                for u in range(GROUP):
-                    code = meta[lay.list + row * lay.pitch + group * GROUP + u]
+                for u in range(lay.group):
+                    code = meta[lay.list + row * lay.pitch + group * lay.group + u]
                     total[code & 15] += jnp.dot(
                         left[row, code >> 13], window[(code >> 4) & 511],
                         preferred_element_type=jnp.float32,
                     )
                 return inner
 
-            lax.fori_loop(0, (meta[row] + GROUP - 1) // GROUP, add_group, 0)
+            lax.fori_loop(0, (meta[row] + lay.group - 1) // lay.group, add_group, 0)
             for at, q in enumerate(HALF_ORDER[half]):
                 stage = stages[2 * half + (1 if at < 2 else 0)]
                 for j in range(per):
@@ -422,6 +423,10 @@
     square_meta = planned(
         square_lay, reach, window_rows, ((0, 0, 0),), table, row_slot, (p_cols,), (out_pcols,)
     )
+    tangent_meta = planned(
+        tangent_lay, reach, window_rows, ((0, 1, 1), (1, 0, 1)), table, row_slot,
+        (p_cols, d_cols), (out_pcols, out_dcols),
+    )
     p_window = inner(p_window)
     d_window = inner(d_window)
     sent_a, keep_a, sent_b, keep_b = block_products(
@@ -429,11 +434,6 @@
     )
     first_a = met(sent_a, 1)
     first_b = met(sent_b, 3)
-    keep_a, later_slot = lax.optimization_barrier((keep_a, row_slot))
-    tangent_meta = planned(
-        tangent_lay, reach, window_rows, ((0, 1, 1), (1, 0, 1)), table, later_slot,
-        (p_cols, d_cols), (out_pcols, out_dcols),
-    )
     tsent_a, tkeep_a, tsent_b, tkeep_b = block_products(
         tangent_lay, (p_blocks, d_blocks), (p_window, d_window), sizes, tangent_meta,
     )

time: 147 us -> 142 us (0.966)
  the two profiles are of different devices: /device:TPU:8 before, /device:TPU:1 now
where the time goes in v4:
time: 142 us; the launch traced here: 141 us
  waiting for transfers between devices  53.5 us (38%)
  Pallas kernels  43.5 us (31%)
  starting transfers between devices  35.9 us (25%)
  other arithmetic  7.07 us (5%)
    ppermute x14, waiting for transfers between devices, swapped(): return lax.ppermute(value, 'rows', pairs)  28.8 us
    ppermute x14, starting transfers between devices, swapped(): return lax.ppermute(value, 'rows', pairs)  24.8 us
    ppermute x8, waiting for transfers between devices, met(): lax.ppermute(value, 'rep', [(i, i ^ flip) for i in range(lax.axis_size('r...  24.7 us
    pallas_call x2, Pallas kernels, block_products(): pl.pallas_call(functools.partial(product_kernel, lay, len(lefts), sizes),...  17.8 us
    pallas_call x2, Pallas kernels, planned(): pl.pallas_call(functools.partial(plan_kernel, lay, reach, window_rows, pr...  11.9 us
    ppermute x8, starting transfers between devices, met(): lax.ppermute(value, 'rep', [(i, i ^ flip) for i in range(lax.axis_size('r...  11.1 us
    convert_element_type x4, other arithmetic, pair_sum(): (keep[1].astype(jnp.float32) + got[1].astype(jnp.float32)).astype(jnp.bfl...  7.07 us
    pallas_call x2, Pallas kernels, finish(): pl.pallas_call(functools.partial(finish_kernel, which), in_specs=[pl.Bloc...  7.02 us
  transfers between devices with their start and end apart: 22, of which 8 were waited for; matrix products, arithmetic and copies ran while one was open for 5% of the time, Pallas kernels for 19%

profile of v4, /device:TPU:1, one launch (start us, length us, event | category | flops | bytes accessed | tf_op | source)
XLA Modules:
  0.0 141.3 jit_solution(18023631076704432719)
XLA Ops:
  0.6 3.0 %pack.1 = (bf16[8,3,128,128]{3,2,1,0:T(8,128)(2,1)}, bf16[6,3,128,128]{3,2,1,0:T(8,128)(2,1)}, bf16[2,3,128,128]{3,2,1,0:T(8,128)(2,1)}, bf16[2,3,128,128]{3,2,1...) custom-call(bf16[8,12,128,128]{3,2,1,0:T(8,128)(2,1)} %p_ref.1, ...), custom_call_target="tpu_custom_call" | custom-call | flops 3000000000 | bytes 4194304 | tf_op jit(solution)/shard_map/pack/pallas_call | solution.py:76
  3.6 2.7 %collective-permute-start.1 = (bf16[8,3,128,128]{3,2,1,0:T(8,128)(2,1)}, bf16[8,3,128,128]{3,2,1,0:T(8,128)(2,1)}, u32[]{:S(2)}, u32[]{:S(2)}) collective-permute-start(bf16[8,3,128,128]{3,2,1,0:T(8,128)(2,1)} %get-tuple-element.20), channel_id=1, source_target_pairs={{0,252},{4,8},{8,4},{12,16},{16,12},{20,24},{24,20},{28,32},{32,28... | collective-permute-start | bytes 2359304 | tf_op jit(solution)/shard_map/ppermute | solution.py:41
  6.3 0.1 collective-permute-start.12
  6.4 11.0 %collective-permute-start.3 = (bf16[2,3,128,128]{3,2,1,0:T(8,128)(2,1)}, bf16[2,3,128,128]{3,2,1,0:T(8,128)(2,1)S(1)}, u32[]{:S(2)}, u32[]{:S(2)}) collective-permute-start(bf16[2,3,128,128]{3,2,1,0:T(8,128)(2,1)} %get-tuple-element.22), channel_id=1, source_target_pairs={{0,8},{4,252},{8,16},{12,4},{16,24},{20,12},{24,32},{28,20},{32,40... | collective-permute-start | bytes 589832 | tf_op jit(solution)/shard_map/ppermute | solution.py:41
  17.4 0.0 collective-permute-start.14
  17.4 0.0 collective-permute-start.2
  17.4 5.0 %collective-permute-done.3 = bf16[2,3,128,128]{3,2,1,0:T(8,128)(2,1)S(1)} collective-permute-done((bf16[2,3,128,128]{3,2,1,0:T(8,128)(2,1)}, bf16[2,3,128,128]{3,2,1,0:T(8,128)(2,1)S(1)}, u32[]{:S(2)}, u32[]{:S(2)}) %collective-permute-start.3) | collective-permute-done | bytes 196640 | tf_op jit(solution)/shard_map/ppermute | solution.py:41
  22.4 0.0 collective-permute-start.4
  22.4 4.3 %collective-permute-done.14 = bf16[2,3,128,128]{3,2,1,0:T(8,128)(2,1)S(1)} collective-permute-done((bf16[2,3,128,128]{3,2,1,0:T(8,128)(2,1)}, bf16[2,3,128,128]{3,2,1,0:T(8,128)(2,1)S(1)}, u32[]{:S(2)}, u32[]{:S(2)}) %collective-permute-start.14) | collective-permute-done | bytes 196640 | tf_op jit(solution)/shard_map/ppermute | solution.py:41
  26.7 0.0 collective-permute-start.15
  26.7 18.5 %collective-permute-done.4 = bf16[2,3,128,128]{3,2,1,0:T(8,128)(2,1)S(1)} collective-permute-done((bf16[2,3,128,128]{3,2,1,0:T(8,128)(2,1)}, bf16[2,3,128,128]{3,2,1,0:T(8,128)(2,1)S(1)}, u32[]{:S(2)}, u32[]{:S(2)}) %collective-permute-start.4) | collective-permute-done | bytes 196640 | tf_op jit(solution)/shard_map/ppermute | solution.py:41
  45.3 5.2 %collective-permute-start.6 = (bf16[2,3,128,128]{3,2,1,0:T(8,128)(2,1)S(1)}, bf16[2,3,128,128]{3,2,1,0:T(8,128)(2,1)S(1)}, u32[]{:S(2)}, u32[]{:S(2)}) collective-permute-start(bf16[2,3,128,128]{3,2,1,0:T(8,128)(2,1)S(1)} %collective-permute-done.3), channel_id=1, source_target_pairs={{0,4},{4,0},{8,12},{12,8},{16,20},{20,16},{24,28},{28,24},{32,36},... | collective-permute-start | bytes 589832 | tf_op jit(solution)/shard_map/ppermute | solution.py:41
  50.5 0.0 collective-permute-done.15
  50.5 2.1 %collective-permute-start.17 = (bf16[2,3,128,128]{3,2,1,0:T(8,128)(2,1)S(1)}, bf16[2,3,128,128]{3,2,1,0:T(8,128)(2,1)S(1)}, u32[]{:S(2)}, u32[]{:S(2)}) collective-permute-start(bf16[2,3,128,128]{3,2,1,0:T(8,128)(2,1)S(1)} %collective-permute-done.14), channel_id=1, source_target_pairs={{0,4},{4,0},{8,12},{12,8},{16,20},{20,16},{24,28},{28,24},{32,36},... | collective-permute-start | bytes 589832 | tf_op jit(solution)/shard_map/ppermute | solution.py:41
  52.6 0.1 collective-permute-start
  52.7 1.0 collective-permute-done.17
  53.7 0.4 collective-permute-start.11
  54.1 0.0 collective-permute-done.1
  54.1 0.3 copy-done.8
  54.4 0.4 collective-permute-start.5
  54.8 0.0 collective-permute-done.12
  54.8 0.1 collective-permute-start.16
  54.9 2.7 %collective-permute-start.13 = (bf16[6,3,128,128]{3,2,1,0:T(8,128)(2,1)}, bf16[6,3,128,128]{3,2,1,0:T(8,128)(2,1)}, u32[]{:S(2)}, u32[]{:S(2)}) collective-permute-start(bf16[6,3,128,128]{3,2,1,0:T(8,128)(2,1)} %get-tuple-element.29), channel_id=1, source_target_pairs={{0,8},{4,252},{8,16},{12,4},{16,24},{20,12},{24,32},{28,20},{32,40... | collective-permute-start | bytes 1769480 | tf_op jit(solution)/shard_map/ppermute | solution.py:41
  57.6 4.2 %plan.2.meta = s32[424]{0:T(512)} custom-call(s32[112]{0:T(128)} %constant.2.clone.table, s32[512]{0:T(512)} %row_slot.3, s32[12,512]{1,0:T(8,128)} %bitcast.38, s32[8,12]{1,0:T(8,128)} %refs_2_.1), custom_call_target="tpu_custom_call" | custom-call | flops 4000000000 | bytes 65536 | tf_op jit(solution)/shard_map/plan/pallas_call | solution.py:166
  61.8 7.7 %plan.3.meta = s32[888]{0:T(1024)} custom-call(s32[112]{0:T(128)} %constant.2.clone.table, s32[512]{0:T(512)} %row_slot.3, s32[12,512]{1,0:T(8,128)} %bitcast.39, s32[12,512]{1,0:T(8,128)} %bitcast.40, s32[8,12]{1,0:T(8,128)} %refs_2_.1, s32[8,12]{1,0:T(8,128)} %refs_3_.1), custom_call_target="tpu_custom_call" | custom-call | flops 4000000000 | bytes 65536 | tf_op jit(solution)/shard_map/plan/pallas_call | solution.py:166
  69.5 0.0 collective-permute-done.13
  69.6 0.0 collective-permute-done.5
  69.6 0.0 collective-permute-done.16
  69.6 10.2 %shard_map.105 = (bf16[2,4,3,128,128]{4,3,2,1,0:T(8,128)(2,1)}, bf16[2,4,3,128,128]{4,3,2,1,0:T(8,128)(2,1)}, bf16[2,4,3,128,128]{4,3,2,1,0:T(8,128)(2,1)}, bf16[2,4,3,128,128]{4,3,2,1,0:T(8,128)(2,1)}) custom-call(s32[888]{0:T(1024)} %plan.3.meta, bf16[8,12,128,128]{3,2,1,0:T(8,128)(2,1)} %p_ref.1, bf16[8,12,128,128]{3,2,1,0:T(8,128)(2,1)} %d_ref.1, ...), custom_call_target="tpu_custom_call" | custom-call | flops 8000000000 | bytes 14942208 | tf_op jit(solution)/shard_map/pallas_call | solution.py:305
  79.8 4.3 %collective-permute-start.20 = (bf16[2,4,3,128,128]{4,3,2,1,0:T(8,128)(2,1)}, bf16[2,4,3,128,128]{4,3,2,1,0:T(8,128)(2,1)}, u32[]{:S(2)}, u32[]{:S(2)}) collective-permute-start(bf16[2,4,3,128,128]{4,3,2,1,0:T(8,128)(2,1)} %get-tuple-element.37), channel_id=1, source_target_pairs={{0,3},{1,2},{2,1},{3,0},{4,7},{5,6},{6,5},{7,4},{8,11},{9,10},{10,... | collective-permute-start | bytes 2359304 | tf_op jit(solution)/shard_map/ppermute | solution.py:328
  84.0 0.0 collective-permute-start.18
  84.1 7.6 %shard_map.104 = (bf16[2,4,3,128,128]{4,3,2,1,0:T(8,128)(2,1)}, bf16[2,4,3,128,128]{4,3,2,1,0:T(8,128)(2,1)}, bf16[2,4,3,128,128]{4,3,2,1,0:T(8,128)(2,1)}, bf16[2,4,3,128,128]{4,3,2,1,0:T(8,128)(2,1)}) custom-call(s32[424]{0:T(512)} %plan.2.meta, bf16[8,12,128,128]{3,2,1,0:T(8,128)(2,1)} %p_ref.1, bf16[24,128,128]{2,1,0:T(8,128)(2,1)} %bitcast.27, ...), custom_call_target="tpu_custom_call" | custom-call | flops 8000000000 | bytes 10616832 | tf_op jit(solution)/shard_map/pallas_call | solution.py:305
  91.7 0.1 collective-permute-start.9
  91.8 1.4 %collective-permute-start.7 = (bf16[2,4,3,128,128]{4,3,2,1,0:T(8,128)(2,1)}, bf16[2,4,3,128,128]{4,3,2,1,0:T(8,128)(2,1)S(1)}, u32[]{:S(2)}, u32[]{:S(2)}) collective-permute-start(bf16[2,4,3,128,128]{4,3,2,1,0:T(8,128)(2,1)} %get-tuple-element.25), channel_id=1, source_target_pairs={{0,1},{1,0},{2,3},{3,2},{4,5},{5,4},{6,7},{7,6},{8,9},{9,8},{10,11... | collective-permute-start | bytes 2359304 | tf_op jit(solution)/shard_map/ppermute | solution.py:328
  93.2 9.1 %collective-permute-done.20.refs_4_ = bf16[2,4,3,128,128]{4,3,2,1,0:T(8,128)(2,1)} collective-permute-done((bf16[2,4,3,128,128]{4,3,2,1,0:T(8,128)(2,1)}, bf16[2,4,3,128,128]{4,3,2,1,0:T(8,128)(2,1)}, u32[]{:S(2)}, u32[]{:S(2)}) %collective-permute-start.20) | collective-permute-done | bytes 786464 | tf_op jit(solution)/shard_map/ppermute | solution.py:328
  102.4 2.0 %fusion.3 = bf16[4,3,128,128]{3,2,1,0:T(8,128)(2,1)} fusion(bf16[2,4,3,128,128]{4,3,2,1,0:T(8,128)(2,1)} %collective-permute-done.20.refs_4_, bf16[2,4,3,128,128]{4,3,2,1,0:T(8,128)(2,1)} %get-tuple-element.36.refs_3_), kind=kLoop, calls=%fused_computation.7 | loop fusion | flops 786432 | bytes 1179648 | tf_op jit(solution)/shard_map/convert_element_type | solution.py:393
  104.3 2.0 %fusion.2 = bf16[4,3,128,128]{3,2,1,0:T(8,128)(2,1)} fusion(bf16[2,4,3,128,128]{4,3,2,1,0:T(8,128)(2,1)} %collective-permute-done.18.refs_1_, bf16[2,4,3,128,128]{4,3,2,1,0:T(8,128)(2,1)} %get-tuple-element.34.refs_0_), kind=kLoop, calls=%fused_computation.6 | loop fusion | flops 786432 | bytes 1179648 | tf_op jit(solution)/shard_map/convert_element_type | solution.py:393
  106.3 2.7 %collective-permute-start.19 = (bf16[4,3,128,128]{3,2,1,0:T(8,128)(2,1)}, bf16[4,3,128,128]{3,2,1,0:T(8,128)(2,1)}, u32[]{:S(2)}, u32[]{:S(2)}) collective-permute-start(bf16[4,3,128,128]{3,2,1,0:T(8,128)(2,1)} %fusion.2), channel_id=1, source_target_pairs={{0,3},{1,2},{2,1},{3,0},{4,7},{5,6},{6,5},{7,4},{8,11},{9,10},{10,... | collective-permute-start | bytes 1179656 | tf_op jit(solution)/shard_map/ppermute | solution.py:328
  109.0 10.3 %collective-permute-done.9.refs_4_ = bf16[2,4,3,128,128]{4,3,2,1,0:T(8,128)(2,1)S(1)} collective-permute-done((bf16[2,4,3,128,128]{4,3,2,1,0:T(8,128)(2,1)}, bf16[2,4,3,128,128]{4,3,2,1,0:T(8,128)(2,1)S(1)}, u32[]{:S(2)}, u32[]{:S(2)}) %collective-permute-start.9) | collective-permute-done | bytes 786464 | tf_op jit(solution)/shard_map/ppermute | solution.py:328
  119.3 2.1 %fusion.1 = bf16[4,3,128,128]{3,2,1,0:T(8,128)(2,1)} fusion(bf16[2,4,3,128,128]{4,3,2,1,0:T(8,128)(2,1)S(1)} %collective-permute-done.9.refs_4_, bf16[2,4,3,128,128]{4,3,2,1,0:T(8,128)(2,1)} %get-tuple-element.26.refs_3_), kind=kLoop, calls=%fused_computation.5 | loop fusion | flops 786432 | bytes 1179648 | tf_op jit(solution)/shard_map/convert_element_type | solution.py:393
  121.5 1.0 fusion
  122.5 0.0 copy-done.2
  122.5 2.7 %collective-permute-start.8 = (bf16[4,3,128,128]{3,2,1,0:T(8,128)(2,1)}, bf16[4,3,128,128]{3,2,1,0:T(8,128)(2,1)}, u32[]{:S(2)}, u32[]{:S(2)}) collective-permute-start(bf16[4,3,128,128]{3,2,1,0:T(8,128)(2,1)} %fusion), channel_id=1, source_target_pairs={{0,3},{1,2},{2,1},{3,0},{4,7},{5,6},{6,5},{7,4},{8,11},{9,10},{10,... | collective-permute-start | bytes 1179656 | tf_op jit(solution)/shard_map/ppermute | solution.py:328
  125.1 3.7 %kept.1.refs_6_ = bf16[2,8,3,128,128]{4,3,2,1,0:T(8,128)(2,1)} custom-call(s32[888]{0:T(1024)} %plan.3.meta, bf16[8,12,128,128]{3,2,1,0:T(8,128)(2,1)} %p_ref.1, bf16[8,12,128,128]{3,2,1,0:T(8,128)(2,1)} %d_ref.1), custom_call_target="tpu_custom_call" | custom-call | flops 3000000000 | bytes 2097152 | tf_op jit(solution)/shard_map/kept/pallas_call | solution.py:206
  128.9 0.3 collective-permute-done.21.refs_5_
  129.2 3.5 %finish.3 = bf16[8,3,128,128]{3,2,1,0:T(8,128)(2,1)} custom-call(s32[8]{0:T(128)} %branch_ref.3, bf16[2,4,3,128,128]{4,3,2,1,0:T(8,128)(2,1)} %get-tuple-element.34.refs_0_, bf16[2,4,3,128,128]{4,3,2,1,0:T(8,128)(2,1)} %collective-permute-done.18.refs_1_, bf16[4,3,128,128]{3,2,1,0:T(8,128)(2,1)} %collective-permute-done.19.refs_2_, ...), custom_call_target="tpu_custom_call" | custom-call | flops 2000000000 | bytes 4194304 | tf_op jit(solution)/shard_map/finish/pallas_call | solution.py:375
  132.7 4.9 %collective-permute-done.10.refs_5_ = bf16[4,3,128,128]{3,2,1,0:T(8,128)(2,1)} collective-permute-done((bf16[4,3,128,128]{3,2,1,0:T(8,128)(2,1)}, bf16[4,3,128,128]{3,2,1,0:T(8,128)(2,1)}, u32[]{:S(2)}, u32[]{:S(2)}) %collective-permute-start.10) | collective-permute-done | bytes 393248 | tf_op jit(solution)/shard_map/ppermute | solution.py:328
  137.6 3.5 %finish.2 = bf16[8,3,128,128]{3,2,1,0:T(8,128)(2,1)} custom-call(s32[8]{0:T(128)} %branch_ref.3, bf16[2,4,3,128,128]{4,3,2,1,0:T(8,128)(2,1)} %get-tuple-element.24.refs_0_, bf16[2,4,3,128,128]{4,3,2,1,0:T(8,128)(2,1)} %copy-done.2, bf16[4,3,128,128]{3,2,1,0:T(8,128)(2,1)} %collective-permute-done.8.refs_2_, ...), custom_call_target="tpu_custom_call" | custom-call | flops 2000000000 | bytes 4194304 | tf_op jit(solution)/shard_map/finish/pallas_call | solution.py:375
  (26 shorter events, 0.1 us)
Async XLA Ops:
  3.6 50.4 %collective-permute-start.1 = (bf16[8,3,128,128]{3,2,1,0:T(8,128)(2,1)}, bf16[8,3,128,128]{3,2,1,0:T(8,128)(2,1)}, u32[]{:S(2)}, u32[]{:S(2)}) collective-permute-start(bf16[8,3,128,128]{3,2,1,0:T(8,128)(2,1)} %get-tuple-element.20), channel_id=1, source_target_pairs={{0,252},{4,8},{8,4},{12,16},{16,12},{20,24},{24,20},{28,32},{32,28... | collective-permute-start | bytes 2359304 | tf_op jit(solution)/shard_map/ppermute | solution.py:41
  6.3 48.4 %collective-permute-start.12 = (bf16[8,3,128,128]{3,2,1,0:T(8,128)(2,1)}, bf16[8,3,128,128]{3,2,1,0:T(8,128)(2,1)}, u32[]{:S(2)}, u32[]{:S(2)}) collective-permute-start(bf16[8,3,128,128]{3,2,1,0:T(8,128)(2,1)} %get-tuple-element.28), channel_id=1, source_target_pairs={{0,252},{4,8},{8,4},{12,16},{16,12},{20,24},{24,20},{28,32},{32,28... | collective-permute-start | bytes 2359304 | tf_op jit(solution)/shard_map/ppermute | solution.py:41
  6.4 16.0 %collective-permute-start.3 = (bf16[2,3,128,128]{3,2,1,0:T(8,128)(2,1)}, bf16[2,3,128,128]{3,2,1,0:T(8,128)(2,1)S(1)}, u32[]{:S(2)}, u32[]{:S(2)}) collective-permute-start(bf16[2,3,128,128]{3,2,1,0:T(8,128)(2,1)} %get-tuple-element.22), channel_id=1, source_target_pairs={{0,8},{4,252},{8,16},{12,4},{16,24},{20,12},{24,32},{28,20},{32,40... | collective-permute-start | bytes 589832 | tf_op jit(solution)/shard_map/ppermute | solution.py:41
  17.4 9.3 %collective-permute-start.14 = (bf16[2,3,128,128]{3,2,1,0:T(8,128)(2,1)}, bf16[2,3,128,128]{3,2,1,0:T(8,128)(2,1)S(1)}, u32[]{:S(2)}, u32[]{:S(2)}) collective-permute-start(bf16[2,3,128,128]{3,2,1,0:T(8,128)(2,1)} %get-tuple-element.30), channel_id=1, source_target_pairs={{0,8},{4,252},{8,16},{12,4},{16,24},{20,12},{24,32},{28,20},{32,40... | collective-permute-start | bytes 589832 | tf_op jit(solution)/shard_map/ppermute | solution.py:41
  17.4 37.5 %collective-permute-start.2 = (bf16[6,3,128,128]{3,2,1,0:T(8,128)(2,1)}, bf16[6,3,128,128]{3,2,1,0:T(8,128)(2,1)}, u32[]{:S(2)}, u32[]{:S(2)}) collective-permute-start(bf16[6,3,128,128]{3,2,1,0:T(8,128)(2,1)} %get-tuple-element.21), channel_id=1, source_target_pairs={{0,8},{4,252},{8,16},{12,4},{16,24},{20,12},{24,32},{28,20},{32,40... | collective-permute-start | bytes 1769480 | tf_op jit(solution)/shard_map/ppermute | solution.py:41
  22.4 22.9 %copy-start.3 = (bf16[2,3,128,128]{3,2,1,0:T(8,128)(2,1)}, bf16[2,3,128,128]{3,2,1,0:T(8,128)(2,1)S(1)}, u32[]{:S(2)}) copy-start(bf16[2,3,128,128]{3,2,1,0:T(8,128)(2,1)S(1)} %collective-permute-done.3) | copy-start | bytes 589828
  22.4 22.9 %collective-permute-start.4 = (bf16[2,3,128,128]{3,2,1,0:T(8,128)(2,1)}, bf16[2,3,128,128]{3,2,1,0:T(8,128)(2,1)S(1)}, u32[]{:S(2)}, u32[]{:S(2)}) collective-permute-start(bf16[2,3,128,128]{3,2,1,0:T(8,128)(2,1)} %get-tuple-element.23), channel_id=1, source_target_pairs={{0,244},{4,16},{8,252},{12,24},{16,4},{20,32},{24,12},{28,40},{32,... | collective-permute-start | bytes 589832 | tf_op jit(solution)/shard_map/ppermute | solution.py:41
  26.7 26.0 %copy-start.5 = (bf16[2,3,128,128]{3,2,1,0:T(8,128)(2,1)}, bf16[2,3,128,128]{3,2,1,0:T(8,128)(2,1)S(1)}, u32[]{:S(2)}) copy-start(bf16[2,3,128,128]{3,2,1,0:T(8,128)(2,1)S(1)} %collective-permute-done.14) | copy-start | bytes 589828
  26.7 23.8 %collective-permute-start.15 = (bf16[2,3,128,128]{3,2,1,0:T(8,128)(2,1)}, bf16[2,3,128,128]{3,2,1,0:T(8,128)(2,1)S(1)}, u32[]{:S(2)}, u32[]{:S(2)}) collective-permute-start(bf16[2,3,128,128]{3,2,1,0:T(8,128)(2,1)} %get-tuple-element.31), channel_id=1, source_target_pairs={{0,244},{4,16},{8,252},{12,24},{16,4},{20,32},{24,12},{28,40},{32,... | collective-permute-start | bytes 589832 | tf_op jit(solution)/shard_map/ppermute | solution.py:41
  45.3 7.4 %copy-start.4 = (bf16[2,3,128,128]{3,2,1,0:T(8,128)(2,1)}, bf16[2,3,128,128]{3,2,1,0:T(8,128)(2,1)S(1)}, u32[]{:S(2)}) copy-start(bf16[2,3,128,128]{3,2,1,0:T(8,128)(2,1)S(1)} %collective-permute-done.4) | copy-start | bytes 589828
  45.3 7.4 %collective-permute-start.6 = (bf16[2,3,128,128]{3,2,1,0:T(8,128)(2,1)S(1)}, bf16[2,3,128,128]{3,2,1,0:T(8,128)(2,1)S(1)}, u32[]{:S(2)}, u32[]{:S(2)}) collective-permute-start(bf16[2,3,128,128]{3,2,1,0:T(8,128)(2,1)S(1)} %collective-permute-done.3), channel_id=1, source_target_pairs={{0,4},{4,0},{8,12},{12,8},{16,20},{20,16},{24,28},{28,24},{32,36},... | collective-permute-start | bytes 589832 | tf_op jit(solution)/shard_map/ppermute | solution.py:41
  50.5 3.6 %copy-start.7 = (bf16[2,3,128,128]{3,2,1,0:T(8,128)(2,1)}, bf16[2,3,128,128]{3,2,1,0:T(8,128)(2,1)S(1)}, u32[]{:S(2)}) copy-start(bf16[2,3,128,128]{3,2,1,0:T(8,128)(2,1)S(1)} %collective-permute-done.15) | copy-start | bytes 589828
  50.5 3.2 %collective-permute-start.17 = (bf16[2,3,128,128]{3,2,1,0:T(8,128)(2,1)S(1)}, bf16[2,3,128,128]{3,2,1,0:T(8,128)(2,1)S(1)}, u32[]{:S(2)}, u32[]{:S(2)}) collective-permute-start(bf16[2,3,128,128]{3,2,1,0:T(8,128)(2,1)S(1)} %collective-permute-done.14), channel_id=1, source_target_pairs={{0,4},{4,0},{8,12},{12,8},{16,20},{20,16},{24,28},{28,24},{32,36},... | collective-permute-start | bytes 589832 | tf_op jit(solution)/shard_map/ppermute | solution.py:41
  52.6 1.1 copy-start.6
  52.6 16.9 %collective-permute-start = (bf16[8,3,128,128]{3,2,1,0:T(8,128)(2,1)}, bf16[8,3,128,128]{3,2,1,0:T(8,128)(2,1)}, u32[]{:S(2)}, u32[]{:S(2)}) collective-permute-start(bf16[8,3,128,128]{3,2,1,0:T(8,128)(2,1)} %get-tuple-element.20), channel_id=1, source_target_pairs={{0,4},{4,0},{8,12},{12,8},{16,20},{20,16},{24,28},{28,24},{32,36},... | collective-permute-start | bytes 2359304 | tf_op jit(solution)/shard_map/ppermute | solution.py:41
  53.7 0.7 copy-start.8
  53.7 15.8 %collective-permute-start.11 = (bf16[8,3,128,128]{3,2,1,0:T(8,128)(2,1)}, bf16[8,3,128,128]{3,2,1,0:T(8,128)(2,1)}, u32[]{:S(2)}, u32[]{:S(2)}) collective-permute-start(bf16[8,3,128,128]{3,2,1,0:T(8,128)(2,1)} %get-tuple-element.28), channel_id=1, source_target_pairs={{0,4},{4,0},{8,12},{12,8},{16,20},{20,16},{24,28},{28,24},{32,36},... | collective-permute-start | bytes 2359304 | tf_op jit(solution)/shard_map/ppermute | solution.py:41
  54.4 15.2 %collective-permute-start.5 = (bf16[8,3,128,128]{3,2,1,0:T(8,128)(2,1)}, bf16[8,3,128,128]{3,2,1,0:T(8,128)(2,1)}, u32[]{:S(2)}, u32[]{:S(2)}) collective-permute-start(bf16[8,3,128,128]{3,2,1,0:T(8,128)(2,1)} %collective-permute-done.1), channel_id=1, source_target_pairs={{0,4},{4,0},{8,12},{12,8},{16,20},{20,16},{24,28},{28,24},{32,36},... | collective-permute-start | bytes 2359304 | tf_op jit(solution)/shard_map/ppermute | solution.py:41
  54.8 14.8 %collective-permute-start.16 = (bf16[8,3,128,128]{3,2,1,0:T(8,128)(2,1)}, bf16[8,3,128,128]{3,2,1,0:T(8,128)(2,1)}, u32[]{:S(2)}, u32[]{:S(2)}) collective-permute-start(bf16[8,3,128,128]{3,2,1,0:T(8,128)(2,1)} %collective-permute-done.12), channel_id=1, source_target_pairs={{0,4},{4,0},{8,12},{12,8},{16,20},{20,16},{24,28},{28,24},{32,36},... | collective-permute-start | bytes 2359304 | tf_op jit(solution)/shard_map/ppermute | solution.py:41
  54.9 14.6 %collective-permute-start.13 = (bf16[6,3,128,128]{3,2,1,0:T(8,128)(2,1)}, bf16[6,3,128,128]{3,2,1,0:T(8,128)(2,1)}, u32[]{:S(2)}, u32[]{:S(2)}) collective-permute-start(bf16[6,3,128,128]{3,2,1,0:T(8,128)(2,1)} %get-tuple-element.29), channel_id=1, source_target_pairs={{0,8},{4,252},{8,16},{12,4},{16,24},{20,12},{24,32},{28,20},{32,40... | collective-permute-start | bytes 1769480 | tf_op jit(solution)/shard_map/ppermute | solution.py:41
  79.8 22.6 %collective-permute-start.20 = (bf16[2,4,3,128,128]{4,3,2,1,0:T(8,128)(2,1)}, bf16[2,4,3,128,128]{4,3,2,1,0:T(8,128)(2,1)}, u32[]{:S(2)}, u32[]{:S(2)}) collective-permute-start(bf16[2,4,3,128,128]{4,3,2,1,0:T(8,128)(2,1)} %get-tuple-element.37), channel_id=1, source_target_pairs={{0,3},{1,2},{2,1},{3,0},{4,7},{5,6},{6,5},{7,4},{8,11},{9,10},{10,... | collective-permute-start | bytes 2359304 | tf_op jit(solution)/shard_map/ppermute | solution.py:328
  84.0 20.3 %collective-permute-start.18 = (bf16[2,4,3,128,128]{4,3,2,1,0:T(8,128)(2,1)}, bf16[2,4,3,128,128]{4,3,2,1,0:T(8,128)(2,1)}, u32[]{:S(2)}, u32[]{:S(2)}) collective-permute-start(bf16[2,4,3,128,128]{4,3,2,1,0:T(8,128)(2,1)} %get-tuple-element.35), channel_id=1, source_target_pairs={{0,1},{1,0},{2,3},{3,2},{4,5},{5,4},{6,7},{7,6},{8,9},{9,8},{10,11... | collective-permute-start | bytes 2359304 | tf_op jit(solution)/shard_map/ppermute | solution.py:328
  91.7 29.8 %copy-start = (bf16[2,4,3,128,128]{4,3,2,1,0:T(8,128)(2,1)S(1)}, bf16[2,4,3,128,128]{4,3,2,1,0:T(8,128)(2,1)}, u32[]{:S(2)}) copy-start(bf16[2,4,3,128,128]{4,3,2,1,0:T(8,128)(2,1)} %get-tuple-element.24.refs_0_) | copy-start | bytes 2359300
  91.7 27.6 %collective-permute-start.9 = (bf16[2,4,3,128,128]{4,3,2,1,0:T(8,128)(2,1)}, bf16[2,4,3,128,128]{4,3,2,1,0:T(8,128)(2,1)S(1)}, u32[]{:S(2)}, u32[]{:S(2)}) collective-permute-start(bf16[2,4,3,128,128]{4,3,2,1,0:T(8,128)(2,1)} %get-tuple-element.27), channel_id=1, source_target_pairs={{0,3},{1,2},{2,1},{3,0},{4,7},{5,6},{6,5},{7,4},{8,11},{9,10},{10,... | collective-permute-start | bytes 2359304 | tf_op jit(solution)/shard_map/ppermute | solution.py:328
  91.8 29.7 %collective-permute-start.7 = (bf16[2,4,3,128,128]{4,3,2,1,0:T(8,128)(2,1)}, bf16[2,4,3,128,128]{4,3,2,1,0:T(8,128)(2,1)S(1)}, u32[]{:S(2)}, u32[]{:S(2)}) collective-permute-start(bf16[2,4,3,128,128]{4,3,2,1,0:T(8,128)(2,1)} %get-tuple-element.25), channel_id=1, source_target_pairs={{0,1},{1,0},{2,3},{3,2},{4,5},{5,4},{6,7},{7,6},{8,9},{9,8},{10,11... | collective-permute-start | bytes 2359304 | tf_op jit(solution)/shard_map/ppermute | solution.py:328
  104.3 24.9 %collective-permute-start.21 = (bf16[4,3,128,128]{3,2,1,0:T(8,128)(2,1)}, bf16[4,3,128,128]{3,2,1,0:T(8,128)(2,1)}, u32[]{:S(2)}, u32[]{:S(2)}) collective-permute-start(bf16[4,3,128,128]{3,2,1,0:T(8,128)(2,1)} %fusion.3), channel_id=1, source_target_pairs={{0,1},{1,0},{2,3},{3,2},{4,5},{5,4},{6,7},{7,6},{8,9},{9,8},{10,11... | collective-permute-start | bytes 1179656 | tf_op jit(solution)/shard_map/ppermute | solution.py:328
  106.3 22.9 %collective-permute-start.19 = (bf16[4,3,128,128]{3,2,1,0:T(8,128)(2,1)}, bf16[4,3,128,128]{3,2,1,0:T(8,128)(2,1)}, u32[]{:S(2)}, u32[]{:S(2)}) collective-permute-start(bf16[4,3,128,128]{3,2,1,0:T(8,128)(2,1)} %fusion.2), channel_id=1, source_target_pairs={{0,3},{1,2},{2,1},{3,0},{4,7},{5,6},{6,5},{7,4},{8,11},{9,10},{10,... | collective-permute-start | bytes 1179656 | tf_op jit(solution)/shard_map/ppermute | solution.py:328
  119.3 3.1 %copy-start.1 = (bf16[2,4,3,128,128]{4,3,2,1,0:T(8,128)(2,1)}, bf16[2,4,3,128,128]{4,3,2,1,0:T(8,128)(2,1)S(1)}, u32[]{:S(2)}) copy-start(bf16[2,4,3,128,128]{4,3,2,1,0:T(8,128)(2,1)S(1)} %collective-permute-done.9.refs_4_) | copy-start | bytes 2359300
  121.5 16.2 %collective-permute-start.10 = (bf16[4,3,128,128]{3,2,1,0:T(8,128)(2,1)}, bf16[4,3,128,128]{3,2,1,0:T(8,128)(2,1)}, u32[]{:S(2)}, u32[]{:S(2)}) collective-permute-start(bf16[4,3,128,128]{3,2,1,0:T(8,128)(2,1)} %fusion.1), channel_id=1, source_target_pairs={{0,1},{1,0},{2,3},{3,2},{4,5},{5,4},{6,7},{7,6},{8,9},{9,8},{10,11... | collective-permute-start | bytes 1179656 | tf_op jit(solution)/shard_map/ppermute | solution.py:328
  121.5 1.0 copy-start.2
  122.5 15.1 %collective-permute-start.8 = (bf16[4,3,128,128]{3,2,1,0:T(8,128)(2,1)}, bf16[4,3,128,128]{3,2,1,0:T(8,128)(2,1)}, u32[]{:S(2)}, u32[]{:S(2)}) collective-permute-start(bf16[4,3,128,128]{3,2,1,0:T(8,128)(2,1)} %fusion), channel_id=1, source_target_pairs={{0,3},{1,2},{2,1},{3,0},{4,7},{5,6},{6,5},{7,4},{8,11},{9,10},{10,... | collective-permute-start | bytes 1179656 | tf_op jit(solution)/shard_map/ppermute | solution.py:328

commit v5 on v4

--- a/solution.py
+++ b/solution.py
@@ -12,7 +12,7 @@
 SPREAD_ROWS = 3
 GROUPS = (16, 32)
 BATCH = 2
-VMEM_LIMIT = 67_000_000
+VMEM_LIMIT = 22 << 20
 
 
 def window_table(slab, margin):
@@ -41,51 +41,39 @@
     return lax.ppermute(value, "rows", pairs)
 
 
-def pack_kernel(far, *refs):
-    blocks, outs, (held, sems) = refs[:2], refs[2:10], refs[10:]
-    slab, per = held.shape[1:3]
+def pack_kernel(far, slab, per, *refs):
+    blocks, outs, sems = refs[:2], refs[2:10], refs[10]
     core, rep = lax.axis_index("rows") % 2, lax.axis_index("rep")
     rest = slab - far
-    loads = [
-        pltpu.make_async_copy(block.at[:, pl.ds(rep * per, per)], held.at[n], sems.at[n, 4])
-        for n, block in enumerate(blocks)
-    ]
-    for load in loads:
-        load.start()
-    stores = []
-    for n, load in enumerate(loads):
-        load.wait()
-        cuts = (
-            held.at[n],
-            held.at[n, pl.ds(core * far, rest)],
-            held.at[n, pl.ds((1 - core) * rest, far)],
-            held.at[n, pl.ds(core * rest, far)],
-        )
-        for i, cut in enumerate(cuts):
-            store = pltpu.make_async_copy(cut, outs[4 * n + i], sems.at[n, i])
-            store.start()
-            stores.append(store)
-    for store in stores:
-        store.wait()
+    cuts = ((core * rest, far), (0, slab), ((1 - core) * rest, far), (core * far, rest))
+    copies = []
+    for n, block in enumerate(blocks):
+        for i, (first, rows) in enumerate(cuts):
+            copies.append(
+                pltpu.make_async_copy(
+                    block.at[pl.ds(first, rows), pl.ds(rep * per, per)], outs[4 * n + i],
+                    sems.at[n, i],
+                )
+            )
+            copies[-1].start()
+    for copy in copies:
+        copy.wait()
 
 
 def packed(p_blocks, d_blocks, per, far):
     slab, _, side, _ = p_blocks.shape
     dtype = p_blocks.dtype
-    shapes = [(slab, per), (slab - far, per), (far, per), (far, per)] * 2
+    shapes = [(far, per), (slab, per), (far, per), (slab - far, per)] * 2
     outs = pl.pallas_call(
-        functools.partial(pack_kernel, far),
-        in_specs=[pl.BlockSpec(memory_space=pl.ANY)] * 2,
+        functools.partial(pack_kernel, far, slab, per),
+        in_specs=[pl.BlockSpec(memory_space=pltpu.HBM)] * 2,
         out_specs=[pl.BlockSpec(memory_space=pl.ANY)] * 8,
         out_shape=[jax.ShapeDtypeStruct(s + (side, side), dtype) for s in shapes],
-        scratch_shapes=[
-            pltpu.VMEM((2, slab, per, side, side), dtype),
-            pltpu.SemaphoreType.DMA((2, 5)),
-        ],
+        scratch_shapes=[pltpu.SemaphoreType.DMA((2, 4))],
         compiler_params=pltpu.CompilerParams(vmem_limit_bytes=VMEM_LIMIT),
         cost_estimate=pl.CostEstimate(flops=3_000_000_000, bytes_accessed=1 << 22, transcendentals=0),
         name="pack",
-    )(p_blocks, d_blocks)
+    )(*(pltpu.with_memory_space_constraint(b, pltpu.HBM) for b in (p_blocks, d_blocks)))
     return outs[:4], outs[4:]
 
 
@@ -404,7 +392,7 @@
     window_rows = sum(sizes)
 
     def outer(pieces):
-        part, near, rest, edge = pieces
+        edge, part, rest, near = pieces
         out1 = swapped(part, -1, 1)
         far2 = swapped(rest, 2, -2)
         near2 = swapped(near, 2, -2)

time: 142 us -> 142 us (level)
  other arithmetic: 7.07 us -> 0.49 us
  waiting for transfers between devices: 53.5 us -> 59.6 us
  Pallas kernels: 43.5 us -> 47.3 us
  starting transfers between devices: 35.9 us -> 33.8 us
    convert_element_type x4, other arithmetic: 7.07 us -> 0.49 us  [pair_sum(): (keep[1].astype(jnp.float32) + got[1].astype(jnp.float32)).astype(jnp.bfl...]
    ppermute x8, waiting for transfers between devices: 24.7 us -> 31.1 us  [met(): lax.ppermute(value, 'rep', [(i, i ^ flip) for i in range(lax.axis_size('r...]
    pallas_call x2, Pallas kernels: 17.8 us -> 22.9 us  [block_products(): pl.pallas_call(functools.partial(product_kernel, lay, len(lefts), sizes),...]
    ppermute x8, starting transfers between devices: 11.1 us -> 9.02 us  [met(): lax.ppermute(value, 'rep', [(i, i ^ flip) for i in range(lax.axis_size('r...]
  transfers between devices with their start and end apart: 22 -> 22, of which waited for: 8 -> 10; matrix products, arithmetic and copies ran while one was open for 5% -> 0% of each run, Pallas kernels for 19% -> 20%
where the time goes in v5:
time: 142 us
  waiting for transfers between devices  59.6 us (42%)
  Pallas kernels  47.3 us (33%)
  starting transfers between devices  33.8 us (24%)
    ppermute x8, waiting for transfers between devices, met(): lax.ppermute(value, 'rep', [(i, i ^ flip) for i in range(lax.axis_size('r...  31.1 us
    ppermute x14, waiting for transfers between devices, swapped(): return lax.ppermute(value, 'rows', pairs)  28.5 us
    ppermute x14, starting transfers between devices, swapped(): return lax.ppermute(value, 'rows', pairs)  24.8 us
    pallas_call x2, Pallas kernels, block_products(): pl.pallas_call(functools.partial(product_kernel, lay, len(lefts), sizes),...  22.9 us
    pallas_call x2, Pallas kernels, planned(): pl.pallas_call(functools.partial(plan_kernel, lay, reach, window_rows, pr...  11.7 us
    ppermute x8, starting transfers between devices, met(): lax.ppermute(value, 'rep', [(i, i ^ flip) for i in range(lax.axis_size('r...  9.02 us
    pallas_call x2, Pallas kernels, finish(): pl.pallas_call(functools.partial(finish_kernel, which), in_specs=[pl.Bloc...  6.63 us
    pallas_call x1, Pallas kernels, kept_blocks(): pl.pallas_call(functools.partial(kept_kernel, lay), in_specs=[pl.BlockSpe...  3.81 us
  transfers between devices with their start and end apart: 22, of which 10 were waited for; matrix products, arithmetic and copies ran while one was open for 0% of the time, Pallas kernels for 20%

profile of v5, /device:TPU:1, one launch (start us, length us, event | category | flops | bytes accessed | tf_op | source)
XLA Modules:
  0.0 142.4 jit_solution(1244718821417574066)
XLA Ops:
  0.6 0.0 copy-start.8
  0.7 2.3 %pack.1 = (bf16[2,3,128,128]{3,2,1,0:T(8,128)(2,1)S(1)}, bf16[8,3,128,128]{3,2,1,0:T(8,128)(2,1)S(1)}, bf16[2,3,128,128]{3,2,1,0:T(8,128)(2,1)S(1)}, bf16[6,3,12...) custom-call(bf16[8,12,128,128]{3,2,1,0:T(8,128)(2,1)} %p_ref.1, ...), custom_call_target="tpu_custom_call" | custom-call | flops 3000000000 | bytes 4194304 | tf_op jit(solution)/shard_map/pack/pallas_call | solution.py:67
  2.9 2.7 %collective-permute-start.1 = (bf16[8,3,128,128]{3,2,1,0:T(8,128)(2,1)S(1)}, bf16[8,3,128,128]{3,2,1,0:T(8,128)(2,1)S(1)}, u32[]{:S(2)}, u32[]{:S(2)}) collective-permute-start(bf16[8,3,128,128]{3,2,1,0:T(8,128)(2,1)S(1)} %get-tuple-element.20), channel_id=1, source_target_pairs={{0,252},{4,8},{8,4},{12,16},{16,12},{20,24},{24,20},{28,32},{32,28... | collective-permute-start | bytes 2359304 | tf_op jit(solution)/shard_map/ppermute | solution.py:41
  5.6 0.1 collective-permute-start.12
  5.7 11.0 %collective-permute-start.3 = (bf16[2,3,128,128]{3,2,1,0:T(8,128)(2,1)S(1)}, bf16[2,3,128,128]{3,2,1,0:T(8,128)(2,1)S(1)}, u32[]{:S(2)}, u32[]{:S(2)}) collective-permute-start(bf16[2,3,128,128]{3,2,1,0:T(8,128)(2,1)S(1)} %get-tuple-element.22), channel_id=1, source_target_pairs={{0,8},{4,252},{8,16},{12,4},{16,24},{20,12},{24,32},{28,20},{32,40... | collective-permute-start | bytes 589832 | tf_op jit(solution)/shard_map/ppermute | solution.py:41
  16.7 0.0 collective-permute-start.14
  16.7 0.0 collective-permute-start.2
  16.7 4.7 %collective-permute-done.3 = bf16[2,3,128,128]{3,2,1,0:T(8,128)(2,1)S(1)} collective-permute-done((bf16[2,3,128,128]{3,2,1,0:T(8,128)(2,1)S(1)}, bf16[2,3,128,128]{3,2,1,0:T(8,128)(2,1)S(1)}, u32[]{:S(2)}, u32[]{:S(2)}) %collective-permute-start.3) | collective-permute-done | bytes 196640 | tf_op jit(solution)/shard_map/ppermute | solution.py:41
  21.4 0.0 collective-permute-start.4
  21.4 4.3 %collective-permute-done.14 = bf16[2,3,128,128]{3,2,1,0:T(8,128)(2,1)S(1)} collective-permute-done((bf16[2,3,128,128]{3,2,1,0:T(8,128)(2,1)S(1)}, bf16[2,3,128,128]{3,2,1,0:T(8,128)(2,1)S(1)}, u32[]{:S(2)}, u32[]{:S(2)}) %collective-permute-start.14) | collective-permute-done | bytes 196640 | tf_op jit(solution)/shard_map/ppermute | solution.py:41
  25.7 18.4 %collective-permute-done.4 = bf16[2,3,128,128]{3,2,1,0:T(8,128)(2,1)S(1)} collective-permute-done((bf16[2,3,128,128]{3,2,1,0:T(8,128)(2,1)S(1)}, bf16[2,3,128,128]{3,2,1,0:T(8,128)(2,1)S(1)}, u32[]{:S(2)}, u32[]{:S(2)}) %collective-permute-start.4) | collective-permute-done | bytes 196640 | tf_op jit(solution)/shard_map/ppermute | solution.py:41
  44.1 5.5 %collective-permute-start.6 = (bf16[2,3,128,128]{3,2,1,0:T(8,128)(2,1)S(1)}, bf16[2,3,128,128]{3,2,1,0:T(8,128)(2,1)S(1)}, u32[]{:S(2)}, u32[]{:S(2)}) collective-permute-start(bf16[2,3,128,128]{3,2,1,0:T(8,128)(2,1)S(1)} %collective-permute-done.3), channel_id=1, source_target_pairs={{0,4},{4,0},{8,12},{12,8},{16,20},{20,16},{24,28},{28,24},{32,36},... | collective-permute-start | bytes 589832 | tf_op jit(solution)/shard_map/ppermute | solution.py:41
  49.6 2.1 %collective-permute-start.17 = (bf16[2,3,128,128]{3,2,1,0:T(8,128)(2,1)S(1)}, bf16[2,3,128,128]{3,2,1,0:T(8,128)(2,1)S(1)}, u32[]{:S(2)}, u32[]{:S(2)}) collective-permute-start(bf16[2,3,128,128]{3,2,1,0:T(8,128)(2,1)S(1)} %collective-permute-done.14), channel_id=1, source_target_pairs={{0,4},{4,0},{8,12},{12,8},{16,20},{20,16},{24,28},{28,24},{32,36},... | collective-permute-start | bytes 589832 | tf_op jit(solution)/shard_map/ppermute | solution.py:41
  51.7 0.0 collective-permute-start
  51.7 1.1 collective-permute-done.17
  52.8 0.4 collective-permute-start.11
  53.2 0.1 collective-permute-start.5
  53.3 0.4 collective-permute-start.16
  53.7 2.6 %collective-permute-start.13 = (bf16[6,3,128,128]{3,2,1,0:T(8,128)(2,1)S(1)}, bf16[6,3,128,128]{3,2,1,0:T(8,128)(2,1)S(1)}, u32[]{:S(2)}, u32[]{:S(2)}) collective-permute-start(bf16[6,3,128,128]{3,2,1,0:T(8,128)(2,1)S(1)} %get-tuple-element.29), channel_id=1, source_target_pairs={{0,8},{4,252},{8,16},{12,4},{16,24},{20,12},{24,32},{28,20},{32,40... | collective-permute-start | bytes 1769480 | tf_op jit(solution)/shard_map/ppermute | solution.py:41
  56.3 0.0 copy-start.3
  56.3 0.0 copy-start.5
  56.3 4.1 %plan.2.meta = s32[424]{0:T(512)S(1)} custom-call(s32[112]{0:T(128)S(1)} %copy-done.8, s32[512]{0:T(512)S(1)} %copy-done.6, s32[12,512]{1,0:T(8,128)S(1)} %bitcast.50, s32[8,12]{1,0:T(8,128)S(1)} %copy-done.4), custom_call_target="tpu_custom_call" | custom-call | flops 4000000000 | bytes 65536 | tf_op jit(solution)/shard_map/plan/pallas_call | solution.py:154
  60.4 0.0 copy-start
  60.4 0.0 copy-start.1
  60.4 7.6 %plan.3.meta = s32[888]{0:T(1024)S(1)} custom-call(s32[112]{0:T(128)S(1)} %copy-done.8, s32[512]{0:T(512)S(1)} %copy-done.6, s32[12,512]{1,0:T(8,128)S(1)} %bitcast.51, s32[12,512]{1,0:T(8,128)S(1)} %bitcast.52, s32[8,12]{1,0:T(8,128)S(1)} %copy-done.4, s32[8,12]{1,0:T(8,128)S(1)} %copy-done.5), custom_call_target="tpu_custom_call" | custom-call | flops 4000000000 | bytes 65536 | tf_op jit(solution)/shard_map/plan/pallas_call | solution.py:154
  68.2 13.7 %shard_map.105 = (bf16[2,4,3,128,128]{4,3,2,1,0:T(8,128)(2,1)S(1)}, bf16[2,4,3,128,128]{4,3,2,1,0:T(8,128)(2,1)S(1)}, bf16[2,4,3,128,128]{4,3,2,1,0:T(8,128)(2,1)S(1)}, bf16[2,4,3,128,128]{4,3,2,1,0:T(8,128)(2,1)S(1)}) custom-call(s32[888]{0:T(1024)S(1)} %plan.3.meta, bf16[8,12,128,128]{3,2,1,0:T(8,128)(2,1)S(1)} %copy-done, ...), custom_call_target="tpu_custom_call" | custom-call | flops 8000000000 | bytes 14942208 | tf_op jit(solution)/shard_map/pallas_call | solution.py:293
  81.9 4.4 %collective-permute-start.20 = (bf16[2,4,3,128,128]{4,3,2,1,0:T(8,128)(2,1)S(1)}, bf16[2,4,3,128,128]{4,3,2,1,0:T(8,128)(2,1)S(1)}, u32[]{:S(2)}, u32[]{:S(2)}) collective-permute-start(bf16[2,4,3,128,128]{4,3,2,1,0:T(8,128)(2,1)S(1)} %get-tuple-element.37), channel_id=1, source_target_pairs={{0,3},{1,2},{2,1},{3,0},{4,7},{5,6},{6,5},{7,4},{8,11},{9,10},{10,... | collective-permute-start | bytes 2359304 | tf_op jit(solution)/shard_map/ppermute | solution.py:316
  86.3 9.2 %shard_map.104 = (bf16[2,4,3,128,128]{4,3,2,1,0:T(8,128)(2,1)S(1)}, bf16[2,4,3,128,128]{4,3,2,1,0:T(8,128)(2,1)S(1)}, bf16[2,4,3,128,128]{4,3,2,1,0:T(8,128)(2,1)S(1)}, bf16[2,4,3,128,128]{4,3,2,1,0:T(8,128)(2,1)S(1)}) custom-call(s32[424]{0:T(512)S(1)} %plan.2.meta, bf16[8,12,128,128]{3,2,1,0:T(8,128)(2,1)S(1)} %copy-done, ...), custom_call_target="tpu_custom_call" | custom-call | flops 8000000000 | bytes 10616832 | tf_op jit(solution)/shard_map/pallas_call | solution.py:293
  95.5 0.1 collective-permute-start.9
  95.6 1.2 collective-permute-start.7
  96.8 7.6 %collective-permute-done.20.refs_4_ = bf16[2,4,3,128,128]{4,3,2,1,0:T(8,128)(2,1)S(1)} collective-permute-done((bf16[2,4,3,128,128]{4,3,2,1,0:T(8,128)(2,1)S(1)}, bf16[2,4,3,128,128]{4,3,2,1,0:T(8,128)(2,1)S(1)}, u32[]{:S(2)}, u32[]{:S(2)}) %collective-permute-start.20) | collective-permute-done | bytes 786464 | tf_op jit(solution)/shard_map/ppermute | solution.py:316
  104.4 0.1 fusion.3
  104.5 0.1 collective-permute-start.21
  104.6 1.2 collective-permute-done.18.refs_1_
  105.8 0.1 fusion.2
  106.0 1.5 %collective-permute-start.19 = (bf16[4,3,128,128]{3,2,1,0:T(8,128)(2,1)S(1)}, bf16[4,3,128,128]{3,2,1,0:T(8,128)(2,1)S(1)}, u32[]{:S(2)}, u32[]{:S(2)}) collective-permute-start(bf16[4,3,128,128]{3,2,1,0:T(8,128)(2,1)S(1)} %fusion.2), channel_id=1, source_target_pairs={{0,3},{1,2},{2,1},{3,0},{4,7},{5,6},{6,5},{7,4},{8,11},{9,10},{10,... | collective-permute-start | bytes 1179656 | tf_op jit(solution)/shard_map/ppermute | solution.py:316
  107.5 13.7 %collective-permute-done.9.refs_4_ = bf16[2,4,3,128,128]{4,3,2,1,0:T(8,128)(2,1)S(1)} collective-permute-done((bf16[2,4,3,128,128]{4,3,2,1,0:T(8,128)(2,1)S(1)}, bf16[2,4,3,128,128]{4,3,2,1,0:T(8,128)(2,1)S(1)}, u32[]{:S(2)}, u32[]{:S(2)}) %collective-permute-start.9) | collective-permute-done | bytes 786464 | tf_op jit(solution)/shard_map/ppermute | solution.py:316
  121.2 0.1 fusion.1
  121.4 0.1 collective-permute-start.10
  121.5 1.2 collective-permute-done.7.refs_1_
  122.7 0.1 fusion
  122.8 0.0 copy-start.7
  122.9 1.6 %collective-permute-start.8 = (bf16[4,3,128,128]{3,2,1,0:T(8,128)(2,1)S(1)}, bf16[4,3,128,128]{3,2,1,0:T(8,128)(2,1)S(1)}, u32[]{:S(2)}, u32[]{:S(2)}) collective-permute-start(bf16[4,3,128,128]{3,2,1,0:T(8,128)(2,1)S(1)} %fusion), channel_id=1, source_target_pairs={{0,3},{1,2},{2,1},{3,0},{4,7},{5,6},{6,5},{7,4},{8,11},{9,10},{10,... | collective-permute-start | bytes 1179656 | tf_op jit(solution)/shard_map/ppermute | solution.py:316
  124.4 3.8 %kept.1.refs_6_ = bf16[2,8,3,128,128]{4,3,2,1,0:T(8,128)(2,1)S(1)} custom-call(s32[888]{0:T(1024)S(1)} %plan.3.meta, bf16[8,12,128,128]{3,2,1,0:T(8,128)(2,1)S(1)} %copy-done, bf16[8,12,128,128]{3,2,1,0:T(8,128)(2,1)S(1)} %copy-done.1), custom_call_target="tpu_custom_call" | custom-call | flops 3000000000 | bytes 2097152 | tf_op jit(solution)/shard_map/kept/pallas_call | solution.py:194
  128.2 2.9 %collective-permute-done.21.refs_5_ = bf16[4,3,128,128]{3,2,1,0:T(8,128)(2,1)S(1)} collective-permute-done((bf16[4,3,128,128]{3,2,1,0:T(8,128)(2,1)S(1)}, bf16[4,3,128,128]{3,2,1,0:T(8,128)(2,1)S(1)}, u32[]{:S(2)}, u32[]{:S(2)}) %collective-permute-start.21) | collective-permute-done | bytes 393248 | tf_op jit(solution)/shard_map/ppermute | solution.py:316
  131.1 3.3 %finish.3 = bf16[8,3,128,128]{3,2,1,0:T(8,128)(2,1)} custom-call(s32[8]{0:T(128)S(1)} %copy-done.7, bf16[2,4,3,128,128]{4,3,2,1,0:T(8,128)(2,1)S(1)} %get-tuple-element.34.refs_0_, bf16[2,4,3,128,128]{4,3,2,1,0:T(8,128)(2,1)S(1)} %collective-permute-done.18.refs_1_, bf16[4,3,128,128]{3,2,1,0:T(8,128)(2,1)S(1)} %collective-permute-done.19.refs_2_, ...), custom_call_target="tpu_custom_call" | custom-call | flops 2000000000 | bytes 4194304 | tf_op jit(solution)/shard_map/finish/pallas_call | solution.py:363
  134.5 4.5 %collective-permute-done.10.refs_5_ = bf16[4,3,128,128]{3,2,1,0:T(8,128)(2,1)S(1)} collective-permute-done((bf16[4,3,128,128]{3,2,1,0:T(8,128)(2,1)S(1)}, bf16[4,3,128,128]{3,2,1,0:T(8,128)(2,1)S(1)}, u32[]{:S(2)}, u32[]{:S(2)}) %collective-permute-start.10) | collective-permute-done | bytes 393248 | tf_op jit(solution)/shard_map/ppermute | solution.py:316
  138.9 3.3 %finish.2 = bf16[8,3,128,128]{3,2,1,0:T(8,128)(2,1)} custom-call(s32[8]{0:T(128)S(1)} %copy-done.7, bf16[2,4,3,128,128]{4,3,2,1,0:T(8,128)(2,1)S(1)} %get-tuple-element.24.refs_0_, bf16[2,4,3,128,128]{4,3,2,1,0:T(8,128)(2,1)S(1)} %collective-permute-done.7.refs_1_, bf16[4,3,128,128]{3,2,1,0:T(8,128)(2,1)S(1)} %collective-permute-done.8.refs_2_, ...), custom_call_target="tpu_custom_call" | custom-call | flops 2000000000 | bytes 4194304 | tf_op jit(solution)/shard_map/finish/pallas_call | solution.py:363
  (26 shorter events, 0.1 us)
Async XLA Ops:
  0.6 55.6 %copy-start.8 = (s32[112]{0:T(128)S(1)}, s32[112]{0:T(128)}, u32[]{:S(2)}) copy-start(s32[112]{0:T(128)} %constant.2.clone.table) | copy-start | bytes 1348
  0.6 55.6 %copy-start.2 = (s32[512,12]{0,1:T(8,128)S(1)}, s32[512,12]{0,1:T(8,128)}, u32[]{:S(2)}) copy-start(s32[512,12]{0,1:T(8,128)} %param.11) | copy-start | bytes 73732
  0.7 55.6 %copy-start.4 = (s32[8,12]{1,0:T(8,128)S(1)}, s32[8,12]{1,0:T(8,128)}, u32[]{:S(2)}) copy-start(s32[8,12]{1,0:T(8,128)} %refs_2_.1) | copy-start | bytes 1156
  0.7 55.6 %copy-start.6 = (s32[512]{0:T(512)S(1)}, s32[512]{0:T(512)}, u32[]{:S(2)}) copy-start(s32[512]{0:T(512)} %row_slot.3) | copy-start | bytes 6148
  2.9 50.2 %collective-permute-start.1 = (bf16[8,3,128,128]{3,2,1,0:T(8,128)(2,1)S(1)}, bf16[8,3,128,128]{3,2,1,0:T(8,128)(2,1)S(1)}, u32[]{:S(2)}, u32[]{:S(2)}) collective-permute-start(bf16[8,3,128,128]{3,2,1,0:T(8,128)(2,1)S(1)} %get-tuple-element.20), channel_id=1, source_target_pairs={{0,252},{4,8},{8,4},{12,16},{16,12},{20,24},{24,20},{28,32},{32,28... | collective-permute-start | bytes 2359304 | tf_op jit(solution)/shard_map/ppermute | solution.py:41
  5.6 47.7 %collective-permute-start.12 = (bf16[8,3,128,128]{3,2,1,0:T(8,128)(2,1)S(1)}, bf16[8,3,128,128]{3,2,1,0:T(8,128)(2,1)S(1)}, u32[]{:S(2)}, u32[]{:S(2)}) collective-permute-start(bf16[8,3,128,128]{3,2,1,0:T(8,128)(2,1)S(1)} %get-tuple-element.28), channel_id=1, source_target_pairs={{0,252},{4,8},{8,4},{12,16},{16,12},{20,24},{24,20},{28,32},{32,28... | collective-permute-start | bytes 2359304 | tf_op jit(solution)/shard_map/ppermute | solution.py:41
  5.7 15.7 %collective-permute-start.3 = (bf16[2,3,128,128]{3,2,1,0:T(8,128)(2,1)S(1)}, bf16[2,3,128,128]{3,2,1,0:T(8,128)(2,1)S(1)}, u32[]{:S(2)}, u32[]{:S(2)}) collective-permute-start(bf16[2,3,128,128]{3,2,1,0:T(8,128)(2,1)S(1)} %get-tuple-element.22), channel_id=1, source_target_pairs={{0,8},{4,252},{8,16},{12,4},{16,24},{20,12},{24,32},{28,20},{32,40... | collective-permute-start | bytes 589832 | tf_op jit(solution)/shard_map/ppermute | solution.py:41
  16.7 9.0 %collective-permute-start.14 = (bf16[2,3,128,128]{3,2,1,0:T(8,128)(2,1)S(1)}, bf16[2,3,128,128]{3,2,1,0:T(8,128)(2,1)S(1)}, u32[]{:S(2)}, u32[]{:S(2)}) collective-permute-start(bf16[2,3,128,128]{3,2,1,0:T(8,128)(2,1)S(1)} %get-tuple-element.30), channel_id=1, source_target_pairs={{0,8},{4,252},{8,16},{12,4},{16,24},{20,12},{24,32},{28,20},{32,40... | collective-permute-start | bytes 589832 | tf_op jit(solution)/shard_map/ppermute | solution.py:41
  16.7 37.0 %collective-permute-start.2 = (bf16[6,3,128,128]{3,2,1,0:T(8,128)(2,1)S(1)}, bf16[6,3,128,128]{3,2,1,0:T(8,128)(2,1)S(1)}, u32[]{:S(2)}, u32[]{:S(2)}) collective-permute-start(bf16[6,3,128,128]{3,2,1,0:T(8,128)(2,1)S(1)} %get-tuple-element.21), channel_id=1, source_target_pairs={{0,8},{4,252},{8,16},{12,4},{16,24},{20,12},{24,32},{28,20},{32,40... | collective-permute-start | bytes 1769480 | tf_op jit(solution)/shard_map/ppermute | solution.py:41
  21.4 22.7 %collective-permute-start.4 = (bf16[2,3,128,128]{3,2,1,0:T(8,128)(2,1)S(1)}, bf16[2,3,128,128]{3,2,1,0:T(8,128)(2,1)S(1)}, u32[]{:S(2)}, u32[]{:S(2)}) collective-permute-start(bf16[2,3,128,128]{3,2,1,0:T(8,128)(2,1)S(1)} %get-tuple-element.23), channel_id=1, source_target_pairs={{0,244},{4,16},{8,252},{12,24},{16,4},{20,32},{24,12},{28,40},{32,... | collective-permute-start | bytes 589832 | tf_op jit(solution)/shard_map/ppermute | solution.py:41
  25.7 23.9 %collective-permute-start.15 = (bf16[2,3,128,128]{3,2,1,0:T(8,128)(2,1)S(1)}, bf16[2,3,128,128]{3,2,1,0:T(8,128)(2,1)S(1)}, u32[]{:S(2)}, u32[]{:S(2)}) collective-permute-start(bf16[2,3,128,128]{3,2,1,0:T(8,128)(2,1)S(1)} %get-tuple-element.31), channel_id=1, source_target_pairs={{0,244},{4,16},{8,252},{12,24},{16,4},{20,32},{24,12},{28,40},{32,... | collective-permute-start | bytes 589832 | tf_op jit(solution)/shard_map/ppermute | solution.py:41
  44.1 7.6 %collective-permute-start.6 = (bf16[2,3,128,128]{3,2,1,0:T(8,128)(2,1)S(1)}, bf16[2,3,128,128]{3,2,1,0:T(8,128)(2,1)S(1)}, u32[]{:S(2)}, u32[]{:S(2)}) collective-permute-start(bf16[2,3,128,128]{3,2,1,0:T(8,128)(2,1)S(1)} %collective-permute-done.3), channel_id=1, source_target_pairs={{0,4},{4,0},{8,12},{12,8},{16,20},{20,16},{24,28},{28,24},{32,36},... | collective-permute-start | bytes 589832 | tf_op jit(solution)/shard_map/ppermute | solution.py:41
  49.6 3.2 %collective-permute-start.17 = (bf16[2,3,128,128]{3,2,1,0:T(8,128)(2,1)S(1)}, bf16[2,3,128,128]{3,2,1,0:T(8,128)(2,1)S(1)}, u32[]{:S(2)}, u32[]{:S(2)}) collective-permute-start(bf16[2,3,128,128]{3,2,1,0:T(8,128)(2,1)S(1)} %collective-permute-done.14), channel_id=1, source_target_pairs={{0,4},{4,0},{8,12},{12,8},{16,20},{20,16},{24,28},{28,24},{32,36},... | collective-permute-start | bytes 589832 | tf_op jit(solution)/shard_map/ppermute | solution.py:41
  51.7 16.4 %collective-permute-start = (bf16[8,3,128,128]{3,2,1,0:T(8,128)(2,1)S(1)}, bf16[8,3,128,128]{3,2,1,0:T(8,128)(2,1)S(1)}, u32[]{:S(2)}, u32[]{:S(2)}) collective-permute-start(bf16[8,3,128,128]{3,2,1,0:T(8,128)(2,1)S(1)} %get-tuple-element.20), channel_id=1, source_target_pairs={{0,4},{4,0},{8,12},{12,8},{16,20},{20,16},{24,28},{28,24},{32,36},... | collective-permute-start | bytes 2359304 | tf_op jit(solution)/shard_map/ppermute | solution.py:41
  52.8 15.3 %collective-permute-start.11 = (bf16[8,3,128,128]{3,2,1,0:T(8,128)(2,1)S(1)}, bf16[8,3,128,128]{3,2,1,0:T(8,128)(2,1)S(1)}, u32[]{:S(2)}, u32[]{:S(2)}) collective-permute-start(bf16[8,3,128,128]{3,2,1,0:T(8,128)(2,1)S(1)} %get-tuple-element.28), channel_id=1, source_target_pairs={{0,4},{4,0},{8,12},{12,8},{16,20},{20,16},{24,28},{28,24},{32,36},... | collective-permute-start | bytes 2359304 | tf_op jit(solution)/shard_map/ppermute | solution.py:41
  53.2 15.0 %collective-permute-start.5 = (bf16[8,3,128,128]{3,2,1,0:T(8,128)(2,1)S(1)}, bf16[8,3,128,128]{3,2,1,0:T(8,128)(2,1)S(1)}, u32[]{:S(2)}, u32[]{:S(2)}) collective-permute-start(bf16[8,3,128,128]{3,2,1,0:T(8,128)(2,1)S(1)} %collective-permute-done.1), channel_id=1, source_target_pairs={{0,4},{4,0},{8,12},{12,8},{16,20},{20,16},{24,28},{28,24},{32,36},... | collective-permute-start | bytes 2359304 | tf_op jit(solution)/shard_map/ppermute | solution.py:41
  53.3 14.8 %collective-permute-start.16 = (bf16[8,3,128,128]{3,2,1,0:T(8,128)(2,1)S(1)}, bf16[8,3,128,128]{3,2,1,0:T(8,128)(2,1)S(1)}, u32[]{:S(2)}, u32[]{:S(2)}) collective-permute-start(bf16[8,3,128,128]{3,2,1,0:T(8,128)(2,1)S(1)} %collective-permute-done.12), channel_id=1, source_target_pairs={{0,4},{4,0},{8,12},{12,8},{16,20},{20,16},{24,28},{28,24},{32,36},... | collective-permute-start | bytes 2359304 | tf_op jit(solution)/shard_map/ppermute | solution.py:41
  53.7 14.4 %collective-permute-start.13 = (bf16[6,3,128,128]{3,2,1,0:T(8,128)(2,1)S(1)}, bf16[6,3,128,128]{3,2,1,0:T(8,128)(2,1)S(1)}, u32[]{:S(2)}, u32[]{:S(2)}) collective-permute-start(bf16[6,3,128,128]{3,2,1,0:T(8,128)(2,1)S(1)} %get-tuple-element.29), channel_id=1, source_target_pairs={{0,8},{4,252},{8,16},{12,4},{16,24},{20,12},{24,32},{28,20},{32,40... | collective-permute-start | bytes 1769480 | tf_op jit(solution)/shard_map/ppermute | solution.py:41
  56.3 4.1 %copy-start.3 = (s32[512,12]{0,1:T(8,128)S(1)}, s32[512,12]{0,1:T(8,128)}, u32[]{:S(2)}) copy-start(s32[512,12]{0,1:T(8,128)} %param.12) | copy-start | bytes 73732
  56.3 4.1 %copy-start.5 = (s32[8,12]{1,0:T(8,128)S(1)}, s32[8,12]{1,0:T(8,128)}, u32[]{:S(2)}) copy-start(s32[8,12]{1,0:T(8,128)} %refs_3_.1) | copy-start | bytes 1156
  60.4 7.7 %copy-start = (bf16[8,12,128,128]{3,2,1,0:T(8,128)(2,1)S(1)}, bf16[8,12,128,128]{3,2,1,0:T(8,128)(2,1)}, u32[]{:S(2)}) copy-start(bf16[8,12,128,128]{3,2,1,0:T(8,128)(2,1)} %p_ref.1) | copy-start | bytes 9437188
  60.4 7.7 %copy-start.1 = (bf16[8,12,128,128]{3,2,1,0:T(8,128)(2,1)S(1)}, bf16[8,12,128,128]{3,2,1,0:T(8,128)(2,1)}, u32[]{:S(2)}) copy-start(bf16[8,12,128,128]{3,2,1,0:T(8,128)(2,1)} %d_ref.1) | copy-start | bytes 9437188
  81.9 22.5 %collective-permute-start.20 = (bf16[2,4,3,128,128]{4,3,2,1,0:T(8,128)(2,1)S(1)}, bf16[2,4,3,128,128]{4,3,2,1,0:T(8,128)(2,1)S(1)}, u32[]{:S(2)}, u32[]{:S(2)}) collective-permute-start(bf16[2,4,3,128,128]{4,3,2,1,0:T(8,128)(2,1)S(1)} %get-tuple-element.37), channel_id=1, source_target_pairs={{0,3},{1,2},{2,1},{3,0},{4,7},{5,6},{6,5},{7,4},{8,11},{9,10},{10,... | collective-permute-start | bytes 2359304 | tf_op jit(solution)/shard_map/ppermute | solution.py:316
  86.3 19.6 %collective-permute-start.18 = (bf16[2,4,3,128,128]{4,3,2,1,0:T(8,128)(2,1)S(1)}, bf16[2,4,3,128,128]{4,3,2,1,0:T(8,128)(2,1)S(1)}, u32[]{:S(2)}, u32[]{:S(2)}) collective-permute-start(bf16[2,4,3,128,128]{4,3,2,1,0:T(8,128)(2,1)S(1)} %get-tuple-element.35), channel_id=1, source_target_pairs={{0,1},{1,0},{2,3},{3,2},{4,5},{5,4},{6,7},{7,6},{8,9},{9,8},{10,11... | collective-permute-start | bytes 2359304 | tf_op jit(solution)/shard_map/ppermute | solution.py:316
  95.5 25.8 %collective-permute-start.9 = (bf16[2,4,3,128,128]{4,3,2,1,0:T(8,128)(2,1)S(1)}, bf16[2,4,3,128,128]{4,3,2,1,0:T(8,128)(2,1)S(1)}, u32[]{:S(2)}, u32[]{:S(2)}) collective-permute-start(bf16[2,4,3,128,128]{4,3,2,1,0:T(8,128)(2,1)S(1)} %get-tuple-element.27), channel_id=1, source_target_pairs={{0,3},{1,2},{2,1},{3,0},{4,7},{5,6},{6,5},{7,4},{8,11},{9,10},{10,... | collective-permute-start | bytes 2359304 | tf_op jit(solution)/shard_map/ppermute | solution.py:316
  95.6 27.1 %collective-permute-start.7 = (bf16[2,4,3,128,128]{4,3,2,1,0:T(8,128)(2,1)S(1)}, bf16[2,4,3,128,128]{4,3,2,1,0:T(8,128)(2,1)S(1)}, u32[]{:S(2)}, u32[]{:S(2)}) collective-permute-start(bf16[2,4,3,128,128]{4,3,2,1,0:T(8,128)(2,1)S(1)} %get-tuple-element.25), channel_id=1, source_target_pairs={{0,1},{1,0},{2,3},{3,2},{4,5},{5,4},{6,7},{7,6},{8,9},{9,8},{10,11... | collective-permute-start | bytes 2359304 | tf_op jit(solution)/shard_map/ppermute | solution.py:316
  104.5 26.6 %collective-permute-start.21 = (bf16[4,3,128,128]{3,2,1,0:T(8,128)(2,1)S(1)}, bf16[4,3,128,128]{3,2,1,0:T(8,128)(2,1)S(1)}, u32[]{:S(2)}, u32[]{:S(2)}) collective-permute-start(bf16[4,3,128,128]{3,2,1,0:T(8,128)(2,1)S(1)} %fusion.3), channel_id=1, source_target_pairs={{0,1},{1,0},{2,3},{3,2},{4,5},{5,4},{6,7},{7,6},{8,9},{9,8},{10,11... | collective-permute-start | bytes 1179656 | tf_op jit(solution)/shard_map/ppermute | solution.py:316
  106.0 25.2 %collective-permute-start.19 = (bf16[4,3,128,128]{3,2,1,0:T(8,128)(2,1)S(1)}, bf16[4,3,128,128]{3,2,1,0:T(8,128)(2,1)S(1)}, u32[]{:S(2)}, u32[]{:S(2)}) collective-permute-start(bf16[4,3,128,128]{3,2,1,0:T(8,128)(2,1)S(1)} %fusion.2), channel_id=1, source_target_pairs={{0,3},{1,2},{2,1},{3,0},{4,7},{5,6},{6,5},{7,4},{8,11},{9,10},{10,... | collective-permute-start | bytes 1179656 | tf_op jit(solution)/shard_map/ppermute | solution.py:316
  121.4 17.5 %collective-permute-start.10 = (bf16[4,3,128,128]{3,2,1,0:T(8,128)(2,1)S(1)}, bf16[4,3,128,128]{3,2,1,0:T(8,128)(2,1)S(1)}, u32[]{:S(2)}, u32[]{:S(2)}) collective-permute-start(bf16[4,3,128,128]{3,2,1,0:T(8,128)(2,1)S(1)} %fusion.1), channel_id=1, source_target_pairs={{0,1},{1,0},{2,3},{3,2},{4,5},{5,4},{6,7},{7,6},{8,9},{9,8},{10,11... | collective-permute-start | bytes 1179656 | tf_op jit(solution)/shard_map/ppermute | solution.py:316
  122.8 8.3 %copy-start.7 = (s32[8]{0:T(128)S(1)}, s32[8]{0:T(128)}, u32[]{:S(2)}) copy-start(s32[8]{0:T(128)} %branch_ref.3) | copy-start | bytes 100
  122.9 16.1 %collective-permute-start.8 = (bf16[4,3,128,128]{3,2,1,0:T(8,128)(2,1)S(1)}, bf16[4,3,128,128]{3,2,1,0:T(8,128)(2,1)S(1)}, u32[]{:S(2)}, u32[]{:S(2)}) collective-permute-start(bf16[4,3,128,128]{3,2,1,0:T(8,128)(2,1)S(1)} %fusion), channel_id=1, source_target_pairs={{0,3},{1,2},{2,1},{3,0},{4,7},{5,6},{6,5},{7,4},{8,11},{9,10},{10,... | collective-permute-start | bytes 1179656 | tf_op jit(solution)/shard_map/ppermute | solution.py:316
